TPU v7x, 1024 devices: a whole 4x8x16 slice. The times are simulated.
1024 devices in a mesh: dp: 8 (over z_lo), blk: 16 (over y, core), aa: 8 (over z_hi, x).
Axes of the slice: x: 4, y: 8, z: 16 (z_hi: 2, z_lo: 8; z = z_hi * 8 + z_lo), core: 2. Of those that a mesh axis runs over, the one named last changes fastest.
Arguments:
- queries: bfloat16 [8, 16384, 2048], P('dp', ('blk', 'aa')), may hold values from -128 to 128
- keys: bfloat16 [8, 16384, 512], P('dp', ('blk', 'aa')), may hold values from -10 to 10
- values: bfloat16 [8, 16384, 512], P('dp', ('blk', 'aa')), may hold values from -6 to 6
- grad_parts: float32 [8, 128, 131072], P('dp', ('blk', 'aa')), may hold values from -768 to 768
Outputs:
- attended: bfloat16 [8, 16384, 2048], P('dp', 'blk', 'aa')
- grad_mean: float32 [131072], P(('blk', 'aa'))
All inputs are finite; a program needn't handle non-finite values.
Results may differ from a plain program's by a relative error of at most 0.008.
Values may be sent and summed in bfloat16 or wider, within the bound.
No kernel may reach another device: no remote copies, remote signals or barrier semaphores. Data moves between devices by JAX's collectives and lax.ppermute only.
A program may use at most 32 MiB of HBM per device.

v0:
```python
import jax
import jax.numpy as jnp
from jax import lax
from jax.sharding import Mesh
from jax.sharding import PartitionSpec as P

HQ = 16
KVH = 4
DH = 128
AA = ("aa_0", "aa_1")
BLK = ("blk_0", "blk_1")
BLK_AA = ("blk_0", "blk_1", "aa_0", "aa_1")


def sent_together(arrays, axis, split_dim, concat_dim, along):
    widths = [a.shape[along] for a in arrays]
    both = jnp.concatenate(arrays, axis=along)
    filled = lax.all_to_all(both, axis, split_axis=split_dim, concat_axis=concat_dim, tiled=True)
    return tuple(jnp.split(filled, [sum(widths[:k]) for k in range(1, len(widths))], axis=along))


def shifted(value, axis, by):
    peers = lax.axis_size(axis)
    pairs = [(i, i + by) for i in range(peers) if 0 <= i + by < peers]
    return lax.ppermute(value, axis, pairs)


def own_block(tiles, axes, order):
    inside = tiles.shape[1:]
    tiles = tiles.reshape(*(lax.axis_size(a) for a in axes), *inside)
    tiles = jnp.moveaxis(tiles, order, range(len(axes))).reshape(-1, *inside)
    for k in order:
        tiles = lax.psum_scatter(tiles, axes[k], scatter_dimension=0, tiled=True)
    return tiles[0]


def in_blocks(value, dim, peers):
    before, after = (value.shape[:dim], value.shape[dim + 1 :])
    return jnp.moveaxis(value.reshape(*before, peers, -1, *after), dim, 0)


def summed_rows(value, axes, order, dim):
    peers = lax.axis_size(axes)
    return own_block(in_blocks(value, dim, peers), axes, order)


def copy_for_each(value, axis):
    peers = lax.axis_size(axis)
    return lax.all_to_all(
        jnp.broadcast_to(value[None], (peers, *value.shape)), axis, 0, 0, tiled=True
    )


def taken_together(value, axis):
    everything = copy_for_each(value, axis)
    return jnp.sum(everything, axis=0)


def attend(queries, keys, values):
    rows = queries.shape[0]
    size_aa = lax.axis_size(AA)
    spread = max(KVH, size_aa)
    q_heads = queries.reshape(rows, HQ, DH)
    k_heads = jnp.repeat(keys.reshape(rows, KVH, DH), spread // KVH, axis=1)
    v_heads = jnp.repeat(values.reshape(rows, KVH, DH), spread // KVH, axis=1)
    q_here, k_here, v_here = (
        lax.all_to_all(q_heads, AA, split_axis=1, concat_axis=0, tiled=True),
        *sent_together((k_heads, v_heads), AA, 1, 0, 2),
    )
    span = q_here.shape[0]
    reach = span // 4
    prior_k, prior_v = shifted((k_here[span - reach :], v_here[span - reach :]), BLK, 1)
    group = q_here.shape[1] // k_here.shape[1]
    k_all = jnp.repeat(jnp.concatenate([prior_k, k_here], 0), group, axis=1)
    v_all = jnp.repeat(jnp.concatenate([prior_v, v_here], 0), group, axis=1)
    step_rows = min(256, reach)
    anchor = lax.axis_index(BLK) * span
    scale = DH ** (-0.5)

    def one_block(index):
        offset = index * step_rows
        q_block = lax.dynamic_slice_in_dim(q_here, offset, step_rows, 0)
        k_block = lax.dynamic_slice_in_dim(k_all, offset, step_rows + reach, 0)
        v_block = lax.dynamic_slice_in_dim(v_all, offset, step_rows + reach, 0)
        scores = (
            jnp.einsum("qhd,khd->hqk", q_block, k_block, preferred_element_type=jnp.float32) * scale
        )
        q_pos = anchor + offset + jnp.arange(step_rows, dtype=jnp.int32)
        k_pos = anchor + offset - reach + jnp.arange(step_rows + reach, dtype=jnp.int32)
        allowed = (k_pos[None, :] <= q_pos[:, None]) & (k_pos[None, :] > q_pos[:, None] - reach)
        scores = jnp.where(allowed[None], scores, -1e30)
        top = jnp.max(scores, axis=-1, keepdims=True)
        expo = jnp.exp(scores - top)
        weights = (expo / jnp.sum(expo, axis=-1, keepdims=True)).astype(jnp.bfloat16)
        out = jnp.einsum("hqk,khd->qhd", weights, v_block, preferred_element_type=jnp.float32)
        return out.astype(jnp.bfloat16)

    blocks = lax.map(one_block, jnp.arange(span // step_rows, dtype=jnp.int32))
    return blocks.reshape(span, -1)


def average(grad_parts):
    members = lax.axis_size(BLK) * lax.axis_size(AA)
    replicas = lax.axis_size("dp")
    flat_grad = grad_parts.reshape(-1)
    share = summed_rows(flat_grad, BLK_AA, (1, 0, 3, 2), 0)
    total = taken_together(share, "dp")
    return total / (members * replicas)


def shards(queries, keys, values, grad_parts):
    attended = attend(queries[0], keys[0], values[0])[None]
    grad_mean = average(grad_parts)
    return (attended, grad_mean)


def solution(mesh):
    torus = Mesh(
        mesh.devices.reshape(mesh.shape["dp"], 8, 2, 2, 4), ("dp", "blk_0", "blk_1", "aa_0", "aa_1")
    )
    placed = (
        P("dp", BLK_AA, None),
        P("dp", BLK_AA, None),
        P("dp", BLK_AA, None),
        P("dp", BLK_AA, None),
    )
    return jax.shard_map(
        shards,
        mesh=torus,
        in_specs=placed,
        out_specs=(P("dp", BLK, AA), P(BLK_AA)),
        check_vma=False,
    )
```

profile of v0, /device:TPU:448, one launch (start us, length us, event | category | flops | bytes accessed | tf_op | source)
XLA Modules:
  0.0 224.7 jit_solution(17533245486268366990)
XLA Ops:
  7.7 2.9 %reduce.4 = f32[131072]{0:T(1024)S(1)} reduce(f32[1,1,131072]{2,1,0:T(1,128)} %param.9, f32[]{:T(128)} %broadcast.117), dimensions={0,1}, to_apply=%param.9.reduce_sub_computation.3 | reduce | bytes 1048580 | tf_op args[3]
  11.3 1.2 reshape.106
  12.5 24.1 %reduce-scatter.3.cloned.1.call-done = f32[64,1024]{1,0:T(8,128)} async-done(((f32[128,1024]{1,0:T(8,128)}), f32[64,1024]{1,0:T(8,128)}) %reduce-scatter.3.cloned.1.call-update) | async-done | bytes 262160 | tf_op jit(solution)/shard_map/reduce_scatter | solution.py:33
  36.7 0.9 copy-done.1
  37.6 0.9 copy-done.2
  38.5 1.3 dynamic-slice
  39.8 1.3 dynamic-slice.2
  41.7 44.6 %reduce-scatter.5.cloned.1.call-done = f32[8,1024]{1,0:T(8,128)} async-done(((f32[64,1024]{1,0:T(8,128)}), f32[8,1024]{1,0:T(8,128)}) %reduce-scatter.5.cloned.1.call-update) | async-done | bytes 32784 | tf_op jit(solution)/shard_map/reduce_scatter | solution.py:33
  86.4 17.5 %all-reduce = f32[8,1024]{1,0:T(8,128)S(1)} all-reduce(f32[8,1024]{1,0:T(8,128)} %reduce-scatter.5.cloned.1.call-done), channel_id=4, replica_groups=mesh['dp'=8,'blk_0'=8,'blk_1'=2,'aa_0'=2,'aa_1'=4] {'aa_1'}, use_global_device_ids=true, to_apply=%region_6.7.clone | all-reduce | flops 8192 | bytes 65536
  103.9 13.7 %all-reduce.1 = f32[2,1024]{1,0:T(2,128)S(1)} all-reduce(f32[2,1024]{1,0:T(2,128)S(1)} %constant_dynamic-slice_fusion.1), channel_id=5, replica_groups=mesh['dp'=8,'blk_0'=8,'blk_1'=2,'aa_0'=2,'aa_1'=4] {'aa_0'}, use_global_device_ids=true, to_apply=%region_7.8.clone | all-reduce | flops 2048 | bytes 16384
  117.7 0.7 constant_dynamic-slice_fusion
  118.3 0.6 broadcast_in_dim.55
  118.9 9.9 %all-to-all-start.2 = ((f32[8,1,1024]{2,1,0:T(1,128)}), f32[8,1,1024]{2,1,0:T(1,128)S(1)}, u32[]{:S(2)}, u32[]{:S(2)}) async-start(f32[8,1,1024]{2,1,0:T(1,128)} %broadcast_in_dim.55), calls=%async_computation.4 | async-start | bytes 65536 | tf_op jit(solution)/shard_map/all_to_all | solution.py:49
  128.9 0.9 pad_maximum_fusion
  129.8 1.9 all-to-all-done.2
  131.7 6.5 %all-to-all-start = ((bf16[128,8,256]{2,0,1:T(8,128)(2,1)}), bf16[128,8,256]{2,0,1:T(8,128)(2,1)S(1)}, u32[]{:S(2)}, u32[]{:S(2)}) async-start(bf16[128,8,256]{2,0,1:T(8,128)(2,1)} %pad_maximum_fusion), calls=%async_computation | async-start | bytes 1048576 | tf_op jit(solution)/shard_map/all_to_all | solution.py:18
  138.2 1.0 copy.42
  139.2 34.4 %all-to-all-done = bf16[128,8,256]{2,0,1:T(8,128)(2,1)S(1)} async-done(((bf16[128,8,256]{2,0,1:T(8,128)(2,1)}), bf16[128,8,256]{2,0,1:T(8,128)(2,1)S(1)}, u32[]{:S(2)}, u32[]{:S(2)}) %all-to-all-start) | async-done | bytes 524320 | tf_op jit(solution)/shard_map/all_to_all | solution.py:18
  173.6 11.5 %all-to-all-start.1 = ((bf16[128,16,128]{0,2,1:T(8,128)(2,1)}), bf16[128,16,128]{0,2,1:T(8,128)(2,1)S(1)}, u32[]{:S(2)}, u32[]{:S(2)}) async-start(bf16[128,16,128]{0,2,1:T(8,128)(2,1)} %bitcast.11), calls=%async_computation.1 | async-start | bytes 1048576 | tf_op jit(solution)/shard_map/all_to_all | solution.py:67
  185.7 1.3 collective-permute-start
  187.1 3.7 %collective-permute-start.1 = (bf16[256,1,128]{2,0,1:T(8,128)(2,1)S(1)}, bf16[256,1,128]{2,0,1:T(8,128)(2,1)S(1)}, u32[]{:S(2)}, u32[]{:S(2)}) collective-permute-start(bf16[256,1,128]{2,0,1:T(8,128)(2,1)S(1)} %get-tuple-element.128), channel_id=1, source_target_pairs={{0,8},{8,16},{16,24},{24,32},{32,40},{40,48},{48,56},{56,64},{64,7... | collective-permute-start | bytes 196616 | tf_op jit(solution)/shard_map/ppermute | solution.py:25
  190.8 11.3 %all-to-all-done.1 = bf16[128,16,128]{0,2,1:T(8,128)(2,1)S(1)} async-done(((bf16[128,16,128]{0,2,1:T(8,128)(2,1)}), bf16[128,16,128]{0,2,1:T(8,128)(2,1)S(1)}, u32[]{:S(2)}, u32[]{:S(2)}) %all-to-all-start.1) | async-done | bytes 524320 | tf_op jit(solution)/shard_map/all_to_all | solution.py:67
  202.7 14.0 %while.13 = (s32[]{:T(128)}, bf16[4,256,2,128]{3,2,1,0:T(2,128)(2,1)S(1)}, s32[4]{0:T(128)S(1)}, bf16[1280,2,128]{0,2,1:T(8,128)(2,1)S(1)}, s32[]{:T(128)}, /*in...) while((s32[]{:T(128)}, ...), condition=%wide.region_3.4_spmd, body=%wide.region_0.3_spmd.sunk | while | flops 204147200 | bytes 2111228 | solution.py:98
  202.8 0.7 dynamic_slice.66
  204.9 1.1 fusion.58
  206.2 0.7 dynamic_slice.66
  208.4 1.1 fusion.58
  209.7 0.7 dynamic_slice.66
  211.9 1.1 fusion.58
  213.2 0.7 dynamic_slice.66
  215.4 1.1 fusion.58
  216.7 1.1 broadcast_in_dim_reshape.3
  (56 shorter events, 6.6 us)
Async XLA Ops:
  7.2 29.5 %reduce-scatter.3.cloned.1.call-start = ((), (), s32[]{:S(2)}) async-start(), calls=%async_computation.5 | async-start | bytes 786432 | tf_op jit(solution)/shard_map/reduce_scatter | solution.py:33
  12.4 73.9 %reduce-scatter.5.cloned.1.call-start = ((), (), s32[]{:S(2)}) async-start(), calls=%async_computation.6 | async-start | bytes 294912 | tf_op jit(solution)/shard_map/reduce_scatter | solution.py:33
  36.6 0.9 copy-start.1
  37.6 0.9 copy-start.2
  118.9 12.7 %all-to-all-start.2 = ((f32[8,1,1024]{2,1,0:T(1,128)}), f32[8,1,1024]{2,1,0:T(1,128)S(1)}, u32[]{:S(2)}, u32[]{:S(2)}) async-start(f32[8,1,1024]{2,1,0:T(1,128)} %broadcast_in_dim.55), calls=%async_computation.4 | async-start | bytes 65536 | tf_op jit(solution)/shard_map/all_to_all | solution.py:49
  129.8 8.4 %copy-start = (bf16[1,128,2048]{2,1,0:T(8,128)(2,1)S(1)}, bf16[1,128,2048]{2,1,0:T(8,128)(2,1)}, u32[]{:S(2)}) copy-start(bf16[1,128,2048]{2,1,0:T(8,128)(2,1)} %param.6) | copy-start | bytes 1572868
  131.7 41.9 %all-to-all-start = ((bf16[128,8,256]{2,0,1:T(8,128)(2,1)}), bf16[128,8,256]{2,0,1:T(8,128)(2,1)S(1)}, u32[]{:S(2)}, u32[]{:S(2)}) async-start(bf16[128,8,256]{2,0,1:T(8,128)(2,1)} %pad_maximum_fusion), calls=%async_computation | async-start | bytes 1048576 | tf_op jit(solution)/shard_map/all_to_all | solution.py:18
  173.6 28.5 %all-to-all-start.1 = ((bf16[128,16,128]{0,2,1:T(8,128)(2,1)}), bf16[128,16,128]{0,2,1:T(8,128)(2,1)S(1)}, u32[]{:S(2)}, u32[]{:S(2)}) async-start(bf16[128,16,128]{0,2,1:T(8,128)(2,1)} %bitcast.11), calls=%async_computation.1 | async-start | bytes 1048576 | tf_op jit(solution)/shard_map/all_to_all | solution.py:67
  185.7 16.6 %collective-permute-start = (bf16[256,1,128]{2,0,1:T(8,128)(2,1)S(1)}, bf16[256,1,128]{2,0,1:T(8,128)(2,1)S(1)}, u32[]{:S(2)}, u32[]{:S(2)}) collective-permute-start(bf16[256,1,128]{2,0,1:T(8,128)(2,1)S(1)} %get-tuple-element.129), channel_id=1, source_target_pairs={{0,8},{8,16},{16,24},{24,32},{32,40},{40,48},{48,56},{56,64},{64,7... | collective-permute-start | bytes 196616 | tf_op jit(solution)/shard_map/ppermute | solution.py:25
  187.1 15.5 %collective-permute-start.1 = (bf16[256,1,128]{2,0,1:T(8,128)(2,1)S(1)}, bf16[256,1,128]{2,0,1:T(8,128)(2,1)S(1)}, u32[]{:S(2)}, u32[]{:S(2)}) collective-permute-start(bf16[256,1,128]{2,0,1:T(8,128)(2,1)S(1)} %get-tuple-element.128), channel_id=1, source_target_pairs={{0,8},{8,16},{16,24},{24,32},{32,40},{40,48},{48,56},{56,64},{64,7... | collective-permute-start | bytes 196616 | tf_op jit(solution)/shard_map/ppermute | solution.py:25
Sparse Core Ops, SparseCore 0:
  12.6 24.0 reduce-scatter.2
  40.0 46.3 reduce-scatter.4
where the time goes:
time: 225 us
  waiting for transfers between devices  116 us (52%)
  starting transfers between devices  33 us (15%)
  blocking collectives  31.3 us (14%)
  between operations  14.9 us (7%)
  local copies, waits for them, and re-layouts  14.3 us (6%)
  matrix products  6.57 us (3%)
  other arithmetic  5.2 us (2%)
  loops' own time  3.06 us (1%)
    reduce_scatter x2, waiting for transfers between devices, own_block(): tiles = lax.psum_scatter(tiles, axes[k], scatter_dimension=0, tiled=True)  68.8 us
    all_to_all x1, waiting for transfers between devices, sent_together(): lax.all_to_all(both, axis, split_axis=split_dim, concat_axis=concat_dim,...  34.4 us
    unnamed x2, blocking collectives  31.3 us
    all_to_all x1, starting transfers between devices, attend(): lax.all_to_all(q_heads, AA, split_axis=1, concat_axis=0, tiled=True)  11.5 us
    all_to_all x1, waiting for transfers between devices, attend(): lax.all_to_all(q_heads, AA, split_axis=1, concat_axis=0, tiled=True)  11.3 us
    all_to_all x1, starting transfers between devices, copy_for_each(): lax.all_to_all(jnp.broadcast_to(value[None], (peers, *value.shape)), axis...  9.9 us
    all_to_all x1, starting transfers between devices, sent_together(): lax.all_to_all(both, axis, split_axis=split_dim, concat_axis=concat_dim,...  6.51 us
    unnamed x12, local copies, waits for them, and re-layouts  6.46 us
  transfers between devices with their start and end apart: 7, of which 5 were waited for; matrix products, arithmetic and copies ran while one was open for 3% of the time, Pallas kernels for 0%

commit v1 on v0

v1 whole, which is shorter than its diff:
```python
import jax
import jax.numpy as jnp
from jax import lax
from jax.experimental import pallas as pl
from jax.experimental.pallas import tpu as pltpu
from jax.sharding import Mesh
from jax.sharding import PartitionSpec as P

DH = 128
BLK = ("blk_0", "blk_1")
AA = ("aa_0", "aa_1")
BLK_AA = ("blk_0", "blk_1", "aa_0", "aa_1")
SWAP = [(0, 1), (1, 0)]


def pack_kernel(side_ref, q_ref, k_ref, v_ref, far_q, far_kv, near):
    side = side_ref[0]
    n, _, wide = far_q.shape
    for x in range(n):
        for half, is_far in ((1 - side, True), (side, False)):
            q_at = pl.multiple_of(half * (n * wide) + x * wide, wide)
            q_part = q_ref[:, pl.ds(q_at, wide)]
            kv_at = pl.multiple_of(half * (n // 2 * DH) + x // 2 * DH, DH)
            k_part = k_ref[:, pl.ds(kv_at, DH)]
            v_part = v_ref[:, pl.ds(kv_at, DH)]
            if is_far:
                far_q[x] = q_part
                if x % 2 == 0:
                    far_kv[x // 2, :, :DH] = k_part
                    far_kv[x // 2, :, DH:] = v_part
            else:
                near[x, :, :wide] = q_part
                near[x, :, wide : wide + DH] = k_part
                near[x, :, wide + DH :] = v_part


def packed(side, q, k, v, n):
    rows, wide = q.shape[0], q.shape[1] // (2 * n)
    vmem = pl.BlockSpec(memory_space=pltpu.VMEM)
    return pl.pallas_call(
        pack_kernel,
        out_shape=(
            jax.ShapeDtypeStruct((n, rows, wide), q.dtype),
            jax.ShapeDtypeStruct((n // 2, rows, 2 * DH), q.dtype),
            jax.ShapeDtypeStruct((n, rows, wide + 2 * DH), q.dtype),
        ),
        in_specs=[pl.BlockSpec(memory_space=pltpu.SMEM), vmem, vmem, vmem],
        out_specs=(vmem, vmem, vmem),
        compiler_params=pltpu.CompilerParams(vmem_limit_bytes=8 << 20),
        name="pack",
    )(side, q, k, v)


def attend_kernel(side_ref, near_ref, far_kv_ref, far_q_ref, prior_ref, out_ref, q_s, k_s, v_s):
    side = side_ref[0]
    half, wide = far_q_ref.shape
    reach = prior_ref.shape[0]
    near_at = pl.multiple_of(side * half, half)
    far_at = pl.multiple_of((1 - side) * half, half)
    k_s[:reach] = prior_ref[:, :DH]
    v_s[:reach] = prior_ref[:, DH:]
    for at, kv in ((near_at, near_ref[:, wide:]), (far_at, far_kv_ref[...])):
        k_s[pl.ds(at + reach, half)] = kv[:, :DH]
        v_s[pl.ds(at + reach, half)] = kv[:, DH:]
    q_s[pl.ds(near_at, half)] = near_ref[:, :wide]
    q_s[pl.ds(far_at, half)] = far_q_ref[...]
    row = lax.broadcasted_iota(jnp.int32, (reach, reach), 0)
    col = lax.broadcasted_iota(jnp.int32, (reach, reach), 1)
    newer = col <= row
    across = (((1,), (1,)), ((), ()))
    for block in range(2 * half // reach):
        rows = pl.ds(block * reach, reach)
        older_rows, newer_rows = rows, pl.ds((block + 1) * reach, reach)
        for head in range(wide // DH):
            lanes = pl.ds(head * DH, DH)
            q = q_s[rows, lanes]
            old = lax.dot_general(q, k_s[older_rows], across, preferred_element_type=jnp.float32)
            new = lax.dot_general(q, k_s[newer_rows], across, preferred_element_type=jnp.float32)
            scores = jnp.where(newer, new, old) * DH**-0.5
            expo = jnp.exp(scores - jnp.max(scores, axis=-1, keepdims=True))
            weights = (expo / jnp.sum(expo, axis=-1, keepdims=True)).astype(jnp.bfloat16)
            none = jnp.zeros_like(weights)
            out = jnp.dot(
                jnp.where(newer, weights, none), v_s[newer_rows], preferred_element_type=jnp.float32
            ) + jnp.dot(
                jnp.where(newer, none, weights), v_s[older_rows], preferred_element_type=jnp.float32
            )
            out_ref[rows, lanes] = out.astype(jnp.bfloat16)


def attended_rows(side, near, far_kv, far_q, prior):
    half, wide = far_q.shape
    reach = prior.shape[0]
    vmem = pl.BlockSpec(memory_space=pltpu.VMEM)
    return pl.pallas_call(
        attend_kernel,
        out_shape=jax.ShapeDtypeStruct((2 * half, wide), jnp.bfloat16),
        in_specs=[pl.BlockSpec(memory_space=pltpu.SMEM), vmem, vmem, vmem, vmem],
        out_specs=vmem,
        scratch_shapes=[
            pltpu.VMEM((2 * half, wide), jnp.bfloat16),
            pltpu.VMEM((2 * half + reach, DH), jnp.bfloat16),
            pltpu.VMEM((2 * half + reach, DH), jnp.bfloat16),
        ],
        cost_estimate=pl.CostEstimate(
            flops=16 * half * wide * reach, bytes_accessed=4 * half * wide * 2, transcendentals=4 * half * reach
        ),
        compiler_params=pltpu.CompilerParams(vmem_limit_bytes=16 << 20),
        name="attend",
    )(side, near, far_kv, far_q, prior)


def step(queries, keys, values, grad_parts):
    n = lax.axis_size("aa_1")
    side = lax.axis_index("aa_0").astype(jnp.int32)
    side_at = side.reshape(1)
    far_q, far_kv, near = packed(side_at, queries[0], keys[0], values[0], n)
    far_kv = lax.ppermute(far_kv, "aa_0", SWAP)
    far_q = lax.ppermute(far_q, "aa_0", SWAP)
    near = lax.all_to_all(near, "aa_1", 0, 0, tiled=True)
    near = near.reshape(-1, near.shape[-1])

    dp, y, c, z, x = (lax.axis_size(a) for a in ("dp", *BLK_AA))
    parts = grad_parts.reshape(y * c, z, x, 1, -1).transpose(0, 2, 1, 3, 4)
    parts = parts.reshape(y * c * x, 1, -1)
    parts = lax.all_to_all(parts, ("blk_0", "blk_1", "aa_1"), 0, 0, tiled=True)
    share = jnp.sum(parts, axis=0).reshape(z, 1, -1)
    share = jnp.broadcast_to(share[None], (dp, *share.shape)).reshape(dp * z, 1, -1)
    share = lax.all_to_all(share, ("dp", "aa_0"), 0, 0, tiled=True)
    grad_mean = jnp.sum(share, axis=(0, 1)) / (dp * y * c * z * x)

    far_kv = lax.all_to_all(jnp.repeat(far_kv, 2, axis=0), "aa_1", 0, 0, tiled=True)
    far_kv = far_kv.reshape(-1, far_kv.shape[-1])
    half = near.shape[0]
    reach = half // 2
    last = jnp.where(side == 1, near[half - reach :, -2 * DH :], far_kv[half - reach :])
    prior = lax.ppermute(last, BLK, [(i, i + 1) for i in range(y * c - 1)])
    far_q = lax.all_to_all(far_q, "aa_1", 0, 0, tiled=True)
    far_q = far_q.reshape(-1, far_q.shape[-1])
    attended = attended_rows(side_at, near, far_kv, far_q, prior)
    return attended[None], grad_mean


def solution(mesh):
    torus = Mesh(
        mesh.devices.reshape(mesh.shape["dp"], 8, 2, 2, 4), ("dp", "blk_0", "blk_1", "aa_0", "aa_1")
    )
    placed = P("dp", BLK_AA, None)
    return jax.shard_map(
        step,
        mesh=torus,
        in_specs=(placed,) * 4,
        out_specs=(P("dp", BLK, AA), P(BLK_AA)),
        check_vma=False,
    )
```

time: 225 us -> 138 us (0.61)
  the two profiles are of different devices: /device:TPU:448 before, /device:TPU:8 now
where the time goes in v1:
time: 138 us; the launch traced here: 137 us
  starting transfers between devices  84.8 us (61%)
  waiting for transfers between devices  26.6 us (19%)
  blocking collectives  10.8 us (8%)
  local copies, waits for them, and re-layouts  6.39 us (5%)
  Pallas kernels  5.24 us (4%)
  other arithmetic  2.85 us (2%)
    all_to_all x1, starting transfers between devices, step(): share = lax.all_to_all(share, ('dp', 'aa_0'), 0, 0, tiled=True)  34.7 us
    ppermute x1, starting transfers between devices, step(): far_kv = lax.ppermute(far_kv, 'aa_0', SWAP)  19.3 us
    ppermute x1, starting transfers between devices, step(): far_q = lax.ppermute(far_q, 'aa_0', SWAP)  12.3 us
    all_to_all x1, blocking collectives, step(): lax.all_to_all(jnp.repeat(far_kv, 2, axis=0), 'aa_1', 0, 0, tiled=True)  10.8 us
    all_to_all x1, starting transfers between devices, step(): parts = lax.all_to_all(parts, ('blk_0', 'blk_1', 'aa_1'), 0, 0, tiled=True)  8.71 us
    ppermute x1, waiting for transfers between devices, step(): far_q = lax.ppermute(far_q, 'aa_0', SWAP)  6.84 us
    all_to_all x1, waiting for transfers between devices, step(): far_q = lax.all_to_all(far_q, 'aa_1', 0, 0, tiled=True)  5.59 us
    ppermute x1, waiting for transfers between devices, step(): prior = lax.ppermute(last, BLK, [(i, i + 1) for i in range(y * c - 1)])  4.36 us
  transfers between devices with their start and end apart: 7, of which 6 were waited for; matrix products, arithmetic and copies ran while one was open for 4% of the time, Pallas kernels for 3%

profile of v1, /device:TPU:8, one launch (start us, length us, event | category | flops | bytes accessed | tf_op | source)
XLA Modules:
  0.0 137.5 jit_solution(2430455030415852036)
XLA Ops:
  0.6 0.0 copy-start.2
  0.6 1.0 copy-done.2
  1.7 0.9 copy-done.3
  2.6 0.9 copy-done.4
  3.5 0.9 pack.1
  4.4 19.3 %collective-permute-start = (bf16[2,128,256]{2,1,0:T(8,128)(2,1)S(1)}, bf16[2,128,256]{2,1,0:T(8,128)(2,1)S(1)}, u32[]{:S(2)}, u32[]{:S(2)}) collective-permute-start(bf16[2,128,256]{2,1,0:T(8,128)(2,1)S(1)} %get-tuple-element.6), channel_id=1, source_target_pairs={{0,4},{4,0},{1,5},{5,1},{2,6},{6,2},{3,7},{7,3},{8,12},{12,8},{9,1... | collective-permute-start | bytes 393224 | tf_op jit(solution)/shard_map/ppermute | solution.py:118
  23.8 3.8 %collective-permute-done = bf16[2,128,256]{2,1,0:T(8,128)(2,1)S(1)} collective-permute-done((bf16[2,128,256]{2,1,0:T(8,128)(2,1)S(1)}, bf16[2,128,256]{2,1,0:T(8,128)(2,1)S(1)}, u32[]{:S(2)}, u32[]{:S(2)}) %collective-permute-start) | collective-permute-done | bytes 131104 | tf_op jit(solution)/shard_map/ppermute | solution.py:118
  27.6 10.8 %all_to_all.25 = bf16[4,128,256]{2,1,0:T(8,128)(2,1)S(1)} all-to-all(bf16[4,128,256]{2,1,0:T(8,128)(2,1)S(1)} %bitcast.24), channel_id=1, replica_groups=mesh['dp'=8,'blk_0'=8,'blk_1'=2,'aa_0'=2,'aa_1'=4] {'aa_1'}, dimensions={0} | all-to-all | bytes 524288 | tf_op jit(solution)/shard_map/all_to_all | solution.py:132
  38.3 3.6 %all-to-all-start = ((bf16[4,128,512]{2,1,0:T(8,128)(2,1)}), bf16[4,128,512]{2,1,0:T(8,128)(2,1)S(1)}, u32[]{:S(2)}, u32[]{:S(2)}) async-start(bf16[4,128,512]{2,1,0:T(8,128)(2,1)} %get-tuple-element.5), calls=%async_computation | async-start | bytes 1048576 | tf_op jit(solution)/shard_map/all_to_all | solution.py:120
  41.9 0.6 broadcast.7
  42.5 1.9 %reduce.4 = f32[131072]{0:T(1024)S(1)} reduce(f32[1,1,131072]{2,1,0:T(1,128)S(1)} %copy-done.5, f32[]{:T(128)} %broadcast.7), dimensions={0,1}, to_apply=%param.7.reduce_sub_computation.3 | reduce | bytes 1048580 | tf_op args[3]
  44.4 0.2 reshape.40
  44.6 0.4 copy.10
  45.0 1.6 %reshape.42 = f32[64,1,2048]{2,1,0:T(1,128)} reshape(f32[16,4,2,1,1024]{4,2,1,0,3:T(2,128)S(1)} %bitcast.23) | data formatting | bytes 1048576 | tf_op jit(solution)/shard_map/reshape | solution.py:125
  46.6 3.4 %all-to-all-done = bf16[4,128,512]{2,1,0:T(8,128)(2,1)S(1)} async-done(((bf16[4,128,512]{2,1,0:T(8,128)(2,1)}), bf16[4,128,512]{2,1,0:T(8,128)(2,1)S(1)}, u32[]{:S(2)}, u32[]{:S(2)}) %all-to-all-start) | async-done | bytes 524320 | tf_op jit(solution)/shard_map/all_to_all | solution.py:120
  50.0 8.7 %all-to-all-start.3 = ((f32[64,1,2048]{2,1,0:T(1,128)}), f32[64,1,2048]{2,1,0:T(1,128)S(1)}, u32[]{:S(2)}, u32[]{:S(2)}) async-start(f32[64,1,2048]{2,1,0:T(1,128)} %reshape.42), calls=%async_computation.3 | async-start | bytes 1048576 | tf_op jit(solution)/shard_map/all_to_all | solution.py:126
  58.7 12.3 %collective-permute-start.1 = (bf16[4,128,256]{2,1,0:T(8,128)(2,1)S(1)}, bf16[4,128,256]{2,1,0:T(8,128)(2,1)}, u32[]{:S(2)}, u32[]{:S(2)}) collective-permute-start(bf16[4,128,256]{2,1,0:T(8,128)(2,1)S(1)} %get-tuple-element.7), channel_id=1, source_target_pairs={{0,4},{4,0},{1,5},{5,1},{2,6},{6,2},{3,7},{7,3},{8,12},{12,8},{9,1... | collective-permute-start | bytes 786440 | tf_op jit(solution)/shard_map/ppermute | solution.py:119
  71.0 6.8 %collective-permute-done.1 = bf16[4,128,256]{2,1,0:T(8,128)(2,1)} collective-permute-done((bf16[4,128,256]{2,1,0:T(8,128)(2,1)S(1)}, bf16[4,128,256]{2,1,0:T(8,128)(2,1)}, u32[]{:S(2)}, u32[]{:S(2)}) %collective-permute-start.1) | collective-permute-done | bytes 262176 | tf_op jit(solution)/shard_map/ppermute | solution.py:119
  77.8 0.0 all-to-all-done.3
  77.9 4.2 %all-to-all-start.2 = ((bf16[4,128,256]{2,1,0:T(8,128)(2,1)}), bf16[4,128,256]{2,1,0:T(8,128)(2,1)S(1)}, u32[]{:S(2)}, u32[]{:S(2)}) async-start(bf16[4,128,256]{2,1,0:T(8,128)(2,1)} %collective-permute-done.1), calls=%async_computation.2 | async-start | bytes 524288 | tf_op jit(solution)/shard_map/all_to_all | solution.py:138
  82.1 0.3 reduce_sum.18
  82.5 0.0 slice-start
  82.5 0.7 broadcast_in_dim.19
  83.2 5.6 %all-to-all-done.2 = bf16[4,128,256]{2,1,0:T(8,128)(2,1)S(1)} async-done(((bf16[4,128,256]{2,1,0:T(8,128)(2,1)}), bf16[4,128,256]{2,1,0:T(8,128)(2,1)S(1)}, u32[]{:S(2)}, u32[]{:S(2)}) %all-to-all-start.2) | async-done | bytes 262176 | tf_op jit(solution)/shard_map/all_to_all | solution.py:138
  88.8 34.7 %all-to-all-start.4 = ((f32[16,1,1024]{2,1,0:T(1,128)}), f32[16,1,1024]{2,1,0:T(1,128)S(1)}, u32[]{:S(2)}, u32[]{:S(2)}) async-start(f32[16,1,1024]{2,1,0:T(1,128)} %broadcast_in_dim.19), calls=%async_computation.4 | async-start | bytes 131072 | tf_op jit(solution)/shard_map/all_to_all | solution.py:129
  123.5 1.9 %collective-permute-start.2 = (bf16[256,256]{1,0:T(8,128)(2,1)S(1)}, bf16[256,256]{1,0:T(8,128)(2,1)S(1)}, u32[]{:S(2)}, u32[]{:S(2)}) collective-permute-start(bf16[256,256]{1,0:T(8,128)(2,1)S(1)} %slice_select_fusion), channel_id=1, source_target_pairs={{0,8},{8,16},{16,24},{24,32},{32,40},{40,48},{48,56},{56,64},{64,7... | collective-permute-start | bytes 393224 | tf_op jit(solution)/shard_map/ppermute | solution.py:137
  125.5 4.4 %collective-permute-done.2.prior_ref = bf16[256,256]{1,0:T(8,128)(2,1)S(1)} collective-permute-done((bf16[256,256]{1,0:T(8,128)(2,1)S(1)}, bf16[256,256]{1,0:T(8,128)(2,1)S(1)}, u32[]{:S(2)}, u32[]{:S(2)}) %collective-permute-start.2) | collective-permute-done | bytes 131104 | tf_op jit(solution)/shard_map/ppermute | solution.py:137
  129.8 0.0 copy-done.1
  129.8 4.3 %attend.1 = bf16[1024,256]{1,0:T(8,128)(2,1)} custom-call(s32[1]{0:T(128)} %bitcast.side_ref, bf16[512,512]{1,0:T(8,128)(2,1)S(1)} %bitcast.17, bf16[512,256]{1,0:T(8,128)(2,1)S(1)} %bitcast.18, bf16[512,256]{1,0:T(8,128)(2,1)S(1)} %bitcast.20, bf16[256,256]{1,0:T(8,128)(2,1)S(1)} %collective-permute-done.2.prior_ref), custom_call_target="tpu_custom_call" | custom-call | flops 536870912 | bytes 1048576 | tf_op jit(solution)/shard_map/attend/pallas_call | solution.py:95
  134.2 2.7 %all-to-all-done.4 = f32[16,1,1024]{2,1,0:T(1,128)S(1)} async-done(((f32[16,1,1024]{2,1,0:T(1,128)}), f32[16,1,1024]{2,1,0:T(1,128)S(1)}, u32[]{:S(2)}, u32[]{:S(2)}) %all-to-all-start.4) | async-done | bytes 65568 | tf_op jit(solution)/shard_map/all_to_all | solution.py:129
  136.8 0.1 reduce_sum.19
  136.9 0.6 broadcast_multiply_fusion
  (12 shorter events, 0.1 us)
Async XLA Ops:
  0.6 1.0 copy-start.2
  1.7 0.9 copy-start.3
  2.6 0.9 copy-start.4
  4.4 23.1 %collective-permute-start = (bf16[2,128,256]{2,1,0:T(8,128)(2,1)S(1)}, bf16[2,128,256]{2,1,0:T(8,128)(2,1)S(1)}, u32[]{:S(2)}, u32[]{:S(2)}) collective-permute-start(bf16[2,128,256]{2,1,0:T(8,128)(2,1)S(1)} %get-tuple-element.6), channel_id=1, source_target_pairs={{0,4},{4,0},{1,5},{5,1},{2,6},{6,2},{3,7},{7,3},{8,12},{12,8},{9,1... | collective-permute-start | bytes 393224 | tf_op jit(solution)/shard_map/ppermute | solution.py:118
  38.3 43.8 %copy-start = (bf16[4,128,256]{2,1,0:T(8,128)(2,1)}, bf16[4,128,256]{2,1,0:T(8,128)(2,1)S(1)}, u32[]{:S(2)}) copy-start(bf16[4,128,256]{2,1,0:T(8,128)(2,1)S(1)} %all_to_all.25) | copy-start | bytes 786436
  38.3 4.2 %copy-start.5 = (f32[1,1,131072]{2,1,0:T(1,128)S(1)}, f32[1,1,131072]{2,1,0:T(1,128)}, u32[]{:S(2)}) copy-start(f32[1,1,131072]{2,1,0:T(1,128)} %param.7) | copy-start | bytes 1572868
  38.3 11.7 %all-to-all-start = ((bf16[4,128,512]{2,1,0:T(8,128)(2,1)}), bf16[4,128,512]{2,1,0:T(8,128)(2,1)S(1)}, u32[]{:S(2)}, u32[]{:S(2)}) async-start(bf16[4,128,512]{2,1,0:T(8,128)(2,1)} %get-tuple-element.5), calls=%async_computation | async-start | bytes 1048576 | tf_op jit(solution)/shard_map/all_to_all | solution.py:120
  50.0 27.9 %all-to-all-start.3 = ((f32[64,1,2048]{2,1,0:T(1,128)}), f32[64,1,2048]{2,1,0:T(1,128)S(1)}, u32[]{:S(2)}, u32[]{:S(2)}) async-start(f32[64,1,2048]{2,1,0:T(1,128)} %reshape.42), calls=%async_computation.3 | async-start | bytes 1048576 | tf_op jit(solution)/shard_map/all_to_all | solution.py:126
  58.7 19.1 %collective-permute-start.1 = (bf16[4,128,256]{2,1,0:T(8,128)(2,1)S(1)}, bf16[4,128,256]{2,1,0:T(8,128)(2,1)}, u32[]{:S(2)}, u32[]{:S(2)}) collective-permute-start(bf16[4,128,256]{2,1,0:T(8,128)(2,1)S(1)} %get-tuple-element.7), channel_id=1, source_target_pairs={{0,4},{4,0},{1,5},{5,1},{2,6},{6,2},{3,7},{7,3},{8,12},{12,8},{9,1... | collective-permute-start | bytes 786440 | tf_op jit(solution)/shard_map/ppermute | solution.py:119
  77.9 10.9 %all-to-all-start.2 = ((bf16[4,128,256]{2,1,0:T(8,128)(2,1)}), bf16[4,128,256]{2,1,0:T(8,128)(2,1)S(1)}, u32[]{:S(2)}, u32[]{:S(2)}) async-start(bf16[4,128,256]{2,1,0:T(8,128)(2,1)} %collective-permute-done.1), calls=%async_computation.2 | async-start | bytes 524288 | tf_op jit(solution)/shard_map/all_to_all | solution.py:138
  82.5 41.0 %slice-start = ((bf16[4,128,256]{2,1,0:T(8,128)(2,1)}), bf16[2,128,256]{2,1,0:T(8,128)(2,1)S(1)}, s32[]{:S(2)}) async-start(bf16[4,128,256]{2,1,0:T(8,128)(2,1)} %copy-done), calls=%async_computation.5 | async-start | bytes 262144 | tf_op jit(solution)/shard_map/slice | solution.py:136
  83.2 46.6 %copy-start.1 = (bf16[4,128,256]{2,1,0:T(8,128)(2,1)S(1)}, bf16[4,128,256]{2,1,0:T(8,128)(2,1)}, u32[]{:S(2)}) copy-start(bf16[4,128,256]{2,1,0:T(8,128)(2,1)} %copy-done) | copy-start | bytes 786436
  88.8 48.1 %all-to-all-start.4 = ((f32[16,1,1024]{2,1,0:T(1,128)}), f32[16,1,1024]{2,1,0:T(1,128)S(1)}, u32[]{:S(2)}, u32[]{:S(2)}) async-start(f32[16,1,1024]{2,1,0:T(1,128)} %broadcast_in_dim.19), calls=%async_computation.4 | async-start | bytes 131072 | tf_op jit(solution)/shard_map/all_to_all | solution.py:129
  123.5 6.3 %collective-permute-start.2 = (bf16[256,256]{1,0:T(8,128)(2,1)S(1)}, bf16[256,256]{1,0:T(8,128)(2,1)S(1)}, u32[]{:S(2)}, u32[]{:S(2)}) collective-permute-start(bf16[256,256]{1,0:T(8,128)(2,1)S(1)} %slice_select_fusion), channel_id=1, source_target_pairs={{0,8},{8,16},{16,24},{24,32},{32,40},{40,48},{48,56},{56,64},{64,7... | collective-permute-start | bytes 393224 | tf_op jit(solution)/shard_map/ppermute | solution.py:137

commit v2 on v1

v2 whole, which is shorter than its diff:
```python
import jax
import jax.numpy as jnp
from jax import lax
from jax.experimental import pallas as pl
from jax.experimental.pallas import tpu as pltpu
from jax.sharding import Mesh
from jax.sharding import PartitionSpec as P

DH = 128
BLK = ("blk_0", "blk_1")
AA = ("aa_0", "aa_1")
BLK_AA = ("blk_0", "blk_1", "aa_0", "aa_1")


def place(at_ref, n):
    at = at_ref[0]
    return lax.div(at, n), lax.rem(at, n)


def pack_kernel(n, at_ref, q_ref, k_ref, v_ref, g_ref, *refs):
    kv_to, q_to, near_to, g_to, sems = refs[:2], refs[2 : 2 + n], refs[2 + n : 2 + 2 * n], refs[-2], refs[-1]
    side, x = place(at_ref, n)
    wide = q_to[0].shape[1]
    moves = []

    def lanes(ref, index, width):
        return ref.at[:, pl.ds(pl.multiple_of(index * width, width), width)]

    def kv_move(head, to, at):
        moves.append((lanes(k_ref, head, DH), to.at[:, at : at + DH]))
        moves.append((lanes(v_ref, head, DH), to.at[:, at + DH : at + 2 * DH]))

    for hop, to in zip((0, n // 2), kv_to):
        kv_move((1 - side) * (n // 2) + lax.div(lax.rem(x + hop, n), 2), to, 0)
    for hop in range(n):
        target = lax.rem(x + hop, n)
        moves.append((lanes(q_ref, (1 - side) * n + target, wide), q_to[hop]))
        moves.append((lanes(q_ref, side * n + target, wide), near_to[hop].at[:, :wide]))
        kv_move(side * (n // 2) + lax.div(target, 2), near_to[hop], wide)
    chunk = g_ref.shape[-1]
    for z in range(g_ref.shape[1]):
        moves.append((g_ref.at[:, z], g_to.at[:, :, :, z * chunk : (z + 1) * chunk]))
    copies = [pltpu.make_async_copy(a, b, sems.at[i]) for i, (a, b) in enumerate(moves)]
    for copy in copies:
        copy.start()
    for copy in copies:
        copy.wait()


def packed(at, q, k, v, g, n):
    rows, wide = q.shape[0], q.shape[1] // (2 * n)
    vmem = pl.BlockSpec(memory_space=pltpu.VMEM)
    hbm = pl.BlockSpec(memory_space=pltpu.HBM)
    piece = jax.ShapeDtypeStruct((rows, wide), q.dtype)
    near = jax.ShapeDtypeStruct((rows, wide + 2 * DH), q.dtype)
    yc, z, x, _, chunk = g.shape
    outs = (
        *(jax.ShapeDtypeStruct((rows, 2 * DH), q.dtype),) * 2,
        *(piece,) * n,
        *(near,) * n,
        jax.ShapeDtypeStruct((yc, x, 1, z * chunk), g.dtype),
    )
    found = pl.pallas_call(
        lambda *refs: pack_kernel(n, *refs),
        out_shape=outs,
        in_specs=[pl.BlockSpec(memory_space=pltpu.SMEM), hbm, hbm, hbm, hbm],
        out_specs=(vmem,) * len(outs),
        scratch_shapes=[pltpu.SemaphoreType.DMA((4 + 4 * n + z,))],
        compiler_params=pltpu.CompilerParams(vmem_limit_bytes=8 << 20),
        name="pack",
    )(at, q, k, v, g)
    return found[:2], found[2 : 2 + n], found[2 + n : 2 + 2 * n], found[-1]


def gather_kernel(n, at_ref, *refs):
    near, own, swapped, (kv_ref, last_ref) = refs[:n], refs[n : n + 2], refs[n + 2], refs[n + 3 :]
    side, x = place(at_ref, n)
    rows, width = own[0].shape

    def put(half, chunk, value):
        kv_ref[pl.ds(pl.multiple_of((half * n + chunk) * rows, rows), rows)] = value

    for hop in range(n):
        put(side, lax.rem(x + n - hop, n), near[hop][:, -width:])
    mate = x + 1 - 2 * lax.rem(x, 2)
    for i, hop in enumerate((0, n // 2)):
        put(1 - side, lax.rem(x + hop, n), own[i][...])
        put(1 - side, lax.rem(mate + hop, n), swapped[i])
    last_ref[...] = kv_ref[kv_ref.shape[0] - last_ref.shape[0] :]


def gathered(at, near, own, swapped, reach):
    n = len(near)
    rows, width = own[0].shape
    vmem = pl.BlockSpec(memory_space=pltpu.VMEM)
    return pl.pallas_call(
        lambda *refs: gather_kernel(n, *refs),
        out_shape=(
            jax.ShapeDtypeStruct((2 * n * rows, width), jnp.bfloat16),
            jax.ShapeDtypeStruct((reach, width), jnp.bfloat16),
        ),
        in_specs=[pl.BlockSpec(memory_space=pltpu.SMEM)] + [vmem] * (n + 3),
        out_specs=(vmem, vmem),
        compiler_params=pltpu.CompilerParams(vmem_limit_bytes=8 << 20),
        name="gather",
    )(at, *near, *own, swapped)


def attend_kernel(n, at_ref, kv_ref, prior_ref, *refs):
    near, far, out_ref, q_s = refs[:n], refs[n : 2 * n], refs[2 * n], refs[2 * n + 1]
    side, x = place(at_ref, n)
    rows, wide = far[0].shape
    reach = prior_ref.shape[0]
    for hop in range(n):
        chunk = lax.rem(x + n - hop, n)
        q_s[pl.ds(pl.multiple_of((side * n + chunk) * rows, rows), rows)] = near[hop][:, :wide]
        q_s[pl.ds(pl.multiple_of(((1 - side) * n + chunk) * rows, rows), rows)] = far[hop][...]
    row = lax.broadcasted_iota(jnp.int32, (reach, reach), 0)
    col = lax.broadcasted_iota(jnp.int32, (reach, reach), 1)
    newer = col <= row
    across = (((1,), (1,)), ((), ()))
    for block in range(2 * n * rows // reach):
        here = pl.ds(block * reach, reach)
        older_ref, older = (kv_ref, pl.ds((block - 1) * reach, reach)) if block else (prior_ref, slice(None))
        for head in range(wide // DH):
            lanes = pl.ds(head * DH, DH)
            q = q_s[here, lanes]
            old = lax.dot_general(q, older_ref[older, :DH], across, preferred_element_type=jnp.float32)
            new = lax.dot_general(q, kv_ref[here, :DH], across, preferred_element_type=jnp.float32)
            scores = jnp.where(newer, new, old) * DH**-0.5
            expo = jnp.exp(scores - jnp.max(scores, axis=-1, keepdims=True))
            weights = (expo / jnp.sum(expo, axis=-1, keepdims=True)).astype(jnp.bfloat16)
            none = jnp.zeros_like(weights)
            out = jnp.dot(
                jnp.where(newer, weights, none), kv_ref[here, DH:], preferred_element_type=jnp.float32
            ) + jnp.dot(
                jnp.where(newer, none, weights), older_ref[older, DH:], preferred_element_type=jnp.float32
            )
            out_ref[here, lanes] = out.astype(jnp.bfloat16)


def attended_rows(at, kv, prior, near, far):
    n = len(near)
    wide, reach = far[0].shape[1], prior.shape[0]
    vmem = pl.BlockSpec(memory_space=pltpu.VMEM)
    total = kv.shape[0]
    return pl.pallas_call(
        lambda *refs: attend_kernel(n, *refs),
        out_shape=jax.ShapeDtypeStruct((total, wide), jnp.bfloat16),
        in_specs=[pl.BlockSpec(memory_space=pltpu.SMEM)] + [vmem] * (2 + 2 * n),
        out_specs=vmem,
        scratch_shapes=[pltpu.VMEM((total, wide), jnp.bfloat16)],
        cost_estimate=pl.CostEstimate(
            flops=8 * total * wide * reach, bytes_accessed=4 * total * wide * 2, transcendentals=2 * total * reach
        ),
        compiler_params=pltpu.CompilerParams(vmem_limit_bytes=16 << 20),
        name="attend",
    )(at, kv, prior, *near, *far)


def step(queries, keys, values, grad_parts):
    dp, y, c, z, n = (lax.axis_size(a) for a in ("dp", *BLK_AA))
    at = lax.axis_index(AA).astype(jnp.int32).reshape(1)
    chunks = grad_parts.reshape(y * c, z, n, 1, -1)
    kv_far, q_far, near, parts = packed(at, queries[0], keys[0], values[0], chunks, n)

    def hopped(value, hop, across):
        pairs = [
            (s * n + x, (1 - s if across else s) * n + (x + hop) % n) for s in range(z) for x in range(n)
        ]
        return lax.ppermute(value, AA, pairs)

    own = [hopped(kv_far[i], hop, True) for i, hop in enumerate((0, n // 2))]
    far = [hopped(q_far[hop], hop, True) for hop in range(n)]
    parts = parts.reshape(y * c * n, 1, -1)
    parts = lax.all_to_all(parts, ("blk_0", "blk_1", "aa_1"), 0, 0, tiled=True)
    near = [near[0]] + [hopped(near[hop], hop, False) for hop in range(1, n)]
    pairs = [(x, x ^ 1) for x in range(n)]
    swapped = lax.ppermute(jnp.stack(own), "aa_1", pairs)
    reach = queries.shape[1] * 2
    kv, last = gathered(at, near, own, swapped, reach)
    prior = lax.ppermute(last, BLK, [(i, i + 1) for i in range(y * c - 1)])

    share = jnp.sum(parts, axis=0).reshape(z, 1, -1)
    share = jnp.broadcast_to(share[None], (dp, *share.shape)).reshape(dp * z, 1, -1)
    share = lax.all_to_all(share, ("dp", "aa_0"), 0, 0, tiled=True)
    grad_mean = jnp.sum(share, axis=(0, 1)) / (dp * y * c * z * n)

    attended = attended_rows(at, kv, prior, near, far)
    return attended[None], grad_mean


def solution(mesh):
    torus = Mesh(
        mesh.devices.reshape(mesh.shape["dp"], 8, 2, 2, 4), ("dp", "blk_0", "blk_1", "aa_0", "aa_1")
    )
    placed = P("dp", BLK_AA, None)
    return jax.shard_map(
        step,
        mesh=torus,
        in_specs=(placed,) * 4,
        out_specs=(P("dp", BLK, AA), P(BLK_AA)),
        check_vma=False,
    )
```

time: 138 us -> 124 us (0.90)
  the two profiles are of different devices: /device:TPU:8 before, /device:TPU:15 now
where the time goes in v2:
time: 124 us
  starting transfers between devices  87.4 us (70%)
  waiting for transfers between devices  24.3 us (20%)
  Pallas kernels  5.54 us (4%)
  local copies, waits for them, and re-layouts  4.64 us (4%)
    ppermute x9, starting transfers between devices, hopped(): return lax.ppermute(value, AA, pairs)  52.7 us
    ppermute x9, waiting for transfers between devices, hopped(): return lax.ppermute(value, AA, pairs)  24.3 us
    all_to_all x1, starting transfers between devices, step(): parts = lax.all_to_all(parts, ('blk_0', 'blk_1', 'aa_1'), 0, 0, tiled=True)  17.4 us
    all_to_all x1, starting transfers between devices, step(): share = lax.all_to_all(share, ('dp', 'aa_0'), 0, 0, tiled=True)  8.68 us
    ppermute x1, starting transfers between devices, step(): prior = lax.ppermute(last, BLK, [(i, i + 1) for i in range(y * c - 1)])  6.62 us
    pallas_call x1, Pallas kernels, attended_rows(): pl.pallas_call(lambda *refs: attend_kernel(n, *refs), out_shape=jax.Shape...  4.23 us
    unnamed x8, local copies, waits for them, and re-layouts  3.88 us
  transfers between devices with their start and end apart: 13, of which 3 were waited for; matrix products, arithmetic and copies ran while one was open for 1% of the time, Pallas kernels for 3%

profile of v2, /device:TPU:15, one launch (start us, length us, event | category | flops | bytes accessed | tf_op | source)
XLA Modules:
  0.0 123.7 jit_solution(1315349976941179566)
XLA Ops:
  0.6 1.0 copy-done
  1.7 1.0 copy-done.1
  2.7 0.9 copy-done.2
  3.6 0.9 copy-done.3
  4.5 1.2 %pack.1 = (bf16[128,256]{1,0:T(8,128)(2,1)S(1)}, bf16[128,256]{1,0:T(8,128)(2,1)S(1)}, bf16[128,256]{1,0:T(8,128)(2,1)S(1)}, bf16[128,256]{1,0:T(8,128)(2,1)S(1)...) custom-call(s32[1]{0:T(128)} %bitcast.refs_0_, ...), custom_call_target="tpu_custom_call" | custom-call | tf_op jit(solution)/shard_map/pack/pallas_call | solution.py:63
  5.8 17.4 %all-to-all-start = ((f32[64,1,2048]{2,1,0:T(1,128)}), f32[64,1,2048]{2,1,0:T(1,128)S(1)}, u32[]{:S(2)}, u32[]{:S(2)}) async-start(f32[64,1,2048]{2,1,0:T(1,128)} %bitcast.8), calls=%async_computation | async-start | bytes 1048576 | tf_op jit(solution)/shard_map/all_to_all | solution.py:176
  23.2 12.4 %collective-permute-start.3 = (bf16[128,256]{1,0:T(8,128)(2,1)S(1)}, bf16[128,256]{1,0:T(8,128)(2,1)S(1)}, u32[]{:S(2)}, u32[]{:S(2)}) collective-permute-start(bf16[128,256]{1,0:T(8,128)(2,1)S(1)} %get-tuple-element.19), channel_id=1, source_target_pairs={{0,4},{1,5},{2,6},{3,7},{4,0},{5,1},{6,2},{7,3},{8,12},{9,13},{10,... | collective-permute-start | bytes 196616 | tf_op jit(solution)/shard_map/ppermute | solution.py:171
  35.7 2.8 %collective-permute-start.4 = (bf16[128,256]{1,0:T(8,128)(2,1)S(1)}, bf16[128,256]{1,0:T(8,128)(2,1)S(1)}, u32[]{:S(2)}, u32[]{:S(2)}) collective-permute-start(bf16[128,256]{1,0:T(8,128)(2,1)S(1)} %get-tuple-element.20), channel_id=1, source_target_pairs={{0,6},{1,7},{2,4},{3,5},{4,2},{5,3},{6,0},{7,1},{8,14},{9,15},{10,... | collective-permute-start | bytes 196616 | tf_op jit(solution)/shard_map/ppermute | solution.py:171
  38.5 3.7 %collective-permute-start = (bf16[128,512]{1,0:T(8,128)(2,1)S(1)}, bf16[128,512]{1,0:T(8,128)(2,1)S(1)}, u32[]{:S(2)}, u32[]{:S(2)}) collective-permute-start(bf16[128,512]{1,0:T(8,128)(2,1)S(1)} %get-tuple-element.16), channel_id=1, source_target_pairs={{0,1},{1,2},{2,3},{3,0},{4,5},{5,6},{6,7},{7,4},{8,9},{9,10},{10,1... | collective-permute-start | bytes 393224 | tf_op jit(solution)/shard_map/ppermute | solution.py:171
  42.2 1.9 %collective-permute-start.1 = (bf16[128,512]{1,0:T(8,128)(2,1)S(1)}, bf16[128,512]{1,0:T(8,128)(2,1)S(1)}, u32[]{:S(2)}, u32[]{:S(2)}) collective-permute-start(bf16[128,512]{1,0:T(8,128)(2,1)S(1)} %get-tuple-element.17), channel_id=1, source_target_pairs={{0,2},{1,3},{2,0},{3,1},{4,6},{5,7},{6,4},{7,5},{8,10},{9,11},{10,... | collective-permute-start | bytes 393224 | tf_op jit(solution)/shard_map/ppermute | solution.py:171
  44.1 2.8 %collective-permute-start.2 = (bf16[128,512]{1,0:T(8,128)(2,1)S(1)}, bf16[128,512]{1,0:T(8,128)(2,1)S(1)}, u32[]{:S(2)}, u32[]{:S(2)}) collective-permute-start(bf16[128,512]{1,0:T(8,128)(2,1)S(1)} %get-tuple-element.18), channel_id=1, source_target_pairs={{0,3},{1,0},{2,1},{3,2},{4,7},{5,4},{6,5},{7,6},{8,11},{9,8},{10,9... | collective-permute-start | bytes 393224 | tf_op jit(solution)/shard_map/ppermute | solution.py:171
  46.9 6.3 %collective-permute-done.4.refs_6_ = bf16[128,256]{1,0:T(8,128)(2,1)S(1)} collective-permute-done((bf16[128,256]{1,0:T(8,128)(2,1)S(1)}, bf16[128,256]{1,0:T(8,128)(2,1)S(1)}, u32[]{:S(2)}, u32[]{:S(2)}) %collective-permute-start.4) | collective-permute-done | bytes 65568 | tf_op jit(solution)/shard_map/ppermute | solution.py:171
  53.2 1.9 %collective-permute-start.5 = (bf16[2,128,256]{2,1,0:T(8,128)(2,1)S(1)}, bf16[2,128,256]{2,1,0:T(8,128)(2,1)S(1)}, u32[]{:S(2)}, u32[]{:S(2)}) collective-permute-start(bf16[2,128,256]{2,1,0:T(8,128)(2,1)S(1)} %pad_maximum_fusion), channel_id=1, source_target_pairs={{0,1},{1,0},{2,3},{3,2},{4,5},{5,4},{6,7},{7,6},{8,9},{9,8},{10,11... | collective-permute-start | bytes 393224 | tf_op jit(solution)/shard_map/ppermute | solution.py:179
  55.2 0.3 reduce_sum.18
  55.5 0.7 broadcast_in_dim.15
  56.2 8.7 %all-to-all-start.1 = ((f32[16,1,1024]{2,1,0:T(1,128)}), f32[16,1,1024]{2,1,0:T(1,128)S(1)}, u32[]{:S(2)}, u32[]{:S(2)}) async-start(f32[16,1,1024]{2,1,0:T(1,128)} %broadcast_in_dim.15), calls=%async_computation.1 | async-start | bytes 131072 | tf_op jit(solution)/shard_map/all_to_all | solution.py:186
  64.9 0.0 collective-permute-done.refs_2_.refs_4_
  64.9 0.0 collective-permute-done.1.refs_3_.refs_5_
  65.0 0.0 collective-permute-done.5.refs_7_
  65.0 0.1 gather.1
  65.0 6.6 %collective-permute-start.6 = (bf16[256,256]{1,0:T(8,128)(2,1)S(1)}, bf16[256,256]{1,0:T(8,128)(2,1)S(1)}, u32[]{:S(2)}, u32[]{:S(2)}) collective-permute-start(bf16[256,256]{1,0:T(8,128)(2,1)S(1)} %get-tuple-element.22), channel_id=1, source_target_pairs={{0,8},{8,16},{16,24},{24,32},{32,40},{40,48},{48,56},{56,64},{64,7... | collective-permute-start | bytes 393224 | tf_op jit(solution)/shard_map/ppermute | solution.py:182
  71.7 12.3 %collective-permute-start.7 = (bf16[128,256]{1,0:T(8,128)(2,1)S(1)}, bf16[128,256]{1,0:T(8,128)(2,1)S(1)}, u32[]{:S(2)}, u32[]{:S(2)}) collective-permute-start(bf16[128,256]{1,0:T(8,128)(2,1)S(1)} %get-tuple-element.23), channel_id=1, source_target_pairs={{0,4},{1,5},{2,6},{3,7},{4,0},{5,1},{6,2},{7,3},{8,12},{9,13},{10,... | collective-permute-start | bytes 196616 | tf_op jit(solution)/shard_map/ppermute | solution.py:171
  83.9 1.9 %collective-permute-start.8 = (bf16[128,256]{1,0:T(8,128)(2,1)S(1)}, bf16[128,256]{1,0:T(8,128)(2,1)S(1)}, u32[]{:S(2)}, u32[]{:S(2)}) collective-permute-start(bf16[128,256]{1,0:T(8,128)(2,1)S(1)} %get-tuple-element.24), channel_id=1, source_target_pairs={{0,5},{1,6},{2,7},{3,4},{4,1},{5,2},{6,3},{7,0},{8,13},{9,14},{10,... | collective-permute-start | bytes 196616 | tf_op jit(solution)/shard_map/ppermute | solution.py:171
  85.9 13.0 %collective-permute-start.9 = (bf16[128,256]{1,0:T(8,128)(2,1)S(1)}, bf16[128,256]{1,0:T(8,128)(2,1)S(1)}, u32[]{:S(2)}, u32[]{:S(2)}) collective-permute-start(bf16[128,256]{1,0:T(8,128)(2,1)S(1)} %get-tuple-element.25), channel_id=1, source_target_pairs={{0,6},{1,7},{2,4},{3,5},{4,2},{5,3},{6,0},{7,1},{8,14},{9,15},{10,... | collective-permute-start | bytes 196616 | tf_op jit(solution)/shard_map/ppermute | solution.py:171
  98.9 1.9 %collective-permute-start.10 = (bf16[128,256]{1,0:T(8,128)(2,1)S(1)}, bf16[128,256]{1,0:T(8,128)(2,1)S(1)}, u32[]{:S(2)}, u32[]{:S(2)}) collective-permute-start(bf16[128,256]{1,0:T(8,128)(2,1)S(1)} %get-tuple-element.26), channel_id=1, source_target_pairs={{0,7},{1,4},{2,5},{3,6},{4,3},{5,0},{6,1},{7,2},{8,15},{9,12},{10,... | collective-permute-start | bytes 196616 | tf_op jit(solution)/shard_map/ppermute | solution.py:171
  100.8 0.0 collective-permute-done.8.refs_8_
  100.8 7.3 %collective-permute-done.9.refs_9_ = bf16[128,256]{1,0:T(8,128)(2,1)S(1)} collective-permute-done((bf16[128,256]{1,0:T(8,128)(2,1)S(1)}, bf16[128,256]{1,0:T(8,128)(2,1)S(1)}, u32[]{:S(2)}, u32[]{:S(2)}) %collective-permute-start.9) | collective-permute-done | bytes 65568 | tf_op jit(solution)/shard_map/ppermute | solution.py:171
  108.1 10.6 %collective-permute-done.10.refs_10_ = bf16[128,256]{1,0:T(8,128)(2,1)S(1)} collective-permute-done((bf16[128,256]{1,0:T(8,128)(2,1)S(1)}, bf16[128,256]{1,0:T(8,128)(2,1)S(1)}, u32[]{:S(2)}, u32[]{:S(2)}) %collective-permute-start.10) | collective-permute-done | bytes 65568 | tf_op jit(solution)/shard_map/ppermute | solution.py:171
  118.8 0.0 collective-permute-done.6.refs_2_
  118.8 4.2 %attend.1 = bf16[1024,256]{1,0:T(8,128)(2,1)} custom-call(s32[1]{0:T(128)} %bitcast.refs_0_, bf16[1024,256]{1,0:T(8,128)(2,1)S(1)} %get-tuple-element.21.refs_1_, bf16[256,256]{1,0:T(8,128)(2,1)S(1)} %collective-permute-done.6.refs_2_, bf16[128,512]{1,0:T(8,128)(2,1)S(1)} %get-tuple-element.15.refs_1_.refs_3_, ...), custom_call_target="tpu_custom_call" | custom-call | flops 536870912 | bytes 2097152 | tf_op jit(solution)/shard_map/attend/pallas_call | solution.py:147
  123.0 0.1 reduce_sum.19
  123.1 0.6 broadcast_multiply_fusion
  (12 shorter events, 0.1 us)
Async XLA Ops:
  0.6 1.0 copy-start
  1.7 1.0 copy-start.1
  2.7 0.9 copy-start.2
  3.6 0.9 copy-start.3
  5.8 49.4 %all-to-all-start = ((f32[64,1,2048]{2,1,0:T(1,128)}), f32[64,1,2048]{2,1,0:T(1,128)S(1)}, u32[]{:S(2)}, u32[]{:S(2)}) async-start(f32[64,1,2048]{2,1,0:T(1,128)} %bitcast.8), calls=%async_computation | async-start | bytes 1048576 | tf_op jit(solution)/shard_map/all_to_all | solution.py:176
  23.2 23.7 %collective-permute-start.3 = (bf16[128,256]{1,0:T(8,128)(2,1)S(1)}, bf16[128,256]{1,0:T(8,128)(2,1)S(1)}, u32[]{:S(2)}, u32[]{:S(2)}) collective-permute-start(bf16[128,256]{1,0:T(8,128)(2,1)S(1)} %get-tuple-element.19), channel_id=1, source_target_pairs={{0,4},{1,5},{2,6},{3,7},{4,0},{5,1},{6,2},{7,3},{8,12},{9,13},{10,... | collective-permute-start | bytes 196616 | tf_op jit(solution)/shard_map/ppermute | solution.py:171
  35.7 17.5 %collective-permute-start.4 = (bf16[128,256]{1,0:T(8,128)(2,1)S(1)}, bf16[128,256]{1,0:T(8,128)(2,1)S(1)}, u32[]{:S(2)}, u32[]{:S(2)}) collective-permute-start(bf16[128,256]{1,0:T(8,128)(2,1)S(1)} %get-tuple-element.20), channel_id=1, source_target_pairs={{0,6},{1,7},{2,4},{3,5},{4,2},{5,3},{6,0},{7,1},{8,14},{9,15},{10,... | collective-permute-start | bytes 196616 | tf_op jit(solution)/shard_map/ppermute | solution.py:171
  38.5 26.4 %collective-permute-start = (bf16[128,512]{1,0:T(8,128)(2,1)S(1)}, bf16[128,512]{1,0:T(8,128)(2,1)S(1)}, u32[]{:S(2)}, u32[]{:S(2)}) collective-permute-start(bf16[128,512]{1,0:T(8,128)(2,1)S(1)} %get-tuple-element.16), channel_id=1, source_target_pairs={{0,1},{1,2},{2,3},{3,0},{4,5},{5,6},{6,7},{7,4},{8,9},{9,10},{10,1... | collective-permute-start | bytes 393224 | tf_op jit(solution)/shard_map/ppermute | solution.py:171
  42.2 22.7 %collective-permute-start.1 = (bf16[128,512]{1,0:T(8,128)(2,1)S(1)}, bf16[128,512]{1,0:T(8,128)(2,1)S(1)}, u32[]{:S(2)}, u32[]{:S(2)}) collective-permute-start(bf16[128,512]{1,0:T(8,128)(2,1)S(1)} %get-tuple-element.17), channel_id=1, source_target_pairs={{0,2},{1,3},{2,0},{3,1},{4,6},{5,7},{6,4},{7,5},{8,10},{9,11},{10,... | collective-permute-start | bytes 393224 | tf_op jit(solution)/shard_map/ppermute | solution.py:171
  44.1 20.8 %collective-permute-start.2 = (bf16[128,512]{1,0:T(8,128)(2,1)S(1)}, bf16[128,512]{1,0:T(8,128)(2,1)S(1)}, u32[]{:S(2)}, u32[]{:S(2)}) collective-permute-start(bf16[128,512]{1,0:T(8,128)(2,1)S(1)} %get-tuple-element.18), channel_id=1, source_target_pairs={{0,3},{1,0},{2,1},{3,2},{4,7},{5,4},{6,5},{7,6},{8,11},{9,8},{10,9... | collective-permute-start | bytes 393224 | tf_op jit(solution)/shard_map/ppermute | solution.py:171
  53.2 11.7 %collective-permute-start.5 = (bf16[2,128,256]{2,1,0:T(8,128)(2,1)S(1)}, bf16[2,128,256]{2,1,0:T(8,128)(2,1)S(1)}, u32[]{:S(2)}, u32[]{:S(2)}) collective-permute-start(bf16[2,128,256]{2,1,0:T(8,128)(2,1)S(1)} %pad_maximum_fusion), channel_id=1, source_target_pairs={{0,1},{1,0},{2,3},{3,2},{4,5},{5,4},{6,7},{7,6},{8,9},{9,8},{10,11... | collective-permute-start | bytes 393224 | tf_op jit(solution)/shard_map/ppermute | solution.py:179
  56.2 66.8 %all-to-all-start.1 = ((f32[16,1,1024]{2,1,0:T(1,128)}), f32[16,1,1024]{2,1,0:T(1,128)S(1)}, u32[]{:S(2)}, u32[]{:S(2)}) async-start(f32[16,1,1024]{2,1,0:T(1,128)} %broadcast_in_dim.15), calls=%async_computation.1 | async-start | bytes 131072 | tf_op jit(solution)/shard_map/all_to_all | solution.py:186
  65.0 53.8 %collective-permute-start.6 = (bf16[256,256]{1,0:T(8,128)(2,1)S(1)}, bf16[256,256]{1,0:T(8,128)(2,1)S(1)}, u32[]{:S(2)}, u32[]{:S(2)}) collective-permute-start(bf16[256,256]{1,0:T(8,128)(2,1)S(1)} %get-tuple-element.22), channel_id=1, source_target_pairs={{0,8},{8,16},{16,24},{24,32},{32,40},{40,48},{48,56},{56,64},{64,7... | collective-permute-start | bytes 393224 | tf_op jit(solution)/shard_map/ppermute | solution.py:182
  71.7 29.2 %collective-permute-start.7 = (bf16[128,256]{1,0:T(8,128)(2,1)S(1)}, bf16[128,256]{1,0:T(8,128)(2,1)S(1)}, u32[]{:S(2)}, u32[]{:S(2)}) collective-permute-start(bf16[128,256]{1,0:T(8,128)(2,1)S(1)} %get-tuple-element.23), channel_id=1, source_target_pairs={{0,4},{1,5},{2,6},{3,7},{4,0},{5,1},{6,2},{7,3},{8,12},{9,13},{10,... | collective-permute-start | bytes 196616 | tf_op jit(solution)/shard_map/ppermute | solution.py:171
  83.9 16.9 %collective-permute-start.8 = (bf16[128,256]{1,0:T(8,128)(2,1)S(1)}, bf16[128,256]{1,0:T(8,128)(2,1)S(1)}, u32[]{:S(2)}, u32[]{:S(2)}) collective-permute-start(bf16[128,256]{1,0:T(8,128)(2,1)S(1)} %get-tuple-element.24), channel_id=1, source_target_pairs={{0,5},{1,6},{2,7},{3,4},{4,1},{5,2},{6,3},{7,0},{8,13},{9,14},{10,... | collective-permute-start | bytes 196616 | tf_op jit(solution)/shard_map/ppermute | solution.py:171
  85.9 22.3 %collective-permute-start.9 = (bf16[128,256]{1,0:T(8,128)(2,1)S(1)}, bf16[128,256]{1,0:T(8,128)(2,1)S(1)}, u32[]{:S(2)}, u32[]{:S(2)}) collective-permute-start(bf16[128,256]{1,0:T(8,128)(2,1)S(1)} %get-tuple-element.25), channel_id=1, source_target_pairs={{0,6},{1,7},{2,4},{3,5},{4,2},{5,3},{6,0},{7,1},{8,14},{9,15},{10,... | collective-permute-start | bytes 196616 | tf_op jit(solution)/shard_map/ppermute | solution.py:171
  98.9 19.9 %collective-permute-start.10 = (bf16[128,256]{1,0:T(8,128)(2,1)S(1)}, bf16[128,256]{1,0:T(8,128)(2,1)S(1)}, u32[]{:S(2)}, u32[]{:S(2)}) collective-permute-start(bf16[128,256]{1,0:T(8,128)(2,1)S(1)} %get-tuple-element.26), channel_id=1, source_target_pairs={{0,7},{1,4},{2,5},{3,6},{4,3},{5,0},{6,1},{7,2},{8,15},{9,12},{10,... | collective-permute-start | bytes 196616 | tf_op jit(solution)/shard_map/ppermute | solution.py:171

commit v3 on v2

v3 whole, which is shorter than its diff:
```python
import jax
import jax.numpy as jnp
from jax import lax
from jax.experimental import pallas as pl
from jax.experimental.pallas import tpu as pltpu
from jax.sharding import Mesh
from jax.sharding import PartitionSpec as P

DH = 128
BLK = ("blk_0", "blk_1")
AA = ("aa_0", "aa_1")
BLK_AA = ("blk_0", "blk_1", "aa_0", "aa_1")


def place(at_ref, n):
    at = at_ref[0]
    return lax.div(at, n), lax.rem(at, n)


def place(at_ref, n):
    at = at_ref[0]
    return lax.div(at, n), lax.rem(at, n)


def run_all(moves, sems):
    copies = [pltpu.make_async_copy(a, b, sems.at[i]) for i, (a, b) in enumerate(moves)]
    for copy in copies:
        copy.start()
    for copy in copies:
        copy.wait()


def lanes_of(ref, index, width):
    return ref.at[:, pl.ds(pl.multiple_of(index * width, width), width)]


def pack_far_kernel(n, at_ref, k_ref, v_ref, kv_to, sems):
    side, _ = place(at_ref, n)
    moves = []
    for i in range(n // 2):
        head = (1 - side) * (n // 2) + i
        moves.append((lanes_of(k_ref, head, DH), kv_to.at[i, :, :DH]))
        moves.append((lanes_of(v_ref, head, DH), kv_to.at[i, :, DH:]))
    run_all(moves, sems)


def pack_kernel(n, at_ref, q_ref, k_ref, v_ref, g_ref, *refs):
    to, g_to, sems = refs[:n], refs[n], refs[n + 1]
    side, x = place(at_ref, n)
    wide = q_ref.shape[1] // (2 * n)
    moves = []
    chunk = g_ref.shape[-1]
    for z in range(g_ref.shape[1]):
        moves.append((g_ref.at[:, z], g_to.at[:, :, :, z * chunk : (z + 1) * chunk]))
    for hop in range(n):
        target = lax.rem(x + hop, n)
        head = side * (n // 2) + lax.div(target, 2)
        moves.append((lanes_of(q_ref, side * n + target, wide), to[hop].at[:, :wide]))
        moves.append((lanes_of(k_ref, head, DH), to[hop].at[:, wide : wide + DH]))
        moves.append((lanes_of(v_ref, head, DH), to[hop].at[:, wide + DH : wide + 2 * DH]))
        moves.append((lanes_of(q_ref, (1 - side) * n + target, wide), to[hop].at[:, wide + 2 * DH :]))
    run_all(moves, sems)


def kernel_call(body, outs, ins, name, scratch=(), limit=8 << 20, **more):
    vmem = pl.BlockSpec(memory_space=pltpu.VMEM)
    settings = dict(
        out_shape=outs,
        in_specs=[pl.BlockSpec(memory_space=pltpu.SMEM)] + [vmem] * (len(ins) - 1),
        out_specs=(vmem,) * len(outs),
        scratch_shapes=list(scratch),
        compiler_params=pltpu.CompilerParams(vmem_limit_bytes=limit),
        name=name,
    )
    settings.update(more)
    return pl.pallas_call(body, **settings)(*ins)


def packed_far(at, k, v, n):
    return kernel_call(
        lambda *refs: pack_far_kernel(n, *refs),
        (jax.ShapeDtypeStruct((n // 2, k.shape[0], 2 * DH), k.dtype),),
        (at, k, v),
        "pack_far",
        scratch=(pltpu.SemaphoreType.DMA((n,)),),
        in_specs=[pl.BlockSpec(memory_space=pltpu.SMEM)] + [pl.BlockSpec(memory_space=pl.ANY)] * 2,
    )[0]


def packed(at, q, k, v, g, n):
    rows, wide = q.shape[0], q.shape[1] // (2 * n)
    yc, z, x, _, chunk = g.shape
    outs = (
        *(jax.ShapeDtypeStruct((rows, 2 * wide + 2 * DH), q.dtype),) * n,
        jax.ShapeDtypeStruct((yc, x, 1, z * chunk), g.dtype),
    )
    found = kernel_call(
        lambda *refs: pack_kernel(n, *refs),
        outs,
        (at, q, k, v, g),
        "pack",
        scratch=(pltpu.SemaphoreType.DMA((4 * n + z,)),),
        in_specs=[pl.BlockSpec(memory_space=pltpu.SMEM)] + [pl.BlockSpec(memory_space=pl.ANY)] * 4,
    )
    return found[:n], found[-1]


def stack_kernel(n, *refs):
    for hop in range(n):
        refs[n][hop] = refs[hop][:, -refs[n].shape[-1] :]


def stacked(pieces, wide):
    n, rows = len(pieces), pieces[0].shape[0]
    vmem = pl.BlockSpec(memory_space=pltpu.VMEM)
    return kernel_call(
        lambda *refs: stack_kernel(n, *refs),
        (jax.ShapeDtypeStruct((n, rows, wide), pieces[0].dtype),),
        tuple(pieces),
        "stack",
        in_specs=[vmem] * n,
    )[0]


def cut_kernel(n, at_ref, kv_ref, *to):
    _, x = place(at_ref, n)
    for hop in range(n):
        to[hop][...] = kv_ref[lax.div(lax.rem(x + hop, n), 2)]


def cut(at, kv, n):
    outs = (jax.ShapeDtypeStruct(kv.shape[1:], kv.dtype),) * n
    return kernel_call(lambda *refs: cut_kernel(n, *refs), outs, (at, kv), "cut")


def gather_kernel(n, at_ref, *refs):
    near, far, (kv_ref, last_ref) = refs[:n], refs[n : 2 * n], refs[2 * n :]
    side, x = place(at_ref, n)
    rows, width = far[0].shape

    def put(half, chunk, value):
        kv_ref[pl.ds(pl.multiple_of((half * n + chunk) * rows, rows), rows)] = value

    for hop in range(n):
        chunk = lax.rem(x + n - hop, n)
        wide = (near[hop].shape[1] - width) // 2
        put(side, chunk, near[hop][:, wide : wide + width])
        put(1 - side, chunk, far[hop][...])
    last_ref[...] = kv_ref[kv_ref.shape[0] - last_ref.shape[0] :]


def gathered(at, near, far, reach):
    rows, width = far[0].shape
    n = len(near)
    outs = (
        jax.ShapeDtypeStruct((2 * n * rows, width), jnp.bfloat16),
        jax.ShapeDtypeStruct((reach, width), jnp.bfloat16),
    )
    return kernel_call(lambda *refs: gather_kernel(n, *refs), outs, (at, *near, *far), "gather")


def attend_kernel(n, is_near, count, at_ref, kv_ref, prior_ref, *refs):
    pieces, out_ref, q_s, older_s, out_s, sem = refs[:count], *refs[-5:]
    side, x = place(at_ref, n)
    half = side if is_near else 1 - side
    rows, wide = q_s.shape[0] // n, q_s.shape[1]
    reach = prior_ref.shape[0]
    for hop in range(n):
        chunk = lax.rem(x + n - hop, n)
        value = pieces[hop][:, :wide] if is_near else pieces[0][hop]
        q_s[pl.ds(pl.multiple_of(chunk * rows, rows), rows)] = value
    start = pl.multiple_of(half * n * rows, reach)

    @pl.when(half == 0)
    def _():
        older_s[...] = prior_ref[...]

    @pl.when(half != 0)
    def _():
        older_s[...] = kv_ref[n * rows - reach : n * rows]

    row = lax.broadcasted_iota(jnp.int32, (reach, reach), 0)
    col = lax.broadcasted_iota(jnp.int32, (reach, reach), 1)
    newer = col <= row
    across = (((1,), (1,)), ((), ()))
    for block in range(n * rows // reach):
        here = pl.ds(block * reach, reach)
        now = pl.ds(pl.multiple_of(start + block * reach, reach), reach)
        if block:
            older_ref, older = kv_ref, pl.ds(pl.multiple_of(start + (block - 1) * reach, reach), reach)
        else:
            older_ref, older = older_s, slice(None)
        for head in range(wide // DH):
            lanes = pl.ds(head * DH, DH)
            q = q_s[here, lanes]
            old = lax.dot_general(q, older_ref[older, :DH], across, preferred_element_type=jnp.float32)
            new = lax.dot_general(q, kv_ref[now, :DH], across, preferred_element_type=jnp.float32)
            scores = jnp.where(newer, new, old) * DH**-0.5
            expo = jnp.exp(scores - jnp.max(scores, axis=-1, keepdims=True))
            weights = (expo / jnp.sum(expo, axis=-1, keepdims=True)).astype(jnp.bfloat16)
            none = jnp.zeros_like(weights)
            out = jnp.dot(
                jnp.where(newer, weights, none), kv_ref[now, DH:], preferred_element_type=jnp.float32
            ) + jnp.dot(
                jnp.where(newer, none, weights), older_ref[older, DH:], preferred_element_type=jnp.float32
            )
            out_s[here, lanes] = out.astype(jnp.bfloat16)
    copy = pltpu.make_async_copy(out_s, out_ref.at[pl.ds(start, n * rows)], sem)
    copy.start()
    copy.wait()


def attended_half(at, kv, prior, pieces, n, wide, onto=None):
    reach, total = prior.shape[0], kv.shape[0]
    vmem, somewhere = pl.BlockSpec(memory_space=pltpu.VMEM), pl.BlockSpec(memory_space=pl.ANY)
    is_near = onto is None
    ins = (at, kv, prior, *pieces) + (() if is_near else (onto,))
    return kernel_call(
        lambda *refs: attend_kernel(n, is_near, len(pieces), *refs),
        (jax.ShapeDtypeStruct((total, wide), jnp.bfloat16),),
        ins,
        "attend",
        scratch=(
            pltpu.VMEM((total // 2, wide), jnp.bfloat16),
            pltpu.VMEM(prior.shape, jnp.bfloat16),
            pltpu.VMEM((total // 2, wide), jnp.bfloat16),
            pltpu.SemaphoreType.DMA,
        ),
        limit=16 << 20,
        in_specs=[pl.BlockSpec(memory_space=pltpu.SMEM)]
        + [vmem] * (2 + len(pieces))
        + ([] if is_near else [somewhere]),
        out_specs=(somewhere,),
        input_output_aliases={} if is_near else {3 + len(pieces): 0},
        cost_estimate=pl.CostEstimate(
            flops=4 * total * wide * reach, bytes_accessed=2 * total * wide * 2, transcendentals=total * reach
        ),
    )[0]


def step(queries, keys, values, grad_parts):
    dp, y, c, z, n = (lax.axis_size(a) for a in ("dp", *BLK_AA))
    at = lax.axis_index(AA).astype(jnp.int32).reshape(1)
    wide = queries.shape[2] // (z * n)
    reach = queries.shape[1] * 2
    chunks = grad_parts.reshape(y * c, z, n, 1, -1)
    kv_far = packed_far(at, keys[0], values[0], n)
    sent, parts = packed(at, queries[0], keys[0], values[0], chunks, n)

    def along_x(value, hop):
        return lax.ppermute(value, "aa_1", [(x, (x + hop) % n) for x in range(n)])

    def across_z(value):
        return lax.ppermute(value, "aa_0", [(s, 1 - s) for s in range(z)])

    kv_far = across_z(kv_far)
    parts = parts.reshape(y * c * n, 1, -1)
    parts = lax.all_to_all(parts, ("blk_0", "blk_1", "aa_1"), 0, 0, tiled=True)
    near = [sent[0]] + [along_x(sent[hop], hop) for hop in range(1, n)]
    q_far = stacked(near, wide)
    q_far = across_z(q_far)
    far = cut(at, kv_far, n)
    far = [far[0]] + [along_x(far[hop], hop) for hop in range(1, n)]
    kv, last = gathered(at, near, far, reach)
    prior = lax.ppermute(last, BLK, [(i, i + 1) for i in range(y * c - 1)])
    rows = attended_half(at, kv, prior, near, n, wide)

    share = jnp.sum(parts, axis=0).reshape(z, 1, -1)
    share = jnp.broadcast_to(share[None], (dp, *share.shape)).reshape(dp * z, 1, -1)
    share = lax.all_to_all(share, ("dp", "aa_0"), 0, 0, tiled=True)
    grad_mean = jnp.sum(share, axis=(0, 1)) / (dp * y * c * z * n)

    rows = attended_half(at, kv, prior, (q_far,), n, wide, rows)
    return rows[None], grad_mean


def solution(mesh):
    torus = Mesh(
        mesh.devices.reshape(mesh.shape["dp"], 8, 2, 2, 4), ("dp", "blk_0", "blk_1", "aa_0", "aa_1")
    )
    placed = P("dp", BLK_AA, None)
    return jax.shard_map(
        step,
        mesh=torus,
        in_specs=(placed,) * 4,
        out_specs=(P("dp", BLK, AA), P(BLK_AA)),
        check_vma=False,
    )
```

time: 124 us -> 97.2 us (0.78)
  the two profiles are of different devices: /device:TPU:15 before, /device:TPU:8 now
where the time goes in v3:
time: 97.2 us; the launch traced here: 96.6 us
  starting transfers between devices  77.5 us (80%)
  Pallas kernels  6.45 us (7%)
  waiting for transfers between devices  6.14 us (6%)
  local copies, waits for them, and re-layouts  4.65 us (5%)
    ppermute x6, starting transfers between devices, along_x(): return lax.ppermute(value, 'aa_1', [(x, (x + hop) % n) for x in range(n)])  22.5 us
    ppermute x2, starting transfers between devices, across_z(): return lax.ppermute(value, 'aa_0', [(s, 1 - s) for s in range(z)])  21 us
    all_to_all x1, starting transfers between devices, step(): parts = lax.all_to_all(parts, ('blk_0', 'blk_1', 'aa_1'), 0, 0, tiled=True)  17.3 us
    all_to_all x1, starting transfers between devices, step(): share = lax.all_to_all(share, ('dp', 'aa_0'), 0, 0, tiled=True)  14.7 us
    pallas_call x7, Pallas kernels, kernel_call(): return pl.pallas_call(body, **settings)(*ins)  6.45 us
    ppermute x1, waiting for transfers between devices, step(): prior = lax.ppermute(last, BLK, [(i, i + 1) for i in range(y * c - 1)])  4.36 us
    unnamed x12, local copies, waits for them, and re-layouts  3.9 us
  transfers between devices with their start and end apart: 11, of which 2 were waited for; matrix products, arithmetic and copies ran while one was open for 1% of the time, Pallas kernels for 5%

profile of v3, /device:TPU:8, one launch (start us, length us, event | category | flops | bytes accessed | tf_op | source)
XLA Modules:
  0.0 96.6 jit_solution(14211812673120913718)
XLA Ops:
  0.6 1.0 %copy-done = bf16[1,128,2048]{2,1,0:T(8,128)(2,1)S(1)} copy-done((bf16[1,128,2048]{2,1,0:T(8,128)(2,1)S(1)}, bf16[1,128,2048]{2,1,0:T(8,128)(2,1)}, u32[]{:S(2)}) %copy-start) | copy-done | bytes 524312
  1.7 1.0 %copy-done.1 = f32[1,1,131072]{2,1,0:T(1,128)S(1)} copy-done((f32[1,1,131072]{2,1,0:T(1,128)S(1)}, f32[1,1,131072]{2,1,0:T(1,128)}, u32[]{:S(2)}) %copy-start.1) | copy-done | bytes 524312
  2.7 0.9 copy-done.2
  3.6 0.9 copy-done.4
  4.5 1.2 %pack.1 = (bf16[128,768]{1,0:T(8,128)(2,1)S(1)}, bf16[128,768]{1,0:T(8,128)(2,1)S(1)}, bf16[128,768]{1,0:T(8,128)(2,1)S(1)}, bf16[128,768]{1,0:T(8,128)(2,1)S(1)}, f32[16,4,1,2048]{3,2,1,0:T(1,128)}) custom-call(s32[1]{0:T(128)} %bitcast.refs_0_, bf16[128,2048]{1,0:T(8,128)(2,1)S(1)} %bitcast.7, bf16[128,512]{1,0:T(8,128)(2,1)S(1)} %bitcast.9, ...), custom_call_target="tpu_custom_call" | custom-call | tf_op jit(solution)/shard_map/pack/pallas_call | solution.py:76
  5.7 0.0 copy-start.3
  5.7 0.0 copy-start.5
  5.7 17.3 %all-to-all-start = ((f32[64,1,2048]{2,1,0:T(1,128)}), f32[64,1,2048]{2,1,0:T(1,128)S(1)}, u32[]{:S(2)}, u32[]{:S(2)}) async-start(f32[64,1,2048]{2,1,0:T(1,128)} %bitcast.6), calls=%async_computation | async-start | bytes 1048576 | tf_op jit(solution)/shard_map/all_to_all | solution.py:258
  23.1 3.4 %collective-permute-start = (bf16[128,768]{1,0:T(8,128)(2,1)S(1)}, bf16[128,768]{1,0:T(8,128)(2,1)S(1)}, u32[]{:S(2)}, u32[]{:S(2)}) collective-permute-start(bf16[128,768]{1,0:T(8,128)(2,1)S(1)} %get-tuple-element.14), channel_id=1, source_target_pairs={{0,1},{1,2},{2,3},{3,0},{4,5},{5,6},{6,7},{7,4},{8,9},{9,10},{10,1... | collective-permute-start | bytes 589832 | tf_op jit(solution)/shard_map/ppermute | solution.py:251
  26.5 4.6 %collective-permute-start.1 = (bf16[128,768]{1,0:T(8,128)(2,1)S(1)}, bf16[128,768]{1,0:T(8,128)(2,1)S(1)}, u32[]{:S(2)}, u32[]{:S(2)}) collective-permute-start(bf16[128,768]{1,0:T(8,128)(2,1)S(1)} %get-tuple-element.15), channel_id=1, source_target_pairs={{0,2},{1,3},{2,0},{3,1},{4,6},{5,7},{6,4},{7,5},{8,10},{9,11},{10,... | collective-permute-start | bytes 589832 | tf_op jit(solution)/shard_map/ppermute | solution.py:251
  31.1 3.4 %collective-permute-start.2 = (bf16[128,768]{1,0:T(8,128)(2,1)S(1)}, bf16[128,768]{1,0:T(8,128)(2,1)S(1)}, u32[]{:S(2)}, u32[]{:S(2)}) collective-permute-start(bf16[128,768]{1,0:T(8,128)(2,1)S(1)} %get-tuple-element.16), channel_id=1, source_target_pairs={{0,3},{1,0},{2,1},{3,2},{4,7},{5,4},{6,5},{7,6},{8,11},{9,8},{10,9... | collective-permute-start | bytes 589832 | tf_op jit(solution)/shard_map/ppermute | solution.py:251
  34.4 0.1 pack_far.1
  34.5 12.7 %collective-permute-start.3 = (bf16[2,128,256]{2,1,0:T(8,128)(2,1)S(1)}, bf16[2,128,256]{2,1,0:T(8,128)(2,1)S(1)}, u32[]{:S(2)}, u32[]{:S(2)}) collective-permute-start(bf16[2,128,256]{2,1,0:T(8,128)(2,1)S(1)} %pack_far.1), channel_id=1, source_target_pairs={{0,4},{4,0},{1,5},{5,1},{2,6},{6,2},{3,7},{7,3},{8,12},{12,8},{9,1... | collective-permute-start | bytes 393224 | tf_op jit(solution)/shard_map/ppermute | solution.py:254
  47.3 0.0 collective-permute-done.refs_2_.refs_1_.refs_4_
  47.3 0.0 collective-permute-done.2.refs_4_.refs_3_.refs_6_
  47.3 8.3 %collective-permute-start.8 = (bf16[4,128,256]{2,1,0:T(8,128)(2,1)S(1)}, bf16[4,128,256]{2,1,0:T(8,128)(2,1)S(1)}, u32[]{:S(2)}, u32[]{:S(2)}) collective-permute-start(bf16[4,128,256]{2,1,0:T(8,128)(2,1)S(1)} %stack.1), channel_id=1, source_target_pairs={{0,4},{4,0},{1,5},{5,1},{2,6},{6,2},{3,7},{7,3},{8,12},{12,8},{9,1... | collective-permute-start | bytes 786440 | tf_op jit(solution)/shard_map/ppermute | solution.py:254
  55.7 4.1 %collective-permute-start.4 = (bf16[128,256]{1,0:T(8,128)(2,1)S(1)}, bf16[128,256]{1,0:T(8,128)(2,1)S(1)}, u32[]{:S(2)}, u32[]{:S(2)}) collective-permute-start(bf16[128,256]{1,0:T(8,128)(2,1)S(1)} %get-tuple-element.18), channel_id=1, source_target_pairs={{0,1},{1,2},{2,3},{3,0},{4,5},{5,6},{6,7},{7,4},{8,9},{9,10},{10,1... | collective-permute-start | bytes 196616 | tf_op jit(solution)/shard_map/ppermute | solution.py:251
  59.8 3.8 %collective-permute-start.5 = (bf16[128,256]{1,0:T(8,128)(2,1)S(1)}, bf16[128,256]{1,0:T(8,128)(2,1)S(1)}, u32[]{:S(2)}, u32[]{:S(2)}) collective-permute-start(bf16[128,256]{1,0:T(8,128)(2,1)S(1)} %get-tuple-element.19), channel_id=1, source_target_pairs={{0,2},{1,3},{2,0},{3,1},{4,6},{5,7},{6,4},{7,5},{8,10},{9,11},{10,... | collective-permute-start | bytes 196616 | tf_op jit(solution)/shard_map/ppermute | solution.py:251
  63.6 3.3 %collective-permute-start.6 = (bf16[128,256]{1,0:T(8,128)(2,1)S(1)}, bf16[128,256]{1,0:T(8,128)(2,1)S(1)}, u32[]{:S(2)}, u32[]{:S(2)}) collective-permute-start(bf16[128,256]{1,0:T(8,128)(2,1)S(1)} %get-tuple-element.20), channel_id=1, source_target_pairs={{0,3},{1,0},{2,1},{3,2},{4,7},{5,4},{6,5},{7,6},{8,11},{9,8},{10,9... | collective-permute-start | bytes 196616 | tf_op jit(solution)/shard_map/ppermute | solution.py:251
  66.9 0.0 all-to-all-done
  66.9 0.3 reduce_sum.18
  67.3 0.7 broadcast_in_dim.15
  68.0 14.7 %all-to-all-start.1 = ((f32[16,1,1024]{2,1,0:T(1,128)}), f32[16,1,1024]{2,1,0:T(1,128)S(1)}, u32[]{:S(2)}, u32[]{:S(2)}) async-start(f32[16,1,1024]{2,1,0:T(1,128)} %broadcast_in_dim.15), calls=%async_computation.1 | async-start | bytes 131072 | tf_op jit(solution)/shard_map/all_to_all | solution.py:270
  82.7 0.0 collective-permute-done.4.refs_6_
  82.7 0.1 gather.1
  82.8 1.9 %collective-permute-start.7 = (bf16[256,256]{1,0:T(8,128)(2,1)S(1)}, bf16[256,256]{1,0:T(8,128)(2,1)S(1)}, u32[]{:S(2)}, u32[]{:S(2)}) collective-permute-start(bf16[256,256]{1,0:T(8,128)(2,1)S(1)} %get-tuple-element.22), channel_id=1, source_target_pairs={{0,8},{8,16},{16,24},{24,32},{32,40},{40,48},{48,56},{56,64},{64,7... | collective-permute-start | bytes 393224 | tf_op jit(solution)/shard_map/ppermute | solution.py:265
  84.7 4.4 %collective-permute-done.7.refs_2_ = bf16[256,256]{1,0:T(8,128)(2,1)S(1)} collective-permute-done((bf16[256,256]{1,0:T(8,128)(2,1)S(1)}, bf16[256,256]{1,0:T(8,128)(2,1)S(1)}, u32[]{:S(2)}, u32[]{:S(2)}) %collective-permute-start.7) | collective-permute-done | bytes 131104 | tf_op jit(solution)/shard_map/ppermute | solution.py:265
  89.1 2.5 %attend.2.refs_4_ = bf16[1024,256]{1,0:T(8,128)(2,1)} custom-call(s32[1]{0:T(128)} %bitcast.refs_0_, bf16[1024,256]{1,0:T(8,128)(2,1)S(1)} %get-tuple-element.21.refs_1_, bf16[256,256]{1,0:T(8,128)(2,1)S(1)} %collective-permute-done.7.refs_2_, bf16[128,768]{1,0:T(8,128)(2,1)S(1)} %get-tuple-element.13.refs_1_.refs_0_.refs_3_, ...), custom_call_target="tpu_custom_call" | custom-call | flops 268435456 | bytes 1048576 | tf_op jit(solution)/shard_map/attend/pallas_call | solution.py:76
  91.6 2.5 %attend.3 = bf16[1024,256]{1,0:T(8,128)(2,1)} custom-call(s32[1]{0:T(128)} %bitcast.refs_0_, bf16[1024,256]{1,0:T(8,128)(2,1)S(1)} %get-tuple-element.21.refs_1_, bf16[256,256]{1,0:T(8,128)(2,1)S(1)} %collective-permute-done.7.refs_2_, bf16[4,128,256]{2,1,0:T(8,128)(2,1)S(1)} %collective-permute-done.8.refs_3_, ...), custom_call_target="tpu_custom_call", output_to_operand_aliasing={{}: (4, {})} | custom-call | flops 268435456 | bytes 1048576 | tf_op jit(solution)/shard_map/attend/pallas_call | solution.py:76
  94.2 1.8 %all-to-all-done.1 = f32[16,1,1024]{2,1,0:T(1,128)S(1)} async-done(((f32[16,1,1024]{2,1,0:T(1,128)}), f32[16,1,1024]{2,1,0:T(1,128)S(1)}, u32[]{:S(2)}, u32[]{:S(2)}) %all-to-all-start.1) | async-done | bytes 65568 | tf_op jit(solution)/shard_map/all_to_all | solution.py:270
  96.0 0.1 reduce_sum.19
  96.0 0.6 broadcast_multiply_fusion
  (15 shorter events, 0.1 us)
Async XLA Ops:
  0.6 1.0 %copy-start = (bf16[1,128,2048]{2,1,0:T(8,128)(2,1)S(1)}, bf16[1,128,2048]{2,1,0:T(8,128)(2,1)}, u32[]{:S(2)}) copy-start(bf16[1,128,2048]{2,1,0:T(8,128)(2,1)} %param.4) | copy-start | bytes 1572868
  1.7 1.0 %copy-start.1 = (f32[1,1,131072]{2,1,0:T(1,128)S(1)}, f32[1,1,131072]{2,1,0:T(1,128)}, u32[]{:S(2)}) copy-start(f32[1,1,131072]{2,1,0:T(1,128)} %param.7) | copy-start | bytes 1572868
  2.7 0.9 copy-start.2
  3.6 0.9 copy-start.4
  5.7 28.7 %copy-start.3 = (bf16[1,128,512]{2,1,0:T(8,128)(2,1)S(1)}, bf16[1,128,512]{2,1,0:T(8,128)(2,1)}, u32[]{:S(2)}) copy-start(bf16[1,128,512]{2,1,0:T(8,128)(2,1)} %param.5) | copy-start | bytes 393220
  5.7 28.7 %copy-start.5 = (bf16[1,128,512]{2,1,0:T(8,128)(2,1)S(1)}, bf16[1,128,512]{2,1,0:T(8,128)(2,1)}, u32[]{:S(2)}) copy-start(bf16[1,128,512]{2,1,0:T(8,128)(2,1)} %param.6) | copy-start | bytes 393220
  5.7 61.2 %all-to-all-start = ((f32[64,1,2048]{2,1,0:T(1,128)}), f32[64,1,2048]{2,1,0:T(1,128)S(1)}, u32[]{:S(2)}, u32[]{:S(2)}) async-start(f32[64,1,2048]{2,1,0:T(1,128)} %bitcast.6), calls=%async_computation | async-start | bytes 1048576 | tf_op jit(solution)/shard_map/all_to_all | solution.py:258
  23.1 24.2 %collective-permute-start = (bf16[128,768]{1,0:T(8,128)(2,1)S(1)}, bf16[128,768]{1,0:T(8,128)(2,1)S(1)}, u32[]{:S(2)}, u32[]{:S(2)}) collective-permute-start(bf16[128,768]{1,0:T(8,128)(2,1)S(1)} %get-tuple-element.14), channel_id=1, source_target_pairs={{0,1},{1,2},{2,3},{3,0},{4,5},{5,6},{6,7},{7,4},{8,9},{9,10},{10,1... | collective-permute-start | bytes 589832 | tf_op jit(solution)/shard_map/ppermute | solution.py:251
  26.5 20.8 %collective-permute-start.1 = (bf16[128,768]{1,0:T(8,128)(2,1)S(1)}, bf16[128,768]{1,0:T(8,128)(2,1)S(1)}, u32[]{:S(2)}, u32[]{:S(2)}) collective-permute-start(bf16[128,768]{1,0:T(8,128)(2,1)S(1)} %get-tuple-element.15), channel_id=1, source_target_pairs={{0,2},{1,3},{2,0},{3,1},{4,6},{5,7},{6,4},{7,5},{8,10},{9,11},{10,... | collective-permute-start | bytes 589832 | tf_op jit(solution)/shard_map/ppermute | solution.py:251
  31.1 16.2 %collective-permute-start.2 = (bf16[128,768]{1,0:T(8,128)(2,1)S(1)}, bf16[128,768]{1,0:T(8,128)(2,1)S(1)}, u32[]{:S(2)}, u32[]{:S(2)}) collective-permute-start(bf16[128,768]{1,0:T(8,128)(2,1)S(1)} %get-tuple-element.16), channel_id=1, source_target_pairs={{0,3},{1,0},{2,1},{3,2},{4,7},{5,4},{6,5},{7,6},{8,11},{9,8},{10,9... | collective-permute-start | bytes 589832 | tf_op jit(solution)/shard_map/ppermute | solution.py:251
  34.5 21.1 %collective-permute-start.3 = (bf16[2,128,256]{2,1,0:T(8,128)(2,1)S(1)}, bf16[2,128,256]{2,1,0:T(8,128)(2,1)S(1)}, u32[]{:S(2)}, u32[]{:S(2)}) collective-permute-start(bf16[2,128,256]{2,1,0:T(8,128)(2,1)S(1)} %pack_far.1), channel_id=1, source_target_pairs={{0,4},{4,0},{1,5},{5,1},{2,6},{6,2},{3,7},{7,3},{8,12},{12,8},{9,1... | collective-permute-start | bytes 393224 | tf_op jit(solution)/shard_map/ppermute | solution.py:254
  47.3 44.3 %collective-permute-start.8 = (bf16[4,128,256]{2,1,0:T(8,128)(2,1)S(1)}, bf16[4,128,256]{2,1,0:T(8,128)(2,1)S(1)}, u32[]{:S(2)}, u32[]{:S(2)}) collective-permute-start(bf16[4,128,256]{2,1,0:T(8,128)(2,1)S(1)} %stack.1), channel_id=1, source_target_pairs={{0,4},{4,0},{1,5},{5,1},{2,6},{6,2},{3,7},{7,3},{8,12},{12,8},{9,1... | collective-permute-start | bytes 786440 | tf_op jit(solution)/shard_map/ppermute | solution.py:254
  55.7 27.0 %collective-permute-start.4 = (bf16[128,256]{1,0:T(8,128)(2,1)S(1)}, bf16[128,256]{1,0:T(8,128)(2,1)S(1)}, u32[]{:S(2)}, u32[]{:S(2)}) collective-permute-start(bf16[128,256]{1,0:T(8,128)(2,1)S(1)} %get-tuple-element.18), channel_id=1, source_target_pairs={{0,1},{1,2},{2,3},{3,0},{4,5},{5,6},{6,7},{7,4},{8,9},{9,10},{10,1... | collective-permute-start | bytes 196616 | tf_op jit(solution)/shard_map/ppermute | solution.py:251
  59.8 22.9 %collective-permute-start.5 = (bf16[128,256]{1,0:T(8,128)(2,1)S(1)}, bf16[128,256]{1,0:T(8,128)(2,1)S(1)}, u32[]{:S(2)}, u32[]{:S(2)}) collective-permute-start(bf16[128,256]{1,0:T(8,128)(2,1)S(1)} %get-tuple-element.19), channel_id=1, source_target_pairs={{0,2},{1,3},{2,0},{3,1},{4,6},{5,7},{6,4},{7,5},{8,10},{9,11},{10,... | collective-permute-start | bytes 196616 | tf_op jit(solution)/shard_map/ppermute | solution.py:251
  63.6 19.1 %collective-permute-start.6 = (bf16[128,256]{1,0:T(8,128)(2,1)S(1)}, bf16[128,256]{1,0:T(8,128)(2,1)S(1)}, u32[]{:S(2)}, u32[]{:S(2)}) collective-permute-start(bf16[128,256]{1,0:T(8,128)(2,1)S(1)} %get-tuple-element.20), channel_id=1, source_target_pairs={{0,3},{1,0},{2,1},{3,2},{4,7},{5,4},{6,5},{7,6},{8,11},{9,8},{10,9... | collective-permute-start | bytes 196616 | tf_op jit(solution)/shard_map/ppermute | solution.py:251
  68.0 27.9 %all-to-all-start.1 = ((f32[16,1,1024]{2,1,0:T(1,128)}), f32[16,1,1024]{2,1,0:T(1,128)S(1)}, u32[]{:S(2)}, u32[]{:S(2)}) async-start(f32[16,1,1024]{2,1,0:T(1,128)} %broadcast_in_dim.15), calls=%async_computation.1 | async-start | bytes 131072 | tf_op jit(solution)/shard_map/all_to_all | solution.py:270
  82.8 6.3 %collective-permute-start.7 = (bf16[256,256]{1,0:T(8,128)(2,1)S(1)}, bf16[256,256]{1,0:T(8,128)(2,1)S(1)}, u32[]{:S(2)}, u32[]{:S(2)}) collective-permute-start(bf16[256,256]{1,0:T(8,128)(2,1)S(1)} %get-tuple-element.22), channel_id=1, source_target_pairs={{0,8},{8,16},{16,24},{24,32},{32,40},{40,48},{48,56},{56,64},{64,7... | collective-permute-start | bytes 393224 | tf_op jit(solution)/shard_map/ppermute | solution.py:265

commit v4 on v3

--- a/solution.py
+++ b/solution.py
@@ -34,9 +34,9 @@
     return ref.at[:, pl.ds(pl.multiple_of(index * width, width), width)]
 
 
-def pack_far_kernel(n, at_ref, k_ref, v_ref, kv_to, sems):
-    side, _ = place(at_ref, n)
-    moves = []
+def pack_far_kernel(n, at_ref, q_ref, k_ref, v_ref, kv_to, sems):
+    side, x = place(at_ref, n)
+    moves = [(lanes_of(q_ref, (1 - side) * n + x, 2 * DH), kv_to.at[n // 2])]
     for i in range(n // 2):
         head = (1 - side) * (n // 2) + i
         moves.append((lanes_of(k_ref, head, DH), kv_to.at[i, :, :DH]))
@@ -58,7 +58,8 @@
         moves.append((lanes_of(q_ref, side * n + target, wide), to[hop].at[:, :wide]))
         moves.append((lanes_of(k_ref, head, DH), to[hop].at[:, wide : wide + DH]))
         moves.append((lanes_of(v_ref, head, DH), to[hop].at[:, wide + DH : wide + 2 * DH]))
-        moves.append((lanes_of(q_ref, (1 - side) * n + target, wide), to[hop].at[:, wide + 2 * DH :]))
+        if hop:
+            moves.append((lanes_of(q_ref, (1 - side) * n + target, wide), to[hop].at[:, wide + 2 * DH :]))
     run_all(moves, sems)
 
 
@@ -76,14 +77,14 @@
     return pl.pallas_call(body, **settings)(*ins)
 
 
-def packed_far(at, k, v, n):
+def packed_far(at, q, k, v, n):
     return kernel_call(
         lambda *refs: pack_far_kernel(n, *refs),
-        (jax.ShapeDtypeStruct((n // 2, k.shape[0], 2 * DH), k.dtype),),
-        (at, k, v),
+        (jax.ShapeDtypeStruct((n // 2 + 1, k.shape[0], 2 * DH), k.dtype),),
+        (at, q, k, v),
         "pack_far",
-        scratch=(pltpu.SemaphoreType.DMA((n,)),),
-        in_specs=[pl.BlockSpec(memory_space=pltpu.SMEM)] + [pl.BlockSpec(memory_space=pl.ANY)] * 2,
+        scratch=(pltpu.SemaphoreType.DMA((n + 1,)),),
+        in_specs=[pl.BlockSpec(memory_space=pltpu.SMEM)] + [pl.BlockSpec(memory_space=pl.ANY)] * 3,
     )[0]
 
 
@@ -91,7 +92,8 @@
     rows, wide = q.shape[0], q.shape[1] // (2 * n)
     yc, z, x, _, chunk = g.shape
     outs = (
-        *(jax.ShapeDtypeStruct((rows, 2 * wide + 2 * DH), q.dtype),) * n,
+        jax.ShapeDtypeStruct((rows, wide + 2 * DH), q.dtype),
+        *(jax.ShapeDtypeStruct((rows, 2 * wide + 2 * DH), q.dtype),) * (n - 1),
         jax.ShapeDtypeStruct((yc, x, 1, z * chunk), g.dtype),
     )
     found = kernel_call(
@@ -99,7 +101,7 @@
         outs,
         (at, q, k, v, g),
         "pack",
-        scratch=(pltpu.SemaphoreType.DMA((4 * n + z,)),),
+        scratch=(pltpu.SemaphoreType.DMA((4 * n - 1 + z,)),),
         in_specs=[pl.BlockSpec(memory_space=pltpu.SMEM)] + [pl.BlockSpec(memory_space=pl.ANY)] * 4,
     )
     return found[:n], found[-1]
@@ -143,7 +145,7 @@
 
     for hop in range(n):
         chunk = lax.rem(x + n - hop, n)
-        wide = (near[hop].shape[1] - width) // 2
+        wide = near[0].shape[1] - width
         put(side, chunk, near[hop][:, wide : wide + width])
         put(1 - side, chunk, far[hop][...])
     last_ref[...] = kv_ref[kv_ref.shape[0] - last_ref.shape[0] :]
@@ -167,7 +169,7 @@
     reach = prior_ref.shape[0]
     for hop in range(n):
         chunk = lax.rem(x + n - hop, n)
-        value = pieces[hop][:, :wide] if is_near else pieces[0][hop]
+        value = pieces[hop][:, :wide] if is_near else pieces[0][hop - 1] if hop else pieces[1][n // 2]
         q_s[pl.ds(pl.multiple_of(chunk * rows, rows), rows)] = value
     start = pl.multiple_of(half * n * rows, reach)
 
@@ -244,7 +246,7 @@
     wide = queries.shape[2] // (z * n)
     reach = queries.shape[1] * 2
     chunks = grad_parts.reshape(y * c, z, n, 1, -1)
-    kv_far = packed_far(at, keys[0], values[0], n)
+    kv_far = packed_far(at, queries[0], keys[0], values[0], n)
     sent, parts = packed(at, queries[0], keys[0], values[0], chunks, n)
 
     def along_x(value, hop):
@@ -254,10 +256,10 @@
         return lax.ppermute(value, "aa_0", [(s, 1 - s) for s in range(z)])
 
     kv_far = across_z(kv_far)
+    near = [sent[0]] + [along_x(sent[hop], hop) for hop in range(1, n)]
     parts = parts.reshape(y * c * n, 1, -1)
     parts = lax.all_to_all(parts, ("blk_0", "blk_1", "aa_1"), 0, 0, tiled=True)
-    near = [sent[0]] + [along_x(sent[hop], hop) for hop in range(1, n)]
-    q_far = stacked(near, wide)
+    q_far = stacked(near[1:], wide)
     q_far = across_z(q_far)
     far = cut(at, kv_far, n)
     far = [far[0]] + [along_x(far[hop], hop) for hop in range(1, n)]
@@ -270,7 +272,7 @@
     share = lax.all_to_all(share, ("dp", "aa_0"), 0, 0, tiled=True)
     grad_mean = jnp.sum(share, axis=(0, 1)) / (dp * y * c * z * n)
 
-    rows = attended_half(at, kv, prior, (q_far,), n, wide, rows)
+    rows = attended_half(at, kv, prior, (q_far, kv_far), n, wide, rows)
     return rows[None], grad_mean
 
 

time: 97.2 us -> 109 us (1.12)
  the two profiles are of different devices: /device:TPU:8 before, /device:TPU:128 now
where the time goes in v4:
time: 109 us; the launch traced here: 108 us
  starting transfers between devices  81.4 us (75%)
  waiting for transfers between devices  14.1 us (13%)
  Pallas kernels  6.44 us (6%)
  local copies, waits for them, and re-layouts  4.67 us (4%)
    ppermute x2, starting transfers between devices, across_z(): return lax.ppermute(value, 'aa_0', [(s, 1 - s) for s in range(z)])  27.8 us
    ppermute x6, starting transfers between devices, along_x(): return lax.ppermute(value, 'aa_1', [(x, (x + hop) % n) for x in range(n)])  21 us
    all_to_all x1, starting transfers between devices, step(): share = lax.all_to_all(share, ('dp', 'aa_0'), 0, 0, tiled=True)  20.5 us
    ppermute x2, waiting for transfers between devices, across_z(): return lax.ppermute(value, 'aa_0', [(s, 1 - s) for s in range(z)])  13.1 us
    all_to_all x1, starting transfers between devices, step(): parts = lax.all_to_all(parts, ('blk_0', 'blk_1', 'aa_1'), 0, 0, tiled=True)  10.7 us
    pallas_call x7, Pallas kernels, kernel_call(): return pl.pallas_call(body, **settings)(*ins)  6.44 us
    unnamed x14, local copies, waits for them, and re-layouts  3.9 us
  transfers between devices with their start and end apart: 11, of which 2 were waited for; matrix products, arithmetic and copies ran while one was open for 1% of the time, Pallas kernels for 5%

profile of v4, /device:TPU:128, one launch (start us, length us, event | category | flops | bytes accessed | tf_op | source)
XLA Modules:
  0.0 108.5 jit_solution(724411247315038319)
XLA Ops:
  0.6 0.0 copy-start
  0.6 1.0 copy-done
  1.7 1.0 copy-done.2
  2.7 0.9 copy-done.3
  3.6 0.9 copy-done.5
  4.5 1.1 %pack.1 = (bf16[128,512]{1,0:T(8,128)(2,1)S(1)}, bf16[128,768]{1,0:T(8,128)(2,1)S(1)}, bf16[128,768]{1,0:T(8,128)(2,1)S(1)}, bf16[128,768]{1,0:T(8,128)(2,1)S(1)}, f32[16,4,1,2048]{3,2,1,0:T(1,128)}) custom-call(s32[1]{0:T(128)} %bitcast.refs_0_, bf16[128,2048]{1,0:T(8,128)(2,1)S(1)} %bitcast.7, bf16[128,512]{1,0:T(8,128)(2,1)S(1)} %bitcast.10, ...), custom_call_target="tpu_custom_call" | custom-call | tf_op jit(solution)/shard_map/pack/pallas_call | solution.py:77
  5.7 0.0 copy-start.1
  5.7 0.0 copy-start.4
  5.7 0.0 copy-start.6
  5.7 10.7 %all-to-all-start = ((f32[64,1,2048]{2,1,0:T(1,128)}), f32[64,1,2048]{2,1,0:T(1,128)S(1)}, u32[]{:S(2)}, u32[]{:S(2)}) async-start(f32[64,1,2048]{2,1,0:T(1,128)} %bitcast.6), calls=%async_computation | async-start | bytes 1048576 | tf_op jit(solution)/shard_map/all_to_all | solution.py:261
  16.5 0.1 pack_far.1
  16.6 17.6 %collective-permute-start.3 = (bf16[3,128,256]{2,1,0:T(8,128)(2,1)S(1)}, bf16[3,128,256]{2,1,0:T(8,128)(2,1)S(1)}, u32[]{:S(2)}, u32[]{:S(2)}) collective-permute-start(bf16[3,128,256]{2,1,0:T(8,128)(2,1)S(1)} %pack_far.1), channel_id=1, source_target_pairs={{0,4},{4,0},{1,5},{5,1},{2,6},{6,2},{3,7},{7,3},{8,12},{12,8},{9,1... | collective-permute-start | bytes 589832 | tf_op jit(solution)/shard_map/ppermute | solution.py:256
  34.2 3.5 %collective-permute-start = (bf16[128,768]{1,0:T(8,128)(2,1)S(1)}, bf16[128,768]{1,0:T(8,128)(2,1)S(1)}, u32[]{:S(2)}, u32[]{:S(2)}) collective-permute-start(bf16[128,768]{1,0:T(8,128)(2,1)S(1)} %get-tuple-element.14), channel_id=1, source_target_pairs={{0,1},{1,2},{2,3},{3,0},{4,5},{5,6},{6,7},{7,4},{8,9},{9,10},{10,1... | collective-permute-start | bytes 589832 | tf_op jit(solution)/shard_map/ppermute | solution.py:253
  37.6 4.6 %collective-permute-start.1 = (bf16[128,768]{1,0:T(8,128)(2,1)S(1)}, bf16[128,768]{1,0:T(8,128)(2,1)S(1)}, u32[]{:S(2)}, u32[]{:S(2)}) collective-permute-start(bf16[128,768]{1,0:T(8,128)(2,1)S(1)} %get-tuple-element.15), channel_id=1, source_target_pairs={{0,2},{1,3},{2,0},{3,1},{4,6},{5,7},{6,4},{7,5},{8,10},{9,11},{10,... | collective-permute-start | bytes 589832 | tf_op jit(solution)/shard_map/ppermute | solution.py:253
  42.2 3.4 %collective-permute-start.2 = (bf16[128,768]{1,0:T(8,128)(2,1)S(1)}, bf16[128,768]{1,0:T(8,128)(2,1)S(1)}, u32[]{:S(2)}, u32[]{:S(2)}) collective-permute-start(bf16[128,768]{1,0:T(8,128)(2,1)S(1)} %get-tuple-element.16), channel_id=1, source_target_pairs={{0,3},{1,0},{2,1},{3,2},{4,7},{5,4},{6,5},{7,6},{8,11},{9,8},{10,9... | collective-permute-start | bytes 589832 | tf_op jit(solution)/shard_map/ppermute | solution.py:253
  45.6 0.0 collective-permute-done.3.refs_1_.refs_4_
  45.7 2.5 %collective-permute-start.4 = (bf16[128,256]{1,0:T(8,128)(2,1)S(1)}, bf16[128,256]{1,0:T(8,128)(2,1)S(1)}, u32[]{:S(2)}, u32[]{:S(2)}) collective-permute-start(bf16[128,256]{1,0:T(8,128)(2,1)S(1)} %get-tuple-element.18), channel_id=1, source_target_pairs={{0,1},{1,2},{2,3},{3,0},{4,5},{5,6},{6,7},{7,4},{8,9},{9,10},{10,1... | collective-permute-start | bytes 196616 | tf_op jit(solution)/shard_map/ppermute | solution.py:253
  48.1 3.7 %collective-permute-start.5 = (bf16[128,256]{1,0:T(8,128)(2,1)S(1)}, bf16[128,256]{1,0:T(8,128)(2,1)S(1)}, u32[]{:S(2)}, u32[]{:S(2)}) collective-permute-start(bf16[128,256]{1,0:T(8,128)(2,1)S(1)} %get-tuple-element.19), channel_id=1, source_target_pairs={{0,2},{1,3},{2,0},{3,1},{4,6},{5,7},{6,4},{7,5},{8,10},{9,11},{10,... | collective-permute-start | bytes 196616 | tf_op jit(solution)/shard_map/ppermute | solution.py:253
  51.9 3.4 %collective-permute-start.6 = (bf16[128,256]{1,0:T(8,128)(2,1)S(1)}, bf16[128,256]{1,0:T(8,128)(2,1)S(1)}, u32[]{:S(2)}, u32[]{:S(2)}) collective-permute-start(bf16[128,256]{1,0:T(8,128)(2,1)S(1)} %get-tuple-element.20), channel_id=1, source_target_pairs={{0,3},{1,0},{2,1},{3,2},{4,7},{5,4},{6,5},{7,6},{8,11},{9,8},{10,9... | collective-permute-start | bytes 196616 | tf_op jit(solution)/shard_map/ppermute | solution.py:253
  55.3 0.3 reduce_sum.18
  55.6 0.7 broadcast_in_dim.15
  56.4 20.5 %all-to-all-start.1 = ((f32[16,1,1024]{2,1,0:T(1,128)}), f32[16,1,1024]{2,1,0:T(1,128)S(1)}, u32[]{:S(2)}, u32[]{:S(2)}) async-start(f32[16,1,1024]{2,1,0:T(1,128)} %broadcast_in_dim.15), calls=%async_computation.1 | async-start | bytes 131072 | tf_op jit(solution)/shard_map/all_to_all | solution.py:272
  76.9 0.0 collective-permute-done.1.refs_3_.refs_1_.refs_5_
  76.9 10.3 %collective-permute-start.8 = (bf16[3,128,256]{2,1,0:T(8,128)(2,1)S(1)}, bf16[3,128,256]{2,1,0:T(8,128)(2,1)S(1)}, u32[]{:S(2)}, u32[]{:S(2)}) collective-permute-start(bf16[3,128,256]{2,1,0:T(8,128)(2,1)S(1)} %stack.1), channel_id=1, source_target_pairs={{0,4},{4,0},{1,5},{5,1},{2,6},{6,2},{3,7},{7,3},{8,12},{12,8},{9,1... | collective-permute-start | bytes 589832 | tf_op jit(solution)/shard_map/ppermute | solution.py:256
  87.3 0.1 gather.1
  87.3 1.3 %collective-permute-start.7 = (bf16[256,256]{1,0:T(8,128)(2,1)S(1)}, bf16[256,256]{1,0:T(8,128)(2,1)S(1)}, u32[]{:S(2)}, u32[]{:S(2)}) collective-permute-start(bf16[256,256]{1,0:T(8,128)(2,1)S(1)} %get-tuple-element.22), channel_id=1, source_target_pairs={{0,8},{8,16},{16,24},{24,32},{32,40},{40,48},{48,56},{56,64},{64,7... | collective-permute-start | bytes 393224 | tf_op jit(solution)/shard_map/ppermute | solution.py:267
  88.6 1.0 collective-permute-done.7.refs_2_
  89.6 2.5 %attend.2.refs_5_ = bf16[1024,256]{1,0:T(8,128)(2,1)} custom-call(s32[1]{0:T(128)} %bitcast.refs_0_, bf16[1024,256]{1,0:T(8,128)(2,1)S(1)} %get-tuple-element.21.refs_1_, bf16[256,256]{1,0:T(8,128)(2,1)S(1)} %collective-permute-done.7.refs_2_, bf16[128,512]{1,0:T(8,128)(2,1)S(1)} %get-tuple-element.13.refs_1_.refs_3_, ...), custom_call_target="tpu_custom_call" | custom-call | flops 268435456 | bytes 1048576 | tf_op jit(solution)/shard_map/attend/pallas_call | solution.py:77
  92.1 13.1 %collective-permute-done.8.refs_3_ = bf16[3,128,256]{2,1,0:T(8,128)(2,1)S(1)} collective-permute-done((bf16[3,128,256]{2,1,0:T(8,128)(2,1)S(1)}, bf16[3,128,256]{2,1,0:T(8,128)(2,1)S(1)}, u32[]{:S(2)}, u32[]{:S(2)}) %collective-permute-start.8) | collective-permute-done | bytes 196640 | tf_op jit(solution)/shard_map/ppermute | solution.py:256
  105.3 2.5 %attend.3 = bf16[1024,256]{1,0:T(8,128)(2,1)} custom-call(s32[1]{0:T(128)} %bitcast.refs_0_, bf16[1024,256]{1,0:T(8,128)(2,1)S(1)} %get-tuple-element.21.refs_1_, bf16[256,256]{1,0:T(8,128)(2,1)S(1)} %collective-permute-done.7.refs_2_, bf16[3,128,256]{2,1,0:T(8,128)(2,1)S(1)} %collective-permute-done.8.refs_3_, ...), custom_call_target="tpu_custom_call", output_to_operand_aliasing={{}: (5, {})} | custom-call | flops 268435456 | bytes 1048576 | tf_op jit(solution)/shard_map/attend/pallas_call | solution.py:77
  107.8 0.1 reduce_sum.19
  107.9 0.6 broadcast_multiply_fusion
  (17 shorter events, 0.1 us)
Async XLA Ops:
  0.6 1.0 copy-start
  1.7 1.0 copy-start.2
  2.7 0.9 copy-start.3
  3.6 0.9 copy-start.5
  5.7 10.8 %copy-start.1 = (bf16[1,128,2048]{2,1,0:T(8,128)(2,1)S(1)}, bf16[1,128,2048]{2,1,0:T(8,128)(2,1)}, u32[]{:S(2)}) copy-start(bf16[1,128,2048]{2,1,0:T(8,128)(2,1)} %param.4) | copy-start | bytes 1572868
  5.7 10.8 %copy-start.4 = (bf16[1,128,512]{2,1,0:T(8,128)(2,1)S(1)}, bf16[1,128,512]{2,1,0:T(8,128)(2,1)}, u32[]{:S(2)}) copy-start(bf16[1,128,512]{2,1,0:T(8,128)(2,1)} %param.5) | copy-start | bytes 393220
  5.7 10.8 %copy-start.6 = (bf16[1,128,512]{2,1,0:T(8,128)(2,1)S(1)}, bf16[1,128,512]{2,1,0:T(8,128)(2,1)}, u32[]{:S(2)}) copy-start(bf16[1,128,512]{2,1,0:T(8,128)(2,1)} %param.6) | copy-start | bytes 393220
  5.7 49.6 %all-to-all-start = ((f32[64,1,2048]{2,1,0:T(1,128)}), f32[64,1,2048]{2,1,0:T(1,128)S(1)}, u32[]{:S(2)}, u32[]{:S(2)}) async-start(f32[64,1,2048]{2,1,0:T(1,128)} %bitcast.6), calls=%async_computation | async-start | bytes 1048576 | tf_op jit(solution)/shard_map/all_to_all | solution.py:261
  16.6 29.0 %collective-permute-start.3 = (bf16[3,128,256]{2,1,0:T(8,128)(2,1)S(1)}, bf16[3,128,256]{2,1,0:T(8,128)(2,1)S(1)}, u32[]{:S(2)}, u32[]{:S(2)}) collective-permute-start(bf16[3,128,256]{2,1,0:T(8,128)(2,1)S(1)} %pack_far.1), channel_id=1, source_target_pairs={{0,4},{4,0},{1,5},{5,1},{2,6},{6,2},{3,7},{7,3},{8,12},{12,8},{9,1... | collective-permute-start | bytes 589832 | tf_op jit(solution)/shard_map/ppermute | solution.py:256
  34.2 17.7 %collective-permute-start = (bf16[128,768]{1,0:T(8,128)(2,1)S(1)}, bf16[128,768]{1,0:T(8,128)(2,1)S(1)}, u32[]{:S(2)}, u32[]{:S(2)}) collective-permute-start(bf16[128,768]{1,0:T(8,128)(2,1)S(1)} %get-tuple-element.14), channel_id=1, source_target_pairs={{0,1},{1,2},{2,3},{3,0},{4,5},{5,6},{6,7},{7,4},{8,9},{9,10},{10,1... | collective-permute-start | bytes 589832 | tf_op jit(solution)/shard_map/ppermute | solution.py:253
  37.6 39.3 %collective-permute-start.1 = (bf16[128,768]{1,0:T(8,128)(2,1)S(1)}, bf16[128,768]{1,0:T(8,128)(2,1)S(1)}, u32[]{:S(2)}, u32[]{:S(2)}) collective-permute-start(bf16[128,768]{1,0:T(8,128)(2,1)S(1)} %get-tuple-element.15), channel_id=1, source_target_pairs={{0,2},{1,3},{2,0},{3,1},{4,6},{5,7},{6,4},{7,5},{8,10},{9,11},{10,... | collective-permute-start | bytes 589832 | tf_op jit(solution)/shard_map/ppermute | solution.py:253
  42.2 34.7 %collective-permute-start.2 = (bf16[128,768]{1,0:T(8,128)(2,1)S(1)}, bf16[128,768]{1,0:T(8,128)(2,1)S(1)}, u32[]{:S(2)}, u32[]{:S(2)}) collective-permute-start(bf16[128,768]{1,0:T(8,128)(2,1)S(1)} %get-tuple-element.16), channel_id=1, source_target_pairs={{0,3},{1,0},{2,1},{3,2},{4,7},{5,4},{6,5},{7,6},{8,11},{9,8},{10,9... | collective-permute-start | bytes 589832 | tf_op jit(solution)/shard_map/ppermute | solution.py:253
  45.7 41.6 %collective-permute-start.4 = (bf16[128,256]{1,0:T(8,128)(2,1)S(1)}, bf16[128,256]{1,0:T(8,128)(2,1)S(1)}, u32[]{:S(2)}, u32[]{:S(2)}) collective-permute-start(bf16[128,256]{1,0:T(8,128)(2,1)S(1)} %get-tuple-element.18), channel_id=1, source_target_pairs={{0,1},{1,2},{2,3},{3,0},{4,5},{5,6},{6,7},{7,4},{8,9},{9,10},{10,1... | collective-permute-start | bytes 196616 | tf_op jit(solution)/shard_map/ppermute | solution.py:253
  48.1 39.1 %collective-permute-start.5 = (bf16[128,256]{1,0:T(8,128)(2,1)S(1)}, bf16[128,256]{1,0:T(8,128)(2,1)S(1)}, u32[]{:S(2)}, u32[]{:S(2)}) collective-permute-start(bf16[128,256]{1,0:T(8,128)(2,1)S(1)} %get-tuple-element.19), channel_id=1, source_target_pairs={{0,2},{1,3},{2,0},{3,1},{4,6},{5,7},{6,4},{7,5},{8,10},{9,11},{10,... | collective-permute-start | bytes 196616 | tf_op jit(solution)/shard_map/ppermute | solution.py:253
  51.9 35.4 %collective-permute-start.6 = (bf16[128,256]{1,0:T(8,128)(2,1)S(1)}, bf16[128,256]{1,0:T(8,128)(2,1)S(1)}, u32[]{:S(2)}, u32[]{:S(2)}) collective-permute-start(bf16[128,256]{1,0:T(8,128)(2,1)S(1)} %get-tuple-element.20), channel_id=1, source_target_pairs={{0,3},{1,0},{2,1},{3,2},{4,7},{5,4},{6,5},{7,6},{8,11},{9,8},{10,9... | collective-permute-start | bytes 196616 | tf_op jit(solution)/shard_map/ppermute | solution.py:253
  56.4 51.4 %all-to-all-start.1 = ((f32[16,1,1024]{2,1,0:T(1,128)}), f32[16,1,1024]{2,1,0:T(1,128)S(1)}, u32[]{:S(2)}, u32[]{:S(2)}) async-start(f32[16,1,1024]{2,1,0:T(1,128)} %broadcast_in_dim.15), calls=%async_computation.1 | async-start | bytes 131072 | tf_op jit(solution)/shard_map/all_to_all | solution.py:272
  76.9 28.3 %collective-permute-start.8 = (bf16[3,128,256]{2,1,0:T(8,128)(2,1)S(1)}, bf16[3,128,256]{2,1,0:T(8,128)(2,1)S(1)}, u32[]{:S(2)}, u32[]{:S(2)}) collective-permute-start(bf16[3,128,256]{2,1,0:T(8,128)(2,1)S(1)} %stack.1), channel_id=1, source_target_pairs={{0,4},{4,0},{1,5},{5,1},{2,6},{6,2},{3,7},{7,3},{8,12},{12,8},{9,1... | collective-permute-start | bytes 589832 | tf_op jit(solution)/shard_map/ppermute | solution.py:256
  87.3 2.3 %collective-permute-start.7 = (bf16[256,256]{1,0:T(8,128)(2,1)S(1)}, bf16[256,256]{1,0:T(8,128)(2,1)S(1)}, u32[]{:S(2)}, u32[]{:S(2)}) collective-permute-start(bf16[256,256]{1,0:T(8,128)(2,1)S(1)} %get-tuple-element.22), channel_id=1, source_target_pairs={{0,8},{8,16},{16,24},{24,32},{32,40},{40,48},{48,56},{56,64},{64,7... | collective-permute-start | bytes 393224 | tf_op jit(solution)/shard_map/ppermute | solution.py:267

commit v5 on v4

--- a/solution.py
+++ b/solution.py
@@ -44,22 +44,22 @@
     run_all(moves, sems)
 
 
-def pack_kernel(n, at_ref, q_ref, k_ref, v_ref, g_ref, *refs):
-    to, g_to, sems = refs[:n], refs[n], refs[n + 1]
-    side, x = place(at_ref, n)
+def pack_kernel(n, at_ref, q_ref, k_ref, v_ref, to, sems):
+    side, _ = place(at_ref, n)
     wide = q_ref.shape[1] // (2 * n)
     moves = []
+    for target in range(n):
+        head = side * (n // 2) + target // 2
+        moves.append((lanes_of(q_ref, side * n + target, wide), to.at[target, :, :wide]))
+        moves.append((lanes_of(k_ref, head, DH), to.at[target, :, wide : wide + DH]))
+        moves.append((lanes_of(v_ref, head, DH), to.at[target, :, wide + DH : wide + 2 * DH]))
+        moves.append((lanes_of(q_ref, (1 - side) * n + target, wide), to.at[target, :, wide + 2 * DH :]))
+    run_all(moves, sems)
+
+
+def pack_parts_kernel(_, g_ref, g_to, sems):
     chunk = g_ref.shape[-1]
-    for z in range(g_ref.shape[1]):
-        moves.append((g_ref.at[:, z], g_to.at[:, :, :, z * chunk : (z + 1) * chunk]))
-    for hop in range(n):
-        target = lax.rem(x + hop, n)
-        head = side * (n // 2) + lax.div(target, 2)
-        moves.append((lanes_of(q_ref, side * n + target, wide), to[hop].at[:, :wide]))
-        moves.append((lanes_of(k_ref, head, DH), to[hop].at[:, wide : wide + DH]))
-        moves.append((lanes_of(v_ref, head, DH), to[hop].at[:, wide + DH : wide + 2 * DH]))
-        if hop:
-            moves.append((lanes_of(q_ref, (1 - side) * n + target, wide), to[hop].at[:, wide + 2 * DH :]))
+    moves = [(g_ref.at[:, z], g_to.at[:, :, :, z * chunk : (z + 1) * chunk]) for z in range(g_ref.shape[1])]
     run_all(moves, sems)
 
 
@@ -88,40 +88,40 @@
     )[0]
 
 
-def packed(at, q, k, v, g, n):
+def packed(at, q, k, v, n):
     rows, wide = q.shape[0], q.shape[1] // (2 * n)
+    return kernel_call(
+        lambda *refs: pack_kernel(n, *refs),
+        (jax.ShapeDtypeStruct((n, rows, 2 * wide + 2 * DH), q.dtype),),
+        (at, q, k, v),
+        "pack",
+        scratch=(pltpu.SemaphoreType.DMA((4 * n,)),),
+        in_specs=[pl.BlockSpec(memory_space=pltpu.SMEM)] + [pl.BlockSpec(memory_space=pl.ANY)] * 3,
+    )[0]
+
+
+def packed_parts(at, g):
     yc, z, x, _, chunk = g.shape
-    outs = (
-        jax.ShapeDtypeStruct((rows, wide + 2 * DH), q.dtype),
-        *(jax.ShapeDtypeStruct((rows, 2 * wide + 2 * DH), q.dtype),) * (n - 1),
-        jax.ShapeDtypeStruct((yc, x, 1, z * chunk), g.dtype),
-    )
-    found = kernel_call(
-        lambda *refs: pack_kernel(n, *refs),
-        outs,
-        (at, q, k, v, g),
-        "pack",
-        scratch=(pltpu.SemaphoreType.DMA((4 * n - 1 + z,)),),
-        in_specs=[pl.BlockSpec(memory_space=pltpu.SMEM)] + [pl.BlockSpec(memory_space=pl.ANY)] * 4,
-    )
-    return found[:n], found[-1]
-
-
-def stack_kernel(n, *refs):
-    for hop in range(n):
-        refs[n][hop] = refs[hop][:, -refs[n].shape[-1] :]
-
-
-def stacked(pieces, wide):
-    n, rows = len(pieces), pieces[0].shape[0]
-    vmem = pl.BlockSpec(memory_space=pltpu.VMEM)
-    return kernel_call(
-        lambda *refs: stack_kernel(n, *refs),
-        (jax.ShapeDtypeStruct((n, rows, wide), pieces[0].dtype),),
-        tuple(pieces),
-        "stack",
-        in_specs=[vmem] * n,
-    )[0]
+    return kernel_call(
+        pack_parts_kernel,
+        (jax.ShapeDtypeStruct((yc, x, 1, z * chunk), g.dtype),),
+        (at, g),
+        "pack_parts",
+        scratch=(pltpu.SemaphoreType.DMA((z,)),),
+        in_specs=[pl.BlockSpec(memory_space=pltpu.SMEM), pl.BlockSpec(memory_space=pl.ANY)],
+    )[0]
+
+
+def stack_kernel(n, at_ref, near_ref, to):
+    _, x = place(at_ref, n)
+    for hop in range(1, n):
+        to[hop - 1] = near_ref[lax.rem(x + n - hop, n), :, -to.shape[-1] :]
+
+
+def stacked(at, near, wide):
+    n, rows = near.shape[:2]
+    outs = (jax.ShapeDtypeStruct((n - 1, rows, wide), near.dtype),)
+    return kernel_call(lambda *refs: stack_kernel(n, *refs), outs, (at, near), "stack")[0]
 
 
 def cut_kernel(n, at_ref, kv_ref, *to):
@@ -136,29 +136,28 @@
 
 
 def gather_kernel(n, at_ref, *refs):
-    near, far, (kv_ref, last_ref) = refs[:n], refs[n : 2 * n], refs[2 * n :]
+    near_ref, far, (kv_ref, last_ref) = refs[0], refs[1 : n + 1], refs[n + 1 :]
     side, x = place(at_ref, n)
     rows, width = far[0].shape
 
     def put(half, chunk, value):
         kv_ref[pl.ds(pl.multiple_of((half * n + chunk) * rows, rows), rows)] = value
 
+    wide = (near_ref.shape[-1] - width) // 2
     for hop in range(n):
-        chunk = lax.rem(x + n - hop, n)
-        wide = near[0].shape[1] - width
-        put(side, chunk, near[hop][:, wide : wide + width])
-        put(1 - side, chunk, far[hop][...])
+        put(side, hop, near_ref[hop, :, wide : wide + width])
+        put(1 - side, lax.rem(x + n - hop, n), far[hop][...])
     last_ref[...] = kv_ref[kv_ref.shape[0] - last_ref.shape[0] :]
 
 
 def gathered(at, near, far, reach):
     rows, width = far[0].shape
-    n = len(near)
+    n = len(far)
     outs = (
         jax.ShapeDtypeStruct((2 * n * rows, width), jnp.bfloat16),
         jax.ShapeDtypeStruct((reach, width), jnp.bfloat16),
     )
-    return kernel_call(lambda *refs: gather_kernel(n, *refs), outs, (at, *near, *far), "gather")
+    return kernel_call(lambda *refs: gather_kernel(n, *refs), outs, (at, near, *far), "gather")
 
 
 def attend_kernel(n, is_near, count, at_ref, kv_ref, prior_ref, *refs):
@@ -168,8 +167,8 @@
     rows, wide = q_s.shape[0] // n, q_s.shape[1]
     reach = prior_ref.shape[0]
     for hop in range(n):
-        chunk = lax.rem(x + n - hop, n)
-        value = pieces[hop][:, :wide] if is_near else pieces[0][hop - 1] if hop else pieces[1][n // 2]
+        chunk = hop if is_near else lax.rem(x + n - hop, n)
+        value = pieces[0][hop, :, :wide] if is_near else pieces[0][hop - 1] if hop else pieces[1][n // 2]
         q_s[pl.ds(pl.multiple_of(chunk * rows, rows), rows)] = value
     start = pl.multiple_of(half * n * rows, reach)
 
@@ -246,8 +245,10 @@
     wide = queries.shape[2] // (z * n)
     reach = queries.shape[1] * 2
     chunks = grad_parts.reshape(y * c, z, n, 1, -1)
-    kv_far = packed_far(at, queries[0], keys[0], values[0], n)
-    sent, parts = packed(at, queries[0], keys[0], values[0], chunks, n)
+    local = queries[0], keys[0], values[0]
+    kv_far = packed_far(at, *local, n)
+    sent = packed(at, *local, n)
+    parts = packed_parts(at, chunks)
 
     def along_x(value, hop):
         return lax.ppermute(value, "aa_1", [(x, (x + hop) % n) for x in range(n)])
@@ -255,17 +256,17 @@
     def across_z(value):
         return lax.ppermute(value, "aa_0", [(s, 1 - s) for s in range(z)])
 
+    near = lax.all_to_all(sent, "aa_1", 0, 0, tiled=True)
     kv_far = across_z(kv_far)
-    near = [sent[0]] + [along_x(sent[hop], hop) for hop in range(1, n)]
     parts = parts.reshape(y * c * n, 1, -1)
     parts = lax.all_to_all(parts, ("blk_0", "blk_1", "aa_1"), 0, 0, tiled=True)
-    q_far = stacked(near[1:], wide)
+    q_far = stacked(at, near, wide)
     q_far = across_z(q_far)
     far = cut(at, kv_far, n)
     far = [far[0]] + [along_x(far[hop], hop) for hop in range(1, n)]
     kv, last = gathered(at, near, far, reach)
     prior = lax.ppermute(last, BLK, [(i, i + 1) for i in range(y * c - 1)])
-    rows = attended_half(at, kv, prior, near, n, wide)
+    rows = attended_half(at, kv, prior, (near,), n, wide)
 
     share = jnp.sum(parts, axis=0).reshape(z, 1, -1)
     share = jnp.broadcast_to(share[None], (dp, *share.shape)).reshape(dp * z, 1, -1)

time: 109 us -> 127 us (1.17)
  the two profiles are of different devices: /device:TPU:128 before, /device:TPU:24 now
where the time goes in v5:
time: 127 us
  starting transfers between devices  84.9 us (67%)
  waiting for transfers between devices  30.7 us (24%)
  Pallas kernels  7.31 us (6%)
  local copies, waits for them, and re-layouts  1.82 us (1%)
    ppermute x2, starting transfers between devices, across_z(): return lax.ppermute(value, 'aa_0', [(s, 1 - s) for s in range(z)])  25.2 us
    all_to_all x1, starting transfers between devices, step(): share = lax.all_to_all(share, ('dp', 'aa_0'), 0, 0, tiled=True)  24.6 us
    all_to_all x1, starting transfers between devices, step(): parts = lax.all_to_all(parts, ('blk_0', 'blk_1', 'aa_1'), 0, 0, tiled=True)  17.2 us
    all_to_all x1, waiting for transfers between devices, step(): parts = lax.all_to_all(parts, ('blk_0', 'blk_1', 'aa_1'), 0, 0, tiled=True)  14 us
    ppermute x2, waiting for transfers between devices, across_z(): return lax.ppermute(value, 'aa_0', [(s, 1 - s) for s in range(z)])  12.4 us
    ppermute x3, starting transfers between devices, along_x(): return lax.ppermute(value, 'aa_1', [(x, (x + hop) % n) for x in range(n)])  12.2 us
    pallas_call x8, Pallas kernels, kernel_call(): return pl.pallas_call(body, **settings)(*ins)  7.31 us
    ppermute x1, waiting for transfers between devices, step(): prior = lax.ppermute(last, BLK, [(i, i + 1) for i in range(y * c - 1)])  4.36 us
  transfers between devices with their start and end apart: 9, of which 4 were waited for; matrix products, arithmetic and copies ran while one was open for 1% of the time, Pallas kernels for 5%

profile of v5, /device:TPU:24, one launch (start us, length us, event | category | flops | bytes accessed | tf_op | source)
XLA Modules:
  0.0 126.6 jit_solution(7804179133626745372)
XLA Ops:
  0.6 1.0 copy-done.3
  1.7 0.8 pack_parts.1
  2.5 0.0 copy-start
  2.5 0.0 copy-start.1
  2.6 0.0 copy-start.2
  2.6 17.2 %all-to-all-start.1 = ((f32[64,1,2048]{2,1,0:T(1,128)}), f32[64,1,2048]{2,1,0:T(1,128)S(1)}, u32[]{:S(2)}, u32[]{:S(2)}) async-start(f32[64,1,2048]{2,1,0:T(1,128)} %bitcast.6), calls=%async_computation.1 | async-start | bytes 1048576 | tf_op jit(solution)/shard_map/all_to_all | solution.py:262
  19.8 1.2 pack.1
  21.0 14.0 %all-to-all-done.1 = f32[64,1,2048]{2,1,0:T(1,128)S(1)} async-done(((f32[64,1,2048]{2,1,0:T(1,128)}), f32[64,1,2048]{2,1,0:T(1,128)S(1)}, u32[]{:S(2)}, u32[]{:S(2)}) %all-to-all-start.1) | async-done | bytes 524320 | tf_op jit(solution)/shard_map/all_to_all | solution.py:262
  35.0 3.7 %all-to-all-start = ((bf16[4,128,768]{2,1,0:T(8,128)(2,1)}), bf16[4,128,768]{2,1,0:T(8,128)(2,1)S(1)}, u32[]{:S(2)}, u32[]{:S(2)}) async-start(bf16[4,128,768]{2,1,0:T(8,128)(2,1)} %pack.1), calls=%async_computation | async-start | bytes 1572864 | tf_op jit(solution)/shard_map/all_to_all | solution.py:259
  38.8 0.1 pack_far.1
  38.8 12.7 %collective-permute-start = (bf16[3,128,256]{2,1,0:T(8,128)(2,1)S(1)}, bf16[3,128,256]{2,1,0:T(8,128)(2,1)S(1)}, u32[]{:S(2)}, u32[]{:S(2)}) collective-permute-start(bf16[3,128,256]{2,1,0:T(8,128)(2,1)S(1)} %pack_far.1), channel_id=1, source_target_pairs={{0,4},{4,0},{1,5},{5,1},{2,6},{6,2},{3,7},{7,3},{8,12},{12,8},{9,1... | collective-permute-start | bytes 589832 | tf_op jit(solution)/shard_map/ppermute | solution.py:257
  51.5 5.5 %collective-permute-done.refs_1_.refs_4_ = bf16[3,128,256]{2,1,0:T(8,128)(2,1)S(1)} collective-permute-done((bf16[3,128,256]{2,1,0:T(8,128)(2,1)S(1)}, bf16[3,128,256]{2,1,0:T(8,128)(2,1)S(1)}, u32[]{:S(2)}, u32[]{:S(2)}) %collective-permute-start) | collective-permute-done | bytes 196640 | tf_op jit(solution)/shard_map/ppermute | solution.py:257
  57.1 4.3 %collective-permute-start.1 = (bf16[128,256]{1,0:T(8,128)(2,1)S(1)}, bf16[128,256]{1,0:T(8,128)(2,1)S(1)}, u32[]{:S(2)}, u32[]{:S(2)}) collective-permute-start(bf16[128,256]{1,0:T(8,128)(2,1)S(1)} %get-tuple-element.9), channel_id=1, source_target_pairs={{0,1},{1,2},{2,3},{3,0},{4,5},{5,6},{6,7},{7,4},{8,9},{9,10},{10,1... | collective-permute-start | bytes 196616 | tf_op jit(solution)/shard_map/ppermute | solution.py:254
  61.3 4.6 %collective-permute-start.2 = (bf16[128,256]{1,0:T(8,128)(2,1)S(1)}, bf16[128,256]{1,0:T(8,128)(2,1)S(1)}, u32[]{:S(2)}, u32[]{:S(2)}) collective-permute-start(bf16[128,256]{1,0:T(8,128)(2,1)S(1)} %get-tuple-element.10), channel_id=1, source_target_pairs={{0,2},{1,3},{2,0},{3,1},{4,6},{5,7},{6,4},{7,5},{8,10},{9,11},{10,... | collective-permute-start | bytes 196616 | tf_op jit(solution)/shard_map/ppermute | solution.py:254
  65.9 3.4 %collective-permute-start.3 = (bf16[128,256]{1,0:T(8,128)(2,1)S(1)}, bf16[128,256]{1,0:T(8,128)(2,1)S(1)}, u32[]{:S(2)}, u32[]{:S(2)}) collective-permute-start(bf16[128,256]{1,0:T(8,128)(2,1)S(1)} %get-tuple-element.11), channel_id=1, source_target_pairs={{0,3},{1,0},{2,1},{3,2},{4,7},{5,4},{6,5},{7,6},{8,11},{9,8},{10,9... | collective-permute-start | bytes 196616 | tf_op jit(solution)/shard_map/ppermute | solution.py:254
  69.3 0.3 reduce_sum.18
  69.7 0.7 broadcast_in_dim.15
  70.4 0.0 all-to-all-done.refs_1_.refs_3_
  70.4 24.6 %all-to-all-start.2 = ((f32[16,1,1024]{2,1,0:T(1,128)}), f32[16,1,1024]{2,1,0:T(1,128)S(1)}, u32[]{:S(2)}, u32[]{:S(2)}) async-start(f32[16,1,1024]{2,1,0:T(1,128)} %broadcast_in_dim.15), calls=%async_computation.2 | async-start | bytes 131072 | tf_op jit(solution)/shard_map/all_to_all | solution.py:273
  95.1 12.5 %collective-permute-start.5 = (bf16[3,128,256]{2,1,0:T(8,128)(2,1)S(1)}, bf16[3,128,256]{2,1,0:T(8,128)(2,1)S(1)}, u32[]{:S(2)}, u32[]{:S(2)}) collective-permute-start(bf16[3,128,256]{2,1,0:T(8,128)(2,1)S(1)} %stack.1), channel_id=1, source_target_pairs={{0,4},{4,0},{1,5},{5,1},{2,6},{6,2},{3,7},{7,3},{8,12},{12,8},{9,1... | collective-permute-start | bytes 589832 | tf_op jit(solution)/shard_map/ppermute | solution.py:257
  107.6 0.0 collective-permute-done.1.refs_3_
  107.6 0.0 collective-permute-done.2.refs_4_
  107.6 0.0 collective-permute-done.3.refs_5_
  107.6 0.1 gather.1
  107.7 1.9 %collective-permute-start.4 = (bf16[256,256]{1,0:T(8,128)(2,1)S(1)}, bf16[256,256]{1,0:T(8,128)(2,1)S(1)}, u32[]{:S(2)}, u32[]{:S(2)}) collective-permute-start(bf16[256,256]{1,0:T(8,128)(2,1)S(1)} %get-tuple-element.13), channel_id=1, source_target_pairs={{0,8},{8,16},{16,24},{24,32},{32,40},{40,48},{48,56},{56,64},{64,7... | collective-permute-start | bytes 393224 | tf_op jit(solution)/shard_map/ppermute | solution.py:268
  109.6 4.4 %collective-permute-done.4.refs_2_ = bf16[256,256]{1,0:T(8,128)(2,1)S(1)} collective-permute-done((bf16[256,256]{1,0:T(8,128)(2,1)S(1)}, bf16[256,256]{1,0:T(8,128)(2,1)S(1)}, u32[]{:S(2)}, u32[]{:S(2)}) %collective-permute-start.4) | collective-permute-done | bytes 131104 | tf_op jit(solution)/shard_map/ppermute | solution.py:268
  114.0 2.5 %attend.2.refs_5_ = bf16[1024,256]{1,0:T(8,128)(2,1)} custom-call(s32[1]{0:T(128)} %bitcast.refs_0_._, bf16[1024,256]{1,0:T(8,128)(2,1)S(1)} %get-tuple-element.12.refs_1_, bf16[256,256]{1,0:T(8,128)(2,1)S(1)} %collective-permute-done.4.refs_2_, bf16[4,128,768]{2,1,0:T(8,128)(2,1)S(1)} %all-to-all-done.refs_1_.refs_3_), custom_call_target="tpu_custom_call" | custom-call | flops 268435456 | bytes 1048576 | tf_op jit(solution)/shard_map/attend/pallas_call | solution.py:77
  116.5 6.9 %collective-permute-done.5.refs_3_ = bf16[3,128,256]{2,1,0:T(8,128)(2,1)S(1)} collective-permute-done((bf16[3,128,256]{2,1,0:T(8,128)(2,1)S(1)}, bf16[3,128,256]{2,1,0:T(8,128)(2,1)S(1)}, u32[]{:S(2)}, u32[]{:S(2)}) %collective-permute-start.5) | collective-permute-done | bytes 196640 | tf_op jit(solution)/shard_map/ppermute | solution.py:257
  123.4 2.5 %attend.3 = bf16[1024,256]{1,0:T(8,128)(2,1)} custom-call(s32[1]{0:T(128)} %bitcast.refs_0_._, bf16[1024,256]{1,0:T(8,128)(2,1)S(1)} %get-tuple-element.12.refs_1_, bf16[256,256]{1,0:T(8,128)(2,1)S(1)} %collective-permute-done.4.refs_2_, bf16[3,128,256]{2,1,0:T(8,128)(2,1)S(1)} %collective-permute-done.5.refs_3_, ...), custom_call_target="tpu_custom_call", output_to_operand_aliasing={{}: (5, {})} | custom-call | flops 268435456 | bytes 1048576 | tf_op jit(solution)/shard_map/attend/pallas_call | solution.py:77
  125.9 0.0 all-to-all-done.2
  125.9 0.1 reduce_sum.19
  126.0 0.6 broadcast_multiply_fusion
  (8 shorter events, 0.1 us)
Async XLA Ops:
  0.6 1.0 copy-start.3
  2.5 17.3 %copy-start = (bf16[1,128,2048]{2,1,0:T(8,128)(2,1)S(1)}, bf16[1,128,2048]{2,1,0:T(8,128)(2,1)}, u32[]{:S(2)}) copy-start(bf16[1,128,2048]{2,1,0:T(8,128)(2,1)} %param.4) | copy-start | bytes 1572868
  2.5 17.3 %copy-start.1 = (bf16[1,128,512]{2,1,0:T(8,128)(2,1)S(1)}, bf16[1,128,512]{2,1,0:T(8,128)(2,1)}, u32[]{:S(2)}) copy-start(bf16[1,128,512]{2,1,0:T(8,128)(2,1)} %param.5) | copy-start | bytes 393220
  2.6 17.3 %copy-start.2 = (bf16[1,128,512]{2,1,0:T(8,128)(2,1)S(1)}, bf16[1,128,512]{2,1,0:T(8,128)(2,1)}, u32[]{:S(2)}) copy-start(bf16[1,128,512]{2,1,0:T(8,128)(2,1)} %param.6) | copy-start | bytes 393220
  2.6 32.5 %all-to-all-start.1 = ((f32[64,1,2048]{2,1,0:T(1,128)}), f32[64,1,2048]{2,1,0:T(1,128)S(1)}, u32[]{:S(2)}, u32[]{:S(2)}) async-start(f32[64,1,2048]{2,1,0:T(1,128)} %bitcast.6), calls=%async_computation.1 | async-start | bytes 1048576 | tf_op jit(solution)/shard_map/all_to_all | solution.py:262
  35.0 35.4 %all-to-all-start = ((bf16[4,128,768]{2,1,0:T(8,128)(2,1)}), bf16[4,128,768]{2,1,0:T(8,128)(2,1)S(1)}, u32[]{:S(2)}, u32[]{:S(2)}) async-start(bf16[4,128,768]{2,1,0:T(8,128)(2,1)} %pack.1), calls=%async_computation | async-start | bytes 1572864 | tf_op jit(solution)/shard_map/all_to_all | solution.py:259
  38.8 18.2 %collective-permute-start = (bf16[3,128,256]{2,1,0:T(8,128)(2,1)S(1)}, bf16[3,128,256]{2,1,0:T(8,128)(2,1)S(1)}, u32[]{:S(2)}, u32[]{:S(2)}) collective-permute-start(bf16[3,128,256]{2,1,0:T(8,128)(2,1)S(1)} %pack_far.1), channel_id=1, source_target_pairs={{0,4},{4,0},{1,5},{5,1},{2,6},{6,2},{3,7},{7,3},{8,12},{12,8},{9,1... | collective-permute-start | bytes 589832 | tf_op jit(solution)/shard_map/ppermute | solution.py:257
  57.1 50.5 %collective-permute-start.1 = (bf16[128,256]{1,0:T(8,128)(2,1)S(1)}, bf16[128,256]{1,0:T(8,128)(2,1)S(1)}, u32[]{:S(2)}, u32[]{:S(2)}) collective-permute-start(bf16[128,256]{1,0:T(8,128)(2,1)S(1)} %get-tuple-element.9), channel_id=1, source_target_pairs={{0,1},{1,2},{2,3},{3,0},{4,5},{5,6},{6,7},{7,4},{8,9},{9,10},{10,1... | collective-permute-start | bytes 196616 | tf_op jit(solution)/shard_map/ppermute | solution.py:254
  61.3 46.3 %collective-permute-start.2 = (bf16[128,256]{1,0:T(8,128)(2,1)S(1)}, bf16[128,256]{1,0:T(8,128)(2,1)S(1)}, u32[]{:S(2)}, u32[]{:S(2)}) collective-permute-start(bf16[128,256]{1,0:T(8,128)(2,1)S(1)} %get-tuple-element.10), channel_id=1, source_target_pairs={{0,2},{1,3},{2,0},{3,1},{4,6},{5,7},{6,4},{7,5},{8,10},{9,11},{10,... | collective-permute-start | bytes 196616 | tf_op jit(solution)/shard_map/ppermute | solution.py:254
  65.9 41.7 %collective-permute-start.3 = (bf16[128,256]{1,0:T(8,128)(2,1)S(1)}, bf16[128,256]{1,0:T(8,128)(2,1)S(1)}, u32[]{:S(2)}, u32[]{:S(2)}) collective-permute-start(bf16[128,256]{1,0:T(8,128)(2,1)S(1)} %get-tuple-element.11), channel_id=1, source_target_pairs={{0,3},{1,0},{2,1},{3,2},{4,7},{5,4},{6,5},{7,6},{8,11},{9,8},{10,9... | collective-permute-start | bytes 196616 | tf_op jit(solution)/shard_map/ppermute | solution.py:254
  70.4 55.5 %all-to-all-start.2 = ((f32[16,1,1024]{2,1,0:T(1,128)}), f32[16,1,1024]{2,1,0:T(1,128)S(1)}, u32[]{:S(2)}, u32[]{:S(2)}) async-start(f32[16,1,1024]{2,1,0:T(1,128)} %broadcast_in_dim.15), calls=%async_computation.2 | async-start | bytes 131072 | tf_op jit(solution)/shard_map/all_to_all | solution.py:273
  95.1 28.3 %collective-permute-start.5 = (bf16[3,128,256]{2,1,0:T(8,128)(2,1)S(1)}, bf16[3,128,256]{2,1,0:T(8,128)(2,1)S(1)}, u32[]{:S(2)}, u32[]{:S(2)}) collective-permute-start(bf16[3,128,256]{2,1,0:T(8,128)(2,1)S(1)} %stack.1), channel_id=1, source_target_pairs={{0,4},{4,0},{1,5},{5,1},{2,6},{6,2},{3,7},{7,3},{8,12},{12,8},{9,1... | collective-permute-start | bytes 589832 | tf_op jit(solution)/shard_map/ppermute | solution.py:257
  107.7 6.3 %collective-permute-start.4 = (bf16[256,256]{1,0:T(8,128)(2,1)S(1)}, bf16[256,256]{1,0:T(8,128)(2,1)S(1)}, u32[]{:S(2)}, u32[]{:S(2)}) collective-permute-start(bf16[256,256]{1,0:T(8,128)(2,1)S(1)} %get-tuple-element.13), channel_id=1, source_target_pairs={{0,8},{8,16},{16,24},{24,32},{32,40},{40,48},{48,56},{56,64},{64,7... | collective-permute-start | bytes 393224 | tf_op jit(solution)/shard_map/ppermute | solution.py:268

commit v6 on v5

--- a/solution.py
+++ b/solution.py
@@ -44,7 +44,7 @@
     run_all(moves, sems)
 
 
-def pack_kernel(n, at_ref, q_ref, k_ref, v_ref, to, sems):
+def pack_kernel(n, at_ref, q_ref, k_ref, v_ref, far_to, to, sems):
     side, _ = place(at_ref, n)
     wide = q_ref.shape[1] // (2 * n)
     moves = []
@@ -53,7 +53,7 @@
         moves.append((lanes_of(q_ref, side * n + target, wide), to.at[target, :, :wide]))
         moves.append((lanes_of(k_ref, head, DH), to.at[target, :, wide : wide + DH]))
         moves.append((lanes_of(v_ref, head, DH), to.at[target, :, wide + DH : wide + 2 * DH]))
-        moves.append((lanes_of(q_ref, (1 - side) * n + target, wide), to.at[target, :, wide + 2 * DH :]))
+        moves.append((lanes_of(q_ref, (1 - side) * n + target, wide), far_to.at[target]))
     run_all(moves, sems)
 
 
@@ -83,6 +83,7 @@
         (jax.ShapeDtypeStruct((n // 2 + 1, k.shape[0], 2 * DH), k.dtype),),
         (at, q, k, v),
         "pack_far",
+        limit=60 << 20,
         scratch=(pltpu.SemaphoreType.DMA((n + 1,)),),
         in_specs=[pl.BlockSpec(memory_space=pltpu.SMEM)] + [pl.BlockSpec(memory_space=pl.ANY)] * 3,
     )[0]
@@ -92,12 +93,15 @@
     rows, wide = q.shape[0], q.shape[1] // (2 * n)
     return kernel_call(
         lambda *refs: pack_kernel(n, *refs),
-        (jax.ShapeDtypeStruct((n, rows, 2 * wide + 2 * DH), q.dtype),),
+        (
+            jax.ShapeDtypeStruct((n, rows, wide), q.dtype),
+            jax.ShapeDtypeStruct((n, rows, wide + 2 * DH), q.dtype),
+        ),
         (at, q, k, v),
         "pack",
         scratch=(pltpu.SemaphoreType.DMA((4 * n,)),),
         in_specs=[pl.BlockSpec(memory_space=pltpu.SMEM)] + [pl.BlockSpec(memory_space=pl.ANY)] * 3,
-    )[0]
+    )
 
 
 def packed_parts(at, g):
@@ -107,6 +111,7 @@
         (jax.ShapeDtypeStruct((yc, x, 1, z * chunk), g.dtype),),
         (at, g),
         "pack_parts",
+        limit=60 << 20,
         scratch=(pltpu.SemaphoreType.DMA((z,)),),
         in_specs=[pl.BlockSpec(memory_space=pltpu.SMEM), pl.BlockSpec(memory_space=pl.ANY)],
     )[0]
@@ -124,40 +129,42 @@
     return kernel_call(lambda *refs: stack_kernel(n, *refs), outs, (at, near), "stack")[0]
 
 
-def cut_kernel(n, at_ref, kv_ref, *to):
+def cut_kernel(n, at_ref, near_ref, kv_ref, *to):
     _, x = place(at_ref, n)
     for hop in range(n):
-        to[hop][...] = kv_ref[lax.div(lax.rem(x + hop, n), 2)]
-
-
-def cut(at, kv, n):
-    outs = (jax.ShapeDtypeStruct(kv.shape[1:], kv.dtype),) * n
-    return kernel_call(lambda *refs: cut_kernel(n, *refs), outs, (at, kv), "cut")
+        target = lax.rem(x + hop, n)
+        to[hop][:, : near_ref.shape[-1]] = near_ref[target]
+        to[hop][:, near_ref.shape[-1] :] = kv_ref[lax.div(target, 2)]
+
+
+def cut(at, near, kv):
+    n, rows, wide = near.shape
+    outs = (jax.ShapeDtypeStruct((rows, wide + kv.shape[-1]), kv.dtype),) * n
+    return kernel_call(lambda *refs: cut_kernel(n, *refs), outs, (at, near, kv), "cut")
 
 
 def gather_kernel(n, at_ref, *refs):
-    near_ref, far, (kv_ref, last_ref) = refs[0], refs[1 : n + 1], refs[n + 1 :]
+    both, (kv_ref, last_ref) = refs[:n], refs[n:]
     side, x = place(at_ref, n)
-    rows, width = far[0].shape
+    rows, width = both[0].shape[0], kv_ref.shape[1]
 
     def put(half, chunk, value):
         kv_ref[pl.ds(pl.multiple_of((half * n + chunk) * rows, rows), rows)] = value
 
-    wide = (near_ref.shape[-1] - width) // 2
     for hop in range(n):
-        put(side, hop, near_ref[hop, :, wide : wide + width])
-        put(1 - side, lax.rem(x + n - hop, n), far[hop][...])
+        chunk = lax.rem(x + n - hop, n)
+        put(side, chunk, both[hop][:, -2 * width : -width])
+        put(1 - side, chunk, both[hop][:, -width:])
     last_ref[...] = kv_ref[kv_ref.shape[0] - last_ref.shape[0] :]
 
 
-def gathered(at, near, far, reach):
-    rows, width = far[0].shape
-    n = len(far)
+def gathered(at, both, reach):
+    n, rows = len(both), both[0].shape[0]
     outs = (
-        jax.ShapeDtypeStruct((2 * n * rows, width), jnp.bfloat16),
-        jax.ShapeDtypeStruct((reach, width), jnp.bfloat16),
-    )
-    return kernel_call(lambda *refs: gather_kernel(n, *refs), outs, (at, near, *far), "gather")
+        jax.ShapeDtypeStruct((2 * n * rows, 2 * DH), jnp.bfloat16),
+        jax.ShapeDtypeStruct((reach, 2 * DH), jnp.bfloat16),
+    )
+    return kernel_call(lambda *refs: gather_kernel(n, *refs), outs, (at, *both), "gather")
 
 
 def attend_kernel(n, is_near, count, at_ref, kv_ref, prior_ref, *refs):
@@ -167,8 +174,8 @@
     rows, wide = q_s.shape[0] // n, q_s.shape[1]
     reach = prior_ref.shape[0]
     for hop in range(n):
-        chunk = hop if is_near else lax.rem(x + n - hop, n)
-        value = pieces[0][hop, :, :wide] if is_near else pieces[0][hop - 1] if hop else pieces[1][n // 2]
+        chunk = lax.rem(x + n - hop, n)
+        value = pieces[hop][:, :wide] if is_near else pieces[0][hop - 1] if hop else pieces[1][n // 2]
         q_s[pl.ds(pl.multiple_of(chunk * rows, rows), rows)] = value
     start = pl.multiple_of(half * n * rows, reach)
 
@@ -247,7 +254,7 @@
     chunks = grad_parts.reshape(y * c, z, n, 1, -1)
     local = queries[0], keys[0], values[0]
     kv_far = packed_far(at, *local, n)
-    sent = packed(at, *local, n)
+    sent, near = packed(at, *local, n)
     parts = packed_parts(at, chunks)
 
     def along_x(value, hop):
@@ -256,17 +263,17 @@
     def across_z(value):
         return lax.ppermute(value, "aa_0", [(s, 1 - s) for s in range(z)])
 
-    near = lax.all_to_all(sent, "aa_1", 0, 0, tiled=True)
+    q_far = lax.all_to_all(sent, "aa_1", 0, 0, tiled=True)
     kv_far = across_z(kv_far)
     parts = parts.reshape(y * c * n, 1, -1)
     parts = lax.all_to_all(parts, ("blk_0", "blk_1", "aa_1"), 0, 0, tiled=True)
-    q_far = stacked(at, near, wide)
+    q_far = stacked(at, q_far, wide)
     q_far = across_z(q_far)
-    far = cut(at, kv_far, n)
-    far = [far[0]] + [along_x(far[hop], hop) for hop in range(1, n)]
-    kv, last = gathered(at, near, far, reach)
+    both = cut(at, near, kv_far)
+    both = [both[0]] + [along_x(both[hop], hop) for hop in range(1, n)]
+    kv, last = gathered(at, both, reach)
     prior = lax.ppermute(last, BLK, [(i, i + 1) for i in range(y * c - 1)])
-    rows = attended_half(at, kv, prior, (near,), n, wide)
+    rows = attended_half(at, kv, prior, both, n, wide)
 
     share = jnp.sum(parts, axis=0).reshape(z, 1, -1)
     share = jnp.broadcast_to(share[None], (dp, *share.shape)).reshape(dp * z, 1, -1)

time: 127 us -> 107 us (0.84)
  the two profiles are of different devices: /device:TPU:24 before, /device:TPU:128 now
where the time goes in v6:
time: 107 us
  starting transfers between devices  76.1 us (71%)
  waiting for transfers between devices  18.5 us (17%)
  Pallas kernels  9.74 us (9%)
    ppermute x2, starting transfers between devices, across_z(): return lax.ppermute(value, 'aa_0', [(s, 1 - s) for s in range(z)])  27.8 us
    all_to_all x1, starting transfers between devices, step(): share = lax.all_to_all(share, ('dp', 'aa_0'), 0, 0, tiled=True)  20.5 us
    ppermute x2, waiting for transfers between devices, across_z(): return lax.ppermute(value, 'aa_0', [(s, 1 - s) for s in range(z)])  17.5 us
    ppermute x3, starting transfers between devices, along_x(): return lax.ppermute(value, 'aa_1', [(x, (x + hop) % n) for x in range(n)])  11.5 us
    all_to_all x1, starting transfers between devices, step(): parts = lax.all_to_all(parts, ('blk_0', 'blk_1', 'aa_1'), 0, 0, tiled=True)  10.6 us
    pallas_call x8, Pallas kernels, kernel_call(): return pl.pallas_call(body, **settings)(*ins)  9.74 us
    all_to_all x1, starting transfers between devices, step(): q_far = lax.all_to_all(sent, 'aa_1', 0, 0, tiled=True)  4.36 us
  transfers between devices with their start and end apart: 9, of which 3 were waited for; matrix products, arithmetic and copies ran while one was open for 1% of the time, Pallas kernels for 7%

profile of v6, /device:TPU:128, one launch (start us, length us, event | category | flops | bytes accessed | tf_op | source)
XLA Modules:
  0.0 106.9 jit_solution(1097871261896798133)
XLA Ops:
  0.6 1.8 %pack_parts.1 = f32[16,4,1,2048]{3,2,1,0:T(1,128)} custom-call(s32[1]{0:T(128)} %bitcast.refs_0_._, f32[16,2,4,1,1024]{4,3,2,1,0:T(1,128)} %bitcast.15), custom_call_target="tpu_custom_call" | custom-call | tf_op jit(solution)/shard_map/pack_parts/pallas_call | solution.py:77
  2.5 10.6 %all-to-all-start.1 = ((f32[64,1,2048]{2,1,0:T(1,128)}), f32[64,1,2048]{2,1,0:T(1,128)S(1)}, u32[]{:S(2)}, u32[]{:S(2)}) async-start(f32[64,1,2048]{2,1,0:T(1,128)} %bitcast.14), calls=%async_computation.1 | async-start | bytes 1048576 | tf_op jit(solution)/shard_map/all_to_all | solution.py:269
  13.1 0.0 copy-start
  13.1 0.0 copy-start.1
  13.1 0.0 copy-start.2
  13.1 1.7 %pack_far.1 = bf16[3,128,256]{2,1,0:T(8,128)(2,1)} custom-call(s32[1]{0:T(128)} %bitcast.refs_0_._, bf16[128,2048]{1,0:T(8,128)(2,1)} %bitcast.7, bf16[128,512]{1,0:T(8,128)(2,1)} %bitcast.9, bf16[128,512]{1,0:T(8,128)(2,1)} %bitcast.11), custom_call_target="tpu_custom_call" | custom-call | tf_op jit(solution)/shard_map/pack_far/pallas_call | solution.py:77
  14.8 17.6 %collective-permute-start = (bf16[3,128,256]{2,1,0:T(8,128)(2,1)}, bf16[3,128,256]{2,1,0:T(8,128)(2,1)S(1)}, u32[]{:S(2)}, u32[]{:S(2)}) collective-permute-start(bf16[3,128,256]{2,1,0:T(8,128)(2,1)} %pack_far.1), channel_id=1, source_target_pairs={{0,4},{4,0},{1,5},{5,1},{2,6},{6,2},{3,7},{7,3},{8,12},{12,8},{9,1... | collective-permute-start | bytes 589832 | tf_op jit(solution)/shard_map/ppermute | solution.py:264
  32.4 1.0 pack.1
  33.4 0.0 all-to-all-done.1
  33.4 4.4 %all-to-all-start = ((bf16[4,128,256]{2,1,0:T(8,128)(2,1)}), bf16[4,128,256]{2,1,0:T(8,128)(2,1)S(1)}, u32[]{:S(2)}, u32[]{:S(2)}) async-start(bf16[4,128,256]{2,1,0:T(8,128)(2,1)} %get-tuple-element.17), calls=%async_computation | async-start | bytes 524288 | tf_op jit(solution)/shard_map/all_to_all | solution.py:266
  37.8 4.4 %collective-permute-done.refs_2_.refs_4_ = bf16[3,128,256]{2,1,0:T(8,128)(2,1)S(1)} collective-permute-done((bf16[3,128,256]{2,1,0:T(8,128)(2,1)}, bf16[3,128,256]{2,1,0:T(8,128)(2,1)S(1)}, u32[]{:S(2)}, u32[]{:S(2)}) %collective-permute-start) | collective-permute-done | bytes 196640 | tf_op jit(solution)/shard_map/ppermute | solution.py:264
  42.1 0.1 cut.1
  42.2 3.5 %collective-permute-start.1 = (bf16[128,768]{1,0:T(8,128)(2,1)S(1)}, bf16[128,768]{1,0:T(8,128)(2,1)S(1)}, u32[]{:S(2)}, u32[]{:S(2)}) collective-permute-start(bf16[128,768]{1,0:T(8,128)(2,1)S(1)} %get-tuple-element.12), channel_id=1, source_target_pairs={{0,1},{1,2},{2,3},{3,0},{4,5},{5,6},{6,7},{7,4},{8,9},{9,10},{10,1... | collective-permute-start | bytes 589832 | tf_op jit(solution)/shard_map/ppermute | solution.py:261
  45.7 4.6 %collective-permute-start.2 = (bf16[128,768]{1,0:T(8,128)(2,1)S(1)}, bf16[128,768]{1,0:T(8,128)(2,1)S(1)}, u32[]{:S(2)}, u32[]{:S(2)}) collective-permute-start(bf16[128,768]{1,0:T(8,128)(2,1)S(1)} %get-tuple-element.13), channel_id=1, source_target_pairs={{0,2},{1,3},{2,0},{3,1},{4,6},{5,7},{6,4},{7,5},{8,10},{9,11},{10,... | collective-permute-start | bytes 589832 | tf_op jit(solution)/shard_map/ppermute | solution.py:261
  50.3 3.4 %collective-permute-start.3 = (bf16[128,768]{1,0:T(8,128)(2,1)S(1)}, bf16[128,768]{1,0:T(8,128)(2,1)S(1)}, u32[]{:S(2)}, u32[]{:S(2)}) collective-permute-start(bf16[128,768]{1,0:T(8,128)(2,1)S(1)} %get-tuple-element.14), channel_id=1, source_target_pairs={{0,3},{1,0},{2,1},{3,2},{4,7},{5,4},{6,5},{7,6},{8,11},{9,8},{10,9... | collective-permute-start | bytes 589832 | tf_op jit(solution)/shard_map/ppermute | solution.py:261
  53.7 0.3 reduce_sum.18
  54.1 0.7 broadcast_in_dim.15
  54.8 0.0 all-to-all-done.refs_1_
  54.8 20.5 %all-to-all-start.2 = ((f32[16,1,1024]{2,1,0:T(1,128)}), f32[16,1,1024]{2,1,0:T(1,128)S(1)}, u32[]{:S(2)}, u32[]{:S(2)}) async-start(f32[16,1,1024]{2,1,0:T(1,128)} %broadcast_in_dim.15), calls=%async_computation.2 | async-start | bytes 131072 | tf_op jit(solution)/shard_map/all_to_all | solution.py:280
  75.3 10.3 %collective-permute-start.5 = (bf16[3,128,256]{2,1,0:T(8,128)(2,1)S(1)}, bf16[3,128,256]{2,1,0:T(8,128)(2,1)S(1)}, u32[]{:S(2)}, u32[]{:S(2)}) collective-permute-start(bf16[3,128,256]{2,1,0:T(8,128)(2,1)S(1)} %stack.1), channel_id=1, source_target_pairs={{0,4},{4,0},{1,5},{5,1},{2,6},{6,2},{3,7},{7,3},{8,12},{12,8},{9,1... | collective-permute-start | bytes 589832 | tf_op jit(solution)/shard_map/ppermute | solution.py:264
  85.6 0.0 collective-permute-done.1.refs_2_.refs_4_
  85.6 0.0 collective-permute-done.2.refs_3_.refs_5_
  85.6 0.0 collective-permute-done.3.refs_4_.refs_6_
  85.7 0.1 gather.1
  85.7 1.3 %collective-permute-start.4 = (bf16[256,256]{1,0:T(8,128)(2,1)S(1)}, bf16[256,256]{1,0:T(8,128)(2,1)S(1)}, u32[]{:S(2)}, u32[]{:S(2)}) collective-permute-start(bf16[256,256]{1,0:T(8,128)(2,1)S(1)} %get-tuple-element.16), channel_id=1, source_target_pairs={{0,8},{8,16},{16,24},{24,32},{32,40},{40,48},{48,56},{56,64},{64,7... | collective-permute-start | bytes 393224 | tf_op jit(solution)/shard_map/ppermute | solution.py:275
  87.0 1.0 collective-permute-done.4.refs_2_
  88.0 2.5 %attend.2.refs_5_ = bf16[1024,256]{1,0:T(8,128)(2,1)} custom-call(s32[1]{0:T(128)} %bitcast.refs_0_._, bf16[1024,256]{1,0:T(8,128)(2,1)S(1)} %get-tuple-element.15.refs_1_, bf16[256,256]{1,0:T(8,128)(2,1)S(1)} %collective-permute-done.4.refs_2_, bf16[128,768]{1,0:T(8,128)(2,1)S(1)} %get-tuple-element.11.refs_1_.refs_3_, ...), custom_call_target="tpu_custom_call" | custom-call | flops 268435456 | bytes 1048576 | tf_op jit(solution)/shard_map/attend/pallas_call | solution.py:77
  90.5 13.2 %collective-permute-done.5.refs_3_ = bf16[3,128,256]{2,1,0:T(8,128)(2,1)S(1)} collective-permute-done((bf16[3,128,256]{2,1,0:T(8,128)(2,1)S(1)}, bf16[3,128,256]{2,1,0:T(8,128)(2,1)S(1)}, u32[]{:S(2)}, u32[]{:S(2)}) %collective-permute-start.5) | collective-permute-done | bytes 196640 | tf_op jit(solution)/shard_map/ppermute | solution.py:264
  103.7 2.5 %attend.3 = bf16[1024,256]{1,0:T(8,128)(2,1)} custom-call(s32[1]{0:T(128)} %bitcast.refs_0_._, bf16[1024,256]{1,0:T(8,128)(2,1)S(1)} %get-tuple-element.15.refs_1_, bf16[256,256]{1,0:T(8,128)(2,1)S(1)} %collective-permute-done.4.refs_2_, bf16[3,128,256]{2,1,0:T(8,128)(2,1)S(1)} %collective-permute-done.5.refs_3_, ...), custom_call_target="tpu_custom_call", output_to_operand_aliasing={{}: (5, {})} | custom-call | flops 268435456 | bytes 1048576 | tf_op jit(solution)/shard_map/attend/pallas_call | solution.py:77
  106.2 0.0 all-to-all-done.2
  106.2 0.1 reduce_sum.19
  106.3 0.6 broadcast_multiply_fusion
  (6 shorter events, 0.1 us)
Async XLA Ops:
  2.5 30.9 %all-to-all-start.1 = ((f32[64,1,2048]{2,1,0:T(1,128)}), f32[64,1,2048]{2,1,0:T(1,128)S(1)}, u32[]{:S(2)}, u32[]{:S(2)}) async-start(f32[64,1,2048]{2,1,0:T(1,128)} %bitcast.14), calls=%async_computation.1 | async-start | bytes 1048576 | tf_op jit(solution)/shard_map/all_to_all | solution.py:269
  13.1 19.3 %copy-start = (bf16[1,128,2048]{2,1,0:T(8,128)(2,1)S(1)}, bf16[1,128,2048]{2,1,0:T(8,128)(2,1)}, u32[]{:S(2)}) copy-start(bf16[1,128,2048]{2,1,0:T(8,128)(2,1)} %param.4) | copy-start | bytes 1572868
  13.1 19.3 %copy-start.1 = (bf16[1,128,512]{2,1,0:T(8,128)(2,1)S(1)}, bf16[1,128,512]{2,1,0:T(8,128)(2,1)}, u32[]{:S(2)}) copy-start(bf16[1,128,512]{2,1,0:T(8,128)(2,1)} %param.5) | copy-start | bytes 393220
  13.1 19.3 %copy-start.2 = (bf16[1,128,512]{2,1,0:T(8,128)(2,1)S(1)}, bf16[1,128,512]{2,1,0:T(8,128)(2,1)}, u32[]{:S(2)}) copy-start(bf16[1,128,512]{2,1,0:T(8,128)(2,1)} %param.6) | copy-start | bytes 393220
  14.8 27.4 %collective-permute-start = (bf16[3,128,256]{2,1,0:T(8,128)(2,1)}, bf16[3,128,256]{2,1,0:T(8,128)(2,1)S(1)}, u32[]{:S(2)}, u32[]{:S(2)}) collective-permute-start(bf16[3,128,256]{2,1,0:T(8,128)(2,1)} %pack_far.1), channel_id=1, source_target_pairs={{0,4},{4,0},{1,5},{5,1},{2,6},{6,2},{3,7},{7,3},{8,12},{12,8},{9,1... | collective-permute-start | bytes 589832 | tf_op jit(solution)/shard_map/ppermute | solution.py:264
  33.4 21.4 %all-to-all-start = ((bf16[4,128,256]{2,1,0:T(8,128)(2,1)}), bf16[4,128,256]{2,1,0:T(8,128)(2,1)S(1)}, u32[]{:S(2)}, u32[]{:S(2)}) async-start(bf16[4,128,256]{2,1,0:T(8,128)(2,1)} %get-tuple-element.17), calls=%async_computation | async-start | bytes 524288 | tf_op jit(solution)/shard_map/all_to_all | solution.py:266
  42.2 43.4 %collective-permute-start.1 = (bf16[128,768]{1,0:T(8,128)(2,1)S(1)}, bf16[128,768]{1,0:T(8,128)(2,1)S(1)}, u32[]{:S(2)}, u32[]{:S(2)}) collective-permute-start(bf16[128,768]{1,0:T(8,128)(2,1)S(1)} %get-tuple-element.12), channel_id=1, source_target_pairs={{0,1},{1,2},{2,3},{3,0},{4,5},{5,6},{6,7},{7,4},{8,9},{9,10},{10,1... | collective-permute-start | bytes 589832 | tf_op jit(solution)/shard_map/ppermute | solution.py:261
  45.7 39.9 %collective-permute-start.2 = (bf16[128,768]{1,0:T(8,128)(2,1)S(1)}, bf16[128,768]{1,0:T(8,128)(2,1)S(1)}, u32[]{:S(2)}, u32[]{:S(2)}) collective-permute-start(bf16[128,768]{1,0:T(8,128)(2,1)S(1)} %get-tuple-element.13), channel_id=1, source_target_pairs={{0,2},{1,3},{2,0},{3,1},{4,6},{5,7},{6,4},{7,5},{8,10},{9,11},{10,... | collective-permute-start | bytes 589832 | tf_op jit(solution)/shard_map/ppermute | solution.py:261
  50.3 35.3 %collective-permute-start.3 = (bf16[128,768]{1,0:T(8,128)(2,1)S(1)}, bf16[128,768]{1,0:T(8,128)(2,1)S(1)}, u32[]{:S(2)}, u32[]{:S(2)}) collective-permute-start(bf16[128,768]{1,0:T(8,128)(2,1)S(1)} %get-tuple-element.14), channel_id=1, source_target_pairs={{0,3},{1,0},{2,1},{3,2},{4,7},{5,4},{6,5},{7,6},{8,11},{9,8},{10,9... | collective-permute-start | bytes 589832 | tf_op jit(solution)/shard_map/ppermute | solution.py:261
  54.8 51.4 %all-to-all-start.2 = ((f32[16,1,1024]{2,1,0:T(1,128)}), f32[16,1,1024]{2,1,0:T(1,128)S(1)}, u32[]{:S(2)}, u32[]{:S(2)}) async-start(f32[16,1,1024]{2,1,0:T(1,128)} %broadcast_in_dim.15), calls=%async_computation.2 | async-start | bytes 131072 | tf_op jit(solution)/shard_map/all_to_all | solution.py:280
  75.3 28.4 %collective-permute-start.5 = (bf16[3,128,256]{2,1,0:T(8,128)(2,1)S(1)}, bf16[3,128,256]{2,1,0:T(8,128)(2,1)S(1)}, u32[]{:S(2)}, u32[]{:S(2)}) collective-permute-start(bf16[3,128,256]{2,1,0:T(8,128)(2,1)S(1)} %stack.1), channel_id=1, source_target_pairs={{0,4},{4,0},{1,5},{5,1},{2,6},{6,2},{3,7},{7,3},{8,12},{12,8},{9,1... | collective-permute-start | bytes 589832 | tf_op jit(solution)/shard_map/ppermute | solution.py:264
  85.7 2.3 %collective-permute-start.4 = (bf16[256,256]{1,0:T(8,128)(2,1)S(1)}, bf16[256,256]{1,0:T(8,128)(2,1)S(1)}, u32[]{:S(2)}, u32[]{:S(2)}) collective-permute-start(bf16[256,256]{1,0:T(8,128)(2,1)S(1)} %get-tuple-element.16), channel_id=1, source_target_pairs={{0,8},{8,16},{16,24},{24,32},{32,40},{40,48},{48,56},{56,64},{64,7... | collective-permute-start | bytes 393224 | tf_op jit(solution)/shard_map/ppermute | solution.py:275

commit v7 on v4

--- a/solution.py
+++ b/solution.py
@@ -83,6 +83,7 @@
         (jax.ShapeDtypeStruct((n // 2 + 1, k.shape[0], 2 * DH), k.dtype),),
         (at, q, k, v),
         "pack_far",
+        limit=60 << 20,
         scratch=(pltpu.SemaphoreType.DMA((n + 1,)),),
         in_specs=[pl.BlockSpec(memory_space=pltpu.SMEM)] + [pl.BlockSpec(memory_space=pl.ANY)] * 3,
     )[0]
@@ -133,6 +134,25 @@
 def cut(at, kv, n):
     outs = (jax.ShapeDtypeStruct(kv.shape[1:], kv.dtype),) * n
     return kernel_call(lambda *refs: cut_kernel(n, *refs), outs, (at, kv), "cut")
+
+
+def share_kernel(copies, parts_ref, to):
+    total = jnp.sum(parts_ref[...], axis=0)
+    chunk = to.shape[-1]
+    for i in range(to.shape[0]):
+        z = i % (to.shape[0] // copies)
+        to[i] = total[:, z * chunk : (z + 1) * chunk]
+
+
+def shared(parts, dp, z):
+    chunk = parts.shape[-1] // z
+    return kernel_call(
+        lambda *refs: share_kernel(dp, *refs),
+        (jax.ShapeDtypeStruct((dp * z, 1, chunk), parts.dtype),),
+        (parts,),
+        "share",
+        in_specs=[pl.BlockSpec(memory_space=pltpu.VMEM)],
+    )[0]
 
 
 def gather_kernel(n, at_ref, *refs):
@@ -267,8 +287,7 @@
     prior = lax.ppermute(last, BLK, [(i, i + 1) for i in range(y * c - 1)])
     rows = attended_half(at, kv, prior, near, n, wide)
 
-    share = jnp.sum(parts, axis=0).reshape(z, 1, -1)
-    share = jnp.broadcast_to(share[None], (dp, *share.shape)).reshape(dp * z, 1, -1)
+    share = shared(parts, dp, z)
     share = lax.all_to_all(share, ("dp", "aa_0"), 0, 0, tiled=True)
     grad_mean = jnp.sum(share, axis=(0, 1)) / (dp * y * c * z * n)
 

time: 109 us -> 110 us (level)
  Pallas kernels: 6.44 us -> 8.85 us
    pallas_call x7 -> x8, Pallas kernels: 6.44 us -> 8.85 us  [kernel_call(): return pl.pallas_call(body, **settings)(*ins)]
    unnamed x14 -> x8, local copies, waits for them, and re-layouts: 3.9 us -> 3.89 us
  transfers between devices with their start and end apart: 11 -> 11, of which waited for: 2 -> 2; matrix products, arithmetic and copies ran while one was open for 1% -> 0% of each run, Pallas kernels for 5% -> 7%
where the time goes in v7:
time: 110 us
  starting transfers between devices  81.5 us (74%)
  waiting for transfers between devices  14.1 us (13%)
  Pallas kernels  8.85 us (8%)
  local copies, waits for them, and re-layouts  3.89 us (4%)
    ppermute x2, starting transfers between devices, across_z(): return lax.ppermute(value, 'aa_0', [(s, 1 - s) for s in range(z)])  27.8 us
    ppermute x6, starting transfers between devices, along_x(): return lax.ppermute(value, 'aa_1', [(x, (x + hop) % n) for x in range(n)])  21.2 us
    all_to_all x1, starting transfers between devices, step(): share = lax.all_to_all(share, ('dp', 'aa_0'), 0, 0, tiled=True)  20.5 us
    ppermute x2, waiting for transfers between devices, across_z(): return lax.ppermute(value, 'aa_0', [(s, 1 - s) for s in range(z)])  13.1 us
    all_to_all x1, starting transfers between devices, step(): parts = lax.all_to_all(parts, ('blk_0', 'blk_1', 'aa_1'), 0, 0, tiled=True)  10.6 us
    pallas_call x8, Pallas kernels, kernel_call(): return pl.pallas_call(body, **settings)(*ins)  8.85 us
    unnamed x8, local copies, waits for them, and re-layouts  3.89 us
  transfers between devices with their start and end apart: 11, of which 2 were waited for; matrix products, arithmetic and copies ran while one was open for 0% of the time, Pallas kernels for 7%

profile of v7, /device:TPU:128, one launch (start us, length us, event | category | flops | bytes accessed | tf_op | source)
XLA Modules:
  0.0 109.8 jit_solution(8606272490576376223)
XLA Ops:
  0.6 0.0 copy-start
  0.6 1.0 copy-done
  1.7 1.0 copy-done.1
  2.7 0.9 copy-done.2
  3.6 0.9 copy-done.3
  4.5 1.1 %pack.1 = (bf16[128,512]{1,0:T(8,128)(2,1)S(1)}, bf16[128,768]{1,0:T(8,128)(2,1)S(1)}, bf16[128,768]{1,0:T(8,128)(2,1)S(1)}, bf16[128,768]{1,0:T(8,128)(2,1)S(1)}, f32[16,4,1,2048]{3,2,1,0:T(1,128)}) custom-call(s32[1]{0:T(128)} %bitcast.refs_0_, bf16[128,2048]{1,0:T(8,128)(2,1)S(1)} %bitcast.8, bf16[128,512]{1,0:T(8,128)(2,1)S(1)} %bitcast.11, ...), custom_call_target="tpu_custom_call" | custom-call | tf_op jit(solution)/shard_map/pack/pallas_call | solution.py:77
  5.7 10.6 %all-to-all-start = ((f32[64,1,2048]{2,1,0:T(1,128)}), f32[64,1,2048]{2,1,0:T(1,128)S(1)}, u32[]{:S(2)}, u32[]{:S(2)}) async-start(f32[64,1,2048]{2,1,0:T(1,128)} %bitcast.6), calls=%async_computation | async-start | bytes 1048576 | tf_op jit(solution)/shard_map/all_to_all | solution.py:281
  16.3 1.6 %pack_far.1 = bf16[3,128,256]{2,1,0:T(8,128)(2,1)} custom-call(s32[1]{0:T(128)} %bitcast.refs_0_, bf16[128,2048]{1,0:T(8,128)(2,1)} %bitcast.7, bf16[128,512]{1,0:T(8,128)(2,1)} %bitcast.10, bf16[128,512]{1,0:T(8,128)(2,1)} %bitcast.12), custom_call_target="tpu_custom_call" | custom-call | tf_op jit(solution)/shard_map/pack_far/pallas_call | solution.py:77
  17.9 17.6 %collective-permute-start.3 = (bf16[3,128,256]{2,1,0:T(8,128)(2,1)}, bf16[3,128,256]{2,1,0:T(8,128)(2,1)S(1)}, u32[]{:S(2)}, u32[]{:S(2)}) collective-permute-start(bf16[3,128,256]{2,1,0:T(8,128)(2,1)} %pack_far.1), channel_id=1, source_target_pairs={{0,4},{4,0},{1,5},{5,1},{2,6},{6,2},{3,7},{7,3},{8,12},{12,8},{9,1... | collective-permute-start | bytes 589832 | tf_op jit(solution)/shard_map/ppermute | solution.py:276
  35.4 3.5 %collective-permute-start = (bf16[128,768]{1,0:T(8,128)(2,1)S(1)}, bf16[128,768]{1,0:T(8,128)(2,1)S(1)}, u32[]{:S(2)}, u32[]{:S(2)}) collective-permute-start(bf16[128,768]{1,0:T(8,128)(2,1)S(1)} %get-tuple-element.14), channel_id=1, source_target_pairs={{0,1},{1,2},{2,3},{3,0},{4,5},{5,6},{6,7},{7,4},{8,9},{9,10},{10,1... | collective-permute-start | bytes 589832 | tf_op jit(solution)/shard_map/ppermute | solution.py:273
  38.9 4.6 %collective-permute-start.1 = (bf16[128,768]{1,0:T(8,128)(2,1)S(1)}, bf16[128,768]{1,0:T(8,128)(2,1)S(1)}, u32[]{:S(2)}, u32[]{:S(2)}) collective-permute-start(bf16[128,768]{1,0:T(8,128)(2,1)S(1)} %get-tuple-element.15), channel_id=1, source_target_pairs={{0,2},{1,3},{2,0},{3,1},{4,6},{5,7},{6,4},{7,5},{8,10},{9,11},{10,... | collective-permute-start | bytes 589832 | tf_op jit(solution)/shard_map/ppermute | solution.py:273
  43.5 3.4 %collective-permute-start.2 = (bf16[128,768]{1,0:T(8,128)(2,1)S(1)}, bf16[128,768]{1,0:T(8,128)(2,1)S(1)}, u32[]{:S(2)}, u32[]{:S(2)}) collective-permute-start(bf16[128,768]{1,0:T(8,128)(2,1)S(1)} %get-tuple-element.16), channel_id=1, source_target_pairs={{0,3},{1,0},{2,1},{3,2},{4,7},{5,4},{6,5},{7,6},{8,11},{9,8},{10,9... | collective-permute-start | bytes 589832 | tf_op jit(solution)/shard_map/ppermute | solution.py:273
  46.9 0.0 collective-permute-done.3.refs_1_.refs_4_
  46.9 2.5 %collective-permute-start.4 = (bf16[128,256]{1,0:T(8,128)(2,1)S(1)}, bf16[128,256]{1,0:T(8,128)(2,1)S(1)}, u32[]{:S(2)}, u32[]{:S(2)}) collective-permute-start(bf16[128,256]{1,0:T(8,128)(2,1)S(1)} %get-tuple-element.18), channel_id=1, source_target_pairs={{0,1},{1,2},{2,3},{3,0},{4,5},{5,6},{6,7},{7,4},{8,9},{9,10},{10,1... | collective-permute-start | bytes 196616 | tf_op jit(solution)/shard_map/ppermute | solution.py:273
  49.4 3.9 %collective-permute-start.5 = (bf16[128,256]{1,0:T(8,128)(2,1)S(1)}, bf16[128,256]{1,0:T(8,128)(2,1)S(1)}, u32[]{:S(2)}, u32[]{:S(2)}) collective-permute-start(bf16[128,256]{1,0:T(8,128)(2,1)S(1)} %get-tuple-element.19), channel_id=1, source_target_pairs={{0,2},{1,3},{2,0},{3,1},{4,6},{5,7},{6,4},{7,5},{8,10},{9,11},{10,... | collective-permute-start | bytes 196616 | tf_op jit(solution)/shard_map/ppermute | solution.py:273
  53.4 0.0 collective-permute-done.refs_2_.refs_0_.refs_4_
  53.4 3.4 %collective-permute-start.6 = (bf16[128,256]{1,0:T(8,128)(2,1)S(1)}, bf16[128,256]{1,0:T(8,128)(2,1)S(1)}, u32[]{:S(2)}, u32[]{:S(2)}) collective-permute-start(bf16[128,256]{1,0:T(8,128)(2,1)S(1)} %get-tuple-element.20), channel_id=1, source_target_pairs={{0,3},{1,0},{2,1},{3,2},{4,7},{5,4},{6,5},{7,6},{8,11},{9,8},{10,9... | collective-permute-start | bytes 196616 | tf_op jit(solution)/shard_map/ppermute | solution.py:273
  56.8 0.0 all-to-all-done.refs_0_
  56.8 0.9 share.1
  57.7 20.5 %all-to-all-start.1 = ((f32[16,1,1024]{2,1,0:T(1,128)}), f32[16,1,1024]{2,1,0:T(1,128)S(1)}, u32[]{:S(2)}, u32[]{:S(2)}) async-start(f32[16,1,1024]{2,1,0:T(1,128)} %share.1), calls=%async_computation.1 | async-start | bytes 131072 | tf_op jit(solution)/shard_map/all_to_all | solution.py:291
  78.2 0.0 collective-permute-done.1.refs_3_.refs_1_.refs_5_
  78.3 10.3 %collective-permute-start.8 = (bf16[3,128,256]{2,1,0:T(8,128)(2,1)S(1)}, bf16[3,128,256]{2,1,0:T(8,128)(2,1)S(1)}, u32[]{:S(2)}, u32[]{:S(2)}) collective-permute-start(bf16[3,128,256]{2,1,0:T(8,128)(2,1)S(1)} %stack.1), channel_id=1, source_target_pairs={{0,4},{4,0},{1,5},{5,1},{2,6},{6,2},{3,7},{7,3},{8,12},{12,8},{9,1... | collective-permute-start | bytes 589832 | tf_op jit(solution)/shard_map/ppermute | solution.py:276
  88.6 0.0 collective-permute-done.4.refs_6_
  88.6 0.0 collective-permute-done.5.refs_7_
  88.6 0.1 gather.1
  88.7 1.3 %collective-permute-start.7 = (bf16[256,256]{1,0:T(8,128)(2,1)S(1)}, bf16[256,256]{1,0:T(8,128)(2,1)S(1)}, u32[]{:S(2)}, u32[]{:S(2)}) collective-permute-start(bf16[256,256]{1,0:T(8,128)(2,1)S(1)} %get-tuple-element.22), channel_id=1, source_target_pairs={{0,8},{8,16},{16,24},{24,32},{32,40},{40,48},{48,56},{56,64},{64,7... | collective-permute-start | bytes 393224 | tf_op jit(solution)/shard_map/ppermute | solution.py:287
  90.0 1.0 collective-permute-done.7.refs_2_
  90.9 2.5 %attend.2.refs_5_ = bf16[1024,256]{1,0:T(8,128)(2,1)} custom-call(s32[1]{0:T(128)} %bitcast.refs_0_, bf16[1024,256]{1,0:T(8,128)(2,1)S(1)} %get-tuple-element.21.refs_1_, bf16[256,256]{1,0:T(8,128)(2,1)S(1)} %collective-permute-done.7.refs_2_, bf16[128,512]{1,0:T(8,128)(2,1)S(1)} %get-tuple-element.13.refs_1_.refs_3_, ...), custom_call_target="tpu_custom_call" | custom-call | flops 268435456 | bytes 1048576 | tf_op jit(solution)/shard_map/attend/pallas_call | solution.py:77
  93.5 13.1 %collective-permute-done.8.refs_3_ = bf16[3,128,256]{2,1,0:T(8,128)(2,1)S(1)} collective-permute-done((bf16[3,128,256]{2,1,0:T(8,128)(2,1)S(1)}, bf16[3,128,256]{2,1,0:T(8,128)(2,1)S(1)}, u32[]{:S(2)}, u32[]{:S(2)}) %collective-permute-start.8) | collective-permute-done | bytes 196640 | tf_op jit(solution)/shard_map/ppermute | solution.py:276
  106.6 2.5 %attend.3 = bf16[1024,256]{1,0:T(8,128)(2,1)} custom-call(s32[1]{0:T(128)} %bitcast.refs_0_, bf16[1024,256]{1,0:T(8,128)(2,1)S(1)} %get-tuple-element.21.refs_1_, bf16[256,256]{1,0:T(8,128)(2,1)S(1)} %collective-permute-done.7.refs_2_, bf16[3,128,256]{2,1,0:T(8,128)(2,1)S(1)} %collective-permute-done.8.refs_3_, ...), custom_call_target="tpu_custom_call", output_to_operand_aliasing={{}: (5, {})} | custom-call | flops 268435456 | bytes 1048576 | tf_op jit(solution)/shard_map/attend/pallas_call | solution.py:77
  109.2 0.1 reduce_sum.9
  109.2 0.6 broadcast_multiply_fusion
  (8 shorter events, 0.1 us)
Async XLA Ops:
  0.6 1.0 copy-start
  1.7 1.0 copy-start.1
  2.7 0.9 copy-start.2
  3.6 0.9 copy-start.3
  5.7 51.1 %all-to-all-start = ((f32[64,1,2048]{2,1,0:T(1,128)}), f32[64,1,2048]{2,1,0:T(1,128)S(1)}, u32[]{:S(2)}, u32[]{:S(2)}) async-start(f32[64,1,2048]{2,1,0:T(1,128)} %bitcast.6), calls=%async_computation | async-start | bytes 1048576 | tf_op jit(solution)/shard_map/all_to_all | solution.py:281
  17.9 29.0 %collective-permute-start.3 = (bf16[3,128,256]{2,1,0:T(8,128)(2,1)}, bf16[3,128,256]{2,1,0:T(8,128)(2,1)S(1)}, u32[]{:S(2)}, u32[]{:S(2)}) collective-permute-start(bf16[3,128,256]{2,1,0:T(8,128)(2,1)} %pack_far.1), channel_id=1, source_target_pairs={{0,4},{4,0},{1,5},{5,1},{2,6},{6,2},{3,7},{7,3},{8,12},{12,8},{9,1... | collective-permute-start | bytes 589832 | tf_op jit(solution)/shard_map/ppermute | solution.py:276
  35.4 17.9 %collective-permute-start = (bf16[128,768]{1,0:T(8,128)(2,1)S(1)}, bf16[128,768]{1,0:T(8,128)(2,1)S(1)}, u32[]{:S(2)}, u32[]{:S(2)}) collective-permute-start(bf16[128,768]{1,0:T(8,128)(2,1)S(1)} %get-tuple-element.14), channel_id=1, source_target_pairs={{0,1},{1,2},{2,3},{3,0},{4,5},{5,6},{6,7},{7,4},{8,9},{9,10},{10,1... | collective-permute-start | bytes 589832 | tf_op jit(solution)/shard_map/ppermute | solution.py:273
  38.9 39.3 %collective-permute-start.1 = (bf16[128,768]{1,0:T(8,128)(2,1)S(1)}, bf16[128,768]{1,0:T(8,128)(2,1)S(1)}, u32[]{:S(2)}, u32[]{:S(2)}) collective-permute-start(bf16[128,768]{1,0:T(8,128)(2,1)S(1)} %get-tuple-element.15), channel_id=1, source_target_pairs={{0,2},{1,3},{2,0},{3,1},{4,6},{5,7},{6,4},{7,5},{8,10},{9,11},{10,... | collective-permute-start | bytes 589832 | tf_op jit(solution)/shard_map/ppermute | solution.py:273
  43.5 34.7 %collective-permute-start.2 = (bf16[128,768]{1,0:T(8,128)(2,1)S(1)}, bf16[128,768]{1,0:T(8,128)(2,1)S(1)}, u32[]{:S(2)}, u32[]{:S(2)}) collective-permute-start(bf16[128,768]{1,0:T(8,128)(2,1)S(1)} %get-tuple-element.16), channel_id=1, source_target_pairs={{0,3},{1,0},{2,1},{3,2},{4,7},{5,4},{6,5},{7,6},{8,11},{9,8},{10,9... | collective-permute-start | bytes 589832 | tf_op jit(solution)/shard_map/ppermute | solution.py:273
  46.9 41.6 %collective-permute-start.4 = (bf16[128,256]{1,0:T(8,128)(2,1)S(1)}, bf16[128,256]{1,0:T(8,128)(2,1)S(1)}, u32[]{:S(2)}, u32[]{:S(2)}) collective-permute-start(bf16[128,256]{1,0:T(8,128)(2,1)S(1)} %get-tuple-element.18), channel_id=1, source_target_pairs={{0,1},{1,2},{2,3},{3,0},{4,5},{5,6},{6,7},{7,4},{8,9},{9,10},{10,1... | collective-permute-start | bytes 196616 | tf_op jit(solution)/shard_map/ppermute | solution.py:273
  49.4 39.2 %collective-permute-start.5 = (bf16[128,256]{1,0:T(8,128)(2,1)S(1)}, bf16[128,256]{1,0:T(8,128)(2,1)S(1)}, u32[]{:S(2)}, u32[]{:S(2)}) collective-permute-start(bf16[128,256]{1,0:T(8,128)(2,1)S(1)} %get-tuple-element.19), channel_id=1, source_target_pairs={{0,2},{1,3},{2,0},{3,1},{4,6},{5,7},{6,4},{7,5},{8,10},{9,11},{10,... | collective-permute-start | bytes 196616 | tf_op jit(solution)/shard_map/ppermute | solution.py:273
  53.4 35.2 %collective-permute-start.6 = (bf16[128,256]{1,0:T(8,128)(2,1)S(1)}, bf16[128,256]{1,0:T(8,128)(2,1)S(1)}, u32[]{:S(2)}, u32[]{:S(2)}) collective-permute-start(bf16[128,256]{1,0:T(8,128)(2,1)S(1)} %get-tuple-element.20), channel_id=1, source_target_pairs={{0,3},{1,0},{2,1},{3,2},{4,7},{5,4},{6,5},{7,6},{8,11},{9,8},{10,9... | collective-permute-start | bytes 196616 | tf_op jit(solution)/shard_map/ppermute | solution.py:273
  57.7 51.4 %all-to-all-start.1 = ((f32[16,1,1024]{2,1,0:T(1,128)}), f32[16,1,1024]{2,1,0:T(1,128)S(1)}, u32[]{:S(2)}, u32[]{:S(2)}) async-start(f32[16,1,1024]{2,1,0:T(1,128)} %share.1), calls=%async_computation.1 | async-start | bytes 131072 | tf_op jit(solution)/shard_map/all_to_all | solution.py:291
  78.3 28.3 %collective-permute-start.8 = (bf16[3,128,256]{2,1,0:T(8,128)(2,1)S(1)}, bf16[3,128,256]{2,1,0:T(8,128)(2,1)S(1)}, u32[]{:S(2)}, u32[]{:S(2)}) collective-permute-start(bf16[3,128,256]{2,1,0:T(8,128)(2,1)S(1)} %stack.1), channel_id=1, source_target_pairs={{0,4},{4,0},{1,5},{5,1},{2,6},{6,2},{3,7},{7,3},{8,12},{12,8},{9,1... | collective-permute-start | bytes 589832 | tf_op jit(solution)/shard_map/ppermute | solution.py:276
  88.7 2.3 %collective-permute-start.7 = (bf16[256,256]{1,0:T(8,128)(2,1)S(1)}, bf16[256,256]{1,0:T(8,128)(2,1)S(1)}, u32[]{:S(2)}, u32[]{:S(2)}) collective-permute-start(bf16[256,256]{1,0:T(8,128)(2,1)S(1)} %get-tuple-element.22), channel_id=1, source_target_pairs={{0,8},{8,16},{16,24},{24,32},{32,40},{40,48},{48,56},{56,64},{64,7... | collective-permute-start | bytes 393224 | tf_op jit(solution)/shard_map/ppermute | solution.py:287

commit v8 on v7

--- a/solution.py
+++ b/solution.py
@@ -44,14 +44,17 @@
     run_all(moves, sems)
 
 
-def pack_kernel(n, at_ref, q_ref, k_ref, v_ref, g_ref, *refs):
-    to, g_to, sems = refs[:n], refs[n], refs[n + 1]
+def pack_parts_kernel(g_ref, g_to, sems):
+    chunk = g_ref.shape[-1]
+    moves = [(g_ref.at[:, z], g_to.at[:, :, :, z * chunk : (z + 1) * chunk]) for z in range(g_ref.shape[1])]
+    run_all(moves, sems)
+
+
+def pack_kernel(n, at_ref, q_ref, k_ref, v_ref, *refs):
+    to, sems = refs[:n], refs[n]
     side, x = place(at_ref, n)
     wide = q_ref.shape[1] // (2 * n)
     moves = []
-    chunk = g_ref.shape[-1]
-    for z in range(g_ref.shape[1]):
-        moves.append((g_ref.at[:, z], g_to.at[:, :, :, z * chunk : (z + 1) * chunk]))
     for hop in range(n):
         target = lax.rem(x + hop, n)
         head = side * (n // 2) + lax.div(target, 2)
@@ -89,23 +92,32 @@
     )[0]
 
 
-def packed(at, q, k, v, g, n):
+def packed(at, q, k, v, n):
     rows, wide = q.shape[0], q.shape[1] // (2 * n)
-    yc, z, x, _, chunk = g.shape
     outs = (
         jax.ShapeDtypeStruct((rows, wide + 2 * DH), q.dtype),
         *(jax.ShapeDtypeStruct((rows, 2 * wide + 2 * DH), q.dtype),) * (n - 1),
-        jax.ShapeDtypeStruct((yc, x, 1, z * chunk), g.dtype),
-    )
-    found = kernel_call(
+    )
+    return kernel_call(
         lambda *refs: pack_kernel(n, *refs),
         outs,
-        (at, q, k, v, g),
+        (at, q, k, v),
         "pack",
-        scratch=(pltpu.SemaphoreType.DMA((4 * n - 1 + z,)),),
-        in_specs=[pl.BlockSpec(memory_space=pltpu.SMEM)] + [pl.BlockSpec(memory_space=pl.ANY)] * 4,
-    )
-    return found[:n], found[-1]
+        scratch=(pltpu.SemaphoreType.DMA((4 * n - 1,)),),
+        in_specs=[pl.BlockSpec(memory_space=pltpu.SMEM)] + [pl.BlockSpec(memory_space=pl.ANY)] * 3,
+    )
+
+
+def packed_parts(g):
+    yc, z, x, _, chunk = g.shape
+    return kernel_call(
+        pack_parts_kernel,
+        (jax.ShapeDtypeStruct((yc, x, 1, z * chunk), g.dtype),),
+        (g,),
+        "pack_parts",
+        scratch=(pltpu.SemaphoreType.DMA((z,)),),
+        in_specs=[pl.BlockSpec(memory_space=pl.ANY)],
+    )[0]
 
 
 def stack_kernel(n, *refs):
@@ -153,6 +165,20 @@
         "share",
         in_specs=[pl.BlockSpec(memory_space=pltpu.VMEM)],
     )[0]
+
+
+def mean_kernel(count, share_ref, to):
+    to[...] = jnp.sum(share_ref[...], axis=0) / count
+
+
+def averaged(share, count):
+    return kernel_call(
+        lambda *refs: mean_kernel(count, *refs),
+        (jax.ShapeDtypeStruct(share.shape[1:], share.dtype),),
+        (share,),
+        "mean",
+        in_specs=[pl.BlockSpec(memory_space=pltpu.VMEM)],
+    )[0].reshape(-1)
 
 
 def gather_kernel(n, at_ref, *refs):
@@ -267,7 +293,8 @@
     reach = queries.shape[1] * 2
     chunks = grad_parts.reshape(y * c, z, n, 1, -1)
     kv_far = packed_far(at, queries[0], keys[0], values[0], n)
-    sent, parts = packed(at, queries[0], keys[0], values[0], chunks, n)
+    sent = packed(at, queries[0], keys[0], values[0], n)
+    parts = packed_parts(chunks)
 
     def along_x(value, hop):
         return lax.ppermute(value, "aa_1", [(x, (x + hop) % n) for x in range(n)])
@@ -289,7 +316,7 @@
 
     share = shared(parts, dp, z)
     share = lax.all_to_all(share, ("dp", "aa_0"), 0, 0, tiled=True)
-    grad_mean = jnp.sum(share, axis=(0, 1)) / (dp * y * c * z * n)
+    grad_mean = averaged(share, dp * y * c * z * n)
 
     rows = attended_half(at, kv, prior, (q_far, kv_far), n, wide, rows)
     return rows[None], grad_mean

time: 110 us -> 107 us (0.973)
  local copies, waits for them, and re-layouts: 3.89 us -> 1.05 us
    unnamed x8, local copies, waits for them, and re-layouts: 3.89 us -> 1.05 us
    pallas_call x8 -> x10, Pallas kernels: 8.85 us -> 9.56 us  [kernel_call(): return pl.pallas_call(body, **settings)(*ins)]
  transfers between devices with their start and end apart: 11 -> 11, of which waited for: 2 -> 2; matrix products, arithmetic and copies ran while one was open for 0% -> 0% of each run, Pallas kernels for 7% -> 8%
where the time goes in v8:
time: 107 us
  starting transfers between devices  81.1 us (76%)
  waiting for transfers between devices  14.1 us (13%)
  Pallas kernels  9.56 us (9%)
    ppermute x2, starting transfers between devices, across_z(): return lax.ppermute(value, 'aa_0', [(s, 1 - s) for s in range(z)])  27.8 us
    ppermute x6, starting transfers between devices, along_x(): return lax.ppermute(value, 'aa_1', [(x, (x + hop) % n) for x in range(n)])  20.9 us
    all_to_all x1, starting transfers between devices, step(): share = lax.all_to_all(share, ('dp', 'aa_0'), 0, 0, tiled=True)  20.5 us
    ppermute x2, waiting for transfers between devices, across_z(): return lax.ppermute(value, 'aa_0', [(s, 1 - s) for s in range(z)])  13.1 us
    all_to_all x1, starting transfers between devices, step(): parts = lax.all_to_all(parts, ('blk_0', 'blk_1', 'aa_1'), 0, 0, tiled=True)  10.6 us
    pallas_call x10, Pallas kernels, kernel_call(): return pl.pallas_call(body, **settings)(*ins)  9.56 us
  transfers between devices with their start and end apart: 11, of which 2 were waited for; matrix products, arithmetic and copies ran while one was open for 0% of the time, Pallas kernels for 8%

profile of v8, /device:TPU:128, one launch (start us, length us, event | category | flops | bytes accessed | tf_op | source)
XLA Modules:
  0.0 106.7 jit_solution(2363350303220953153)
XLA Ops:
  0.6 1.0 copy-done.1
  1.7 0.8 pack_parts.1
  2.5 10.6 %all-to-all-start = ((f32[64,1,2048]{2,1,0:T(1,128)}), f32[64,1,2048]{2,1,0:T(1,128)S(1)}, u32[]{:S(2)}, u32[]{:S(2)}) async-start(f32[64,1,2048]{2,1,0:T(1,128)} %bitcast.6), calls=%async_computation | async-start | bytes 1048576 | tf_op jit(solution)/shard_map/all_to_all | solution.py:308
  13.1 0.0 copy-start
  13.1 0.0 copy-start.2
  13.2 0.0 copy-start.3
  13.2 1.6 %pack_far.1 = bf16[3,128,256]{2,1,0:T(8,128)(2,1)} custom-call(s32[1]{0:T(128)} %bitcast.refs_0_, bf16[128,2048]{1,0:T(8,128)(2,1)} %bitcast.8, bf16[128,512]{1,0:T(8,128)(2,1)} %bitcast.11, bf16[128,512]{1,0:T(8,128)(2,1)} %bitcast.13), custom_call_target="tpu_custom_call" | custom-call | tf_op jit(solution)/shard_map/pack_far/pallas_call | solution.py:80
  14.8 17.6 %collective-permute-start.3 = (bf16[3,128,256]{2,1,0:T(8,128)(2,1)}, bf16[3,128,256]{2,1,0:T(8,128)(2,1)S(1)}, u32[]{:S(2)}, u32[]{:S(2)}) collective-permute-start(bf16[3,128,256]{2,1,0:T(8,128)(2,1)} %pack_far.1), channel_id=1, source_target_pairs={{0,4},{4,0},{1,5},{5,1},{2,6},{6,2},{3,7},{7,3},{8,12},{12,8},{9,1... | collective-permute-start | bytes 589832 | tf_op jit(solution)/shard_map/ppermute | solution.py:303
  32.4 0.3 pack.1
  32.7 3.5 %collective-permute-start = (bf16[128,768]{1,0:T(8,128)(2,1)S(1)}, bf16[128,768]{1,0:T(8,128)(2,1)S(1)}, u32[]{:S(2)}, u32[]{:S(2)}) collective-permute-start(bf16[128,768]{1,0:T(8,128)(2,1)S(1)} %get-tuple-element.13), channel_id=1, source_target_pairs={{0,1},{1,2},{2,3},{3,0},{4,5},{5,6},{6,7},{7,4},{8,9},{9,10},{10,1... | collective-permute-start | bytes 589832 | tf_op jit(solution)/shard_map/ppermute | solution.py:300
  36.2 4.6 %collective-permute-start.1 = (bf16[128,768]{1,0:T(8,128)(2,1)S(1)}, bf16[128,768]{1,0:T(8,128)(2,1)S(1)}, u32[]{:S(2)}, u32[]{:S(2)}) collective-permute-start(bf16[128,768]{1,0:T(8,128)(2,1)S(1)} %get-tuple-element.14), channel_id=1, source_target_pairs={{0,2},{1,3},{2,0},{3,1},{4,6},{5,7},{6,4},{7,5},{8,10},{9,11},{10,... | collective-permute-start | bytes 589832 | tf_op jit(solution)/shard_map/ppermute | solution.py:300
  40.8 3.4 %collective-permute-start.2 = (bf16[128,768]{1,0:T(8,128)(2,1)S(1)}, bf16[128,768]{1,0:T(8,128)(2,1)S(1)}, u32[]{:S(2)}, u32[]{:S(2)}) collective-permute-start(bf16[128,768]{1,0:T(8,128)(2,1)S(1)} %get-tuple-element.15), channel_id=1, source_target_pairs={{0,3},{1,0},{2,1},{3,2},{4,7},{5,4},{6,5},{7,6},{8,11},{9,8},{10,9... | collective-permute-start | bytes 589832 | tf_op jit(solution)/shard_map/ppermute | solution.py:300
  44.2 0.0 collective-permute-done.3.refs_1_.refs_4_
  44.2 2.5 %collective-permute-start.4 = (bf16[128,256]{1,0:T(8,128)(2,1)S(1)}, bf16[128,256]{1,0:T(8,128)(2,1)S(1)}, u32[]{:S(2)}, u32[]{:S(2)}) collective-permute-start(bf16[128,256]{1,0:T(8,128)(2,1)S(1)} %get-tuple-element.17), channel_id=1, source_target_pairs={{0,1},{1,2},{2,3},{3,0},{4,5},{5,6},{6,7},{7,4},{8,9},{9,10},{10,1... | collective-permute-start | bytes 196616 | tf_op jit(solution)/shard_map/ppermute | solution.py:300
  46.7 3.6 %collective-permute-start.5 = (bf16[128,256]{1,0:T(8,128)(2,1)S(1)}, bf16[128,256]{1,0:T(8,128)(2,1)S(1)}, u32[]{:S(2)}, u32[]{:S(2)}) collective-permute-start(bf16[128,256]{1,0:T(8,128)(2,1)S(1)} %get-tuple-element.18), channel_id=1, source_target_pairs={{0,2},{1,3},{2,0},{3,1},{4,6},{5,7},{6,4},{7,5},{8,10},{9,11},{10,... | collective-permute-start | bytes 196616 | tf_op jit(solution)/shard_map/ppermute | solution.py:300
  50.3 0.0 collective-permute-done.refs_2_.refs_0_.refs_4_
  50.3 3.4 %collective-permute-start.6 = (bf16[128,256]{1,0:T(8,128)(2,1)S(1)}, bf16[128,256]{1,0:T(8,128)(2,1)S(1)}, u32[]{:S(2)}, u32[]{:S(2)}) collective-permute-start(bf16[128,256]{1,0:T(8,128)(2,1)S(1)} %get-tuple-element.19), channel_id=1, source_target_pairs={{0,3},{1,0},{2,1},{3,2},{4,7},{5,4},{6,5},{7,6},{8,11},{9,8},{10,9... | collective-permute-start | bytes 196616 | tf_op jit(solution)/shard_map/ppermute | solution.py:300
  53.7 0.0 all-to-all-done.refs_0_
  53.7 0.9 share.1
  54.7 20.5 %all-to-all-start.1 = ((f32[16,1,1024]{2,1,0:T(1,128)}), f32[16,1,1024]{2,1,0:T(1,128)S(1)}, u32[]{:S(2)}, u32[]{:S(2)}) async-start(f32[16,1,1024]{2,1,0:T(1,128)} %share.1), calls=%async_computation.1 | async-start | bytes 131072 | tf_op jit(solution)/shard_map/all_to_all | solution.py:318
  75.2 0.0 collective-permute-done.1.refs_3_.refs_1_.refs_5_
  75.2 0.0 collective-permute-done.2.refs_4_.refs_2_.refs_6_
  75.2 10.3 %collective-permute-start.8 = (bf16[3,128,256]{2,1,0:T(8,128)(2,1)S(1)}, bf16[3,128,256]{2,1,0:T(8,128)(2,1)S(1)}, u32[]{:S(2)}, u32[]{:S(2)}) collective-permute-start(bf16[3,128,256]{2,1,0:T(8,128)(2,1)S(1)} %stack.1), channel_id=1, source_target_pairs={{0,4},{4,0},{1,5},{5,1},{2,6},{6,2},{3,7},{7,3},{8,12},{12,8},{9,1... | collective-permute-start | bytes 589832 | tf_op jit(solution)/shard_map/ppermute | solution.py:303
  85.5 0.0 collective-permute-done.4.refs_6_
  85.5 0.1 gather.1
  85.6 1.3 %collective-permute-start.7 = (bf16[256,256]{1,0:T(8,128)(2,1)S(1)}, bf16[256,256]{1,0:T(8,128)(2,1)S(1)}, u32[]{:S(2)}, u32[]{:S(2)}) collective-permute-start(bf16[256,256]{1,0:T(8,128)(2,1)S(1)} %get-tuple-element.21), channel_id=1, source_target_pairs={{0,8},{8,16},{16,24},{24,32},{32,40},{40,48},{48,56},{56,64},{64,7... | collective-permute-start | bytes 393224 | tf_op jit(solution)/shard_map/ppermute | solution.py:314
  86.9 1.0 collective-permute-done.7.refs_2_
  87.9 2.5 %attend.2.refs_5_ = bf16[1024,256]{1,0:T(8,128)(2,1)} custom-call(s32[1]{0:T(128)} %bitcast.refs_0_, bf16[1024,256]{1,0:T(8,128)(2,1)S(1)} %get-tuple-element.20.refs_1_, bf16[256,256]{1,0:T(8,128)(2,1)S(1)} %collective-permute-done.7.refs_2_, bf16[128,512]{1,0:T(8,128)(2,1)S(1)} %get-tuple-element.12.refs_1_.refs_3_, ...), custom_call_target="tpu_custom_call" | custom-call | flops 268435456 | bytes 1048576 | tf_op jit(solution)/shard_map/attend/pallas_call | solution.py:80
  90.4 13.1 %collective-permute-done.8.refs_3_ = bf16[3,128,256]{2,1,0:T(8,128)(2,1)S(1)} collective-permute-done((bf16[3,128,256]{2,1,0:T(8,128)(2,1)S(1)}, bf16[3,128,256]{2,1,0:T(8,128)(2,1)S(1)}, u32[]{:S(2)}, u32[]{:S(2)}) %collective-permute-start.8) | collective-permute-done | bytes 196640 | tf_op jit(solution)/shard_map/ppermute | solution.py:303
  103.5 2.5 %attend.3 = bf16[1024,256]{1,0:T(8,128)(2,1)} custom-call(s32[1]{0:T(128)} %bitcast.refs_0_, bf16[1024,256]{1,0:T(8,128)(2,1)S(1)} %get-tuple-element.20.refs_1_, bf16[256,256]{1,0:T(8,128)(2,1)S(1)} %collective-permute-done.7.refs_2_, bf16[3,128,256]{2,1,0:T(8,128)(2,1)S(1)} %collective-permute-done.8.refs_3_, ...), custom_call_target="tpu_custom_call", output_to_operand_aliasing={{}: (5, {})} | custom-call | flops 268435456 | bytes 1048576 | tf_op jit(solution)/shard_map/attend/pallas_call | solution.py:80
  106.1 0.0 all-to-all-done.1.refs_0_
  106.1 0.6 mean.1
  (8 shorter events, 0.1 us)
Async XLA Ops:
  0.6 1.0 copy-start.1
  2.5 51.2 %all-to-all-start = ((f32[64,1,2048]{2,1,0:T(1,128)}), f32[64,1,2048]{2,1,0:T(1,128)S(1)}, u32[]{:S(2)}, u32[]{:S(2)}) async-start(f32[64,1,2048]{2,1,0:T(1,128)} %bitcast.6), calls=%async_computation | async-start | bytes 1048576 | tf_op jit(solution)/shard_map/all_to_all | solution.py:308
  13.1 19.3 %copy-start = (bf16[1,128,2048]{2,1,0:T(8,128)(2,1)S(1)}, bf16[1,128,2048]{2,1,0:T(8,128)(2,1)}, u32[]{:S(2)}) copy-start(bf16[1,128,2048]{2,1,0:T(8,128)(2,1)} %param.4) | copy-start | bytes 1572868
  13.1 19.2 %copy-start.2 = (bf16[1,128,512]{2,1,0:T(8,128)(2,1)S(1)}, bf16[1,128,512]{2,1,0:T(8,128)(2,1)}, u32[]{:S(2)}) copy-start(bf16[1,128,512]{2,1,0:T(8,128)(2,1)} %param.5) | copy-start | bytes 393220
  13.2 19.2 %copy-start.3 = (bf16[1,128,512]{2,1,0:T(8,128)(2,1)S(1)}, bf16[1,128,512]{2,1,0:T(8,128)(2,1)}, u32[]{:S(2)}) copy-start(bf16[1,128,512]{2,1,0:T(8,128)(2,1)} %param.6) | copy-start | bytes 393220
  14.8 29.4 %collective-permute-start.3 = (bf16[3,128,256]{2,1,0:T(8,128)(2,1)}, bf16[3,128,256]{2,1,0:T(8,128)(2,1)S(1)}, u32[]{:S(2)}, u32[]{:S(2)}) collective-permute-start(bf16[3,128,256]{2,1,0:T(8,128)(2,1)} %pack_far.1), channel_id=1, source_target_pairs={{0,4},{4,0},{1,5},{5,1},{2,6},{6,2},{3,7},{7,3},{8,12},{12,8},{9,1... | collective-permute-start | bytes 589832 | tf_op jit(solution)/shard_map/ppermute | solution.py:303
  32.7 17.6 %collective-permute-start = (bf16[128,768]{1,0:T(8,128)(2,1)S(1)}, bf16[128,768]{1,0:T(8,128)(2,1)S(1)}, u32[]{:S(2)}, u32[]{:S(2)}) collective-permute-start(bf16[128,768]{1,0:T(8,128)(2,1)S(1)} %get-tuple-element.13), channel_id=1, source_target_pairs={{0,1},{1,2},{2,3},{3,0},{4,5},{5,6},{6,7},{7,4},{8,9},{9,10},{10,1... | collective-permute-start | bytes 589832 | tf_op jit(solution)/shard_map/ppermute | solution.py:300
  36.2 38.9 %collective-permute-start.1 = (bf16[128,768]{1,0:T(8,128)(2,1)S(1)}, bf16[128,768]{1,0:T(8,128)(2,1)S(1)}, u32[]{:S(2)}, u32[]{:S(2)}) collective-permute-start(bf16[128,768]{1,0:T(8,128)(2,1)S(1)} %get-tuple-element.14), channel_id=1, source_target_pairs={{0,2},{1,3},{2,0},{3,1},{4,6},{5,7},{6,4},{7,5},{8,10},{9,11},{10,... | collective-permute-start | bytes 589832 | tf_op jit(solution)/shard_map/ppermute | solution.py:300
  40.8 34.4 %collective-permute-start.2 = (bf16[128,768]{1,0:T(8,128)(2,1)S(1)}, bf16[128,768]{1,0:T(8,128)(2,1)S(1)}, u32[]{:S(2)}, u32[]{:S(2)}) collective-permute-start(bf16[128,768]{1,0:T(8,128)(2,1)S(1)} %get-tuple-element.15), channel_id=1, source_target_pairs={{0,3},{1,0},{2,1},{3,2},{4,7},{5,4},{6,5},{7,6},{8,11},{9,8},{10,9... | collective-permute-start | bytes 589832 | tf_op jit(solution)/shard_map/ppermute | solution.py:300
  44.2 41.3 %collective-permute-start.4 = (bf16[128,256]{1,0:T(8,128)(2,1)S(1)}, bf16[128,256]{1,0:T(8,128)(2,1)S(1)}, u32[]{:S(2)}, u32[]{:S(2)}) collective-permute-start(bf16[128,256]{1,0:T(8,128)(2,1)S(1)} %get-tuple-element.17), channel_id=1, source_target_pairs={{0,1},{1,2},{2,3},{3,0},{4,5},{5,6},{6,7},{7,4},{8,9},{9,10},{10,1... | collective-permute-start | bytes 196616 | tf_op jit(solution)/shard_map/ppermute | solution.py:300
  46.7 38.8 %collective-permute-start.5 = (bf16[128,256]{1,0:T(8,128)(2,1)S(1)}, bf16[128,256]{1,0:T(8,128)(2,1)S(1)}, u32[]{:S(2)}, u32[]{:S(2)}) collective-permute-start(bf16[128,256]{1,0:T(8,128)(2,1)S(1)} %get-tuple-element.18), channel_id=1, source_target_pairs={{0,2},{1,3},{2,0},{3,1},{4,6},{5,7},{6,4},{7,5},{8,10},{9,11},{10,... | collective-permute-start | bytes 196616 | tf_op jit(solution)/shard_map/ppermute | solution.py:300
  50.3 35.2 %collective-permute-start.6 = (bf16[128,256]{1,0:T(8,128)(2,1)S(1)}, bf16[128,256]{1,0:T(8,128)(2,1)S(1)}, u32[]{:S(2)}, u32[]{:S(2)}) collective-permute-start(bf16[128,256]{1,0:T(8,128)(2,1)S(1)} %get-tuple-element.19), channel_id=1, source_target_pairs={{0,3},{1,0},{2,1},{3,2},{4,7},{5,4},{6,5},{7,6},{8,11},{9,8},{10,9... | collective-permute-start | bytes 196616 | tf_op jit(solution)/shard_map/ppermute | solution.py:300
  54.7 51.4 %all-to-all-start.1 = ((f32[16,1,1024]{2,1,0:T(1,128)}), f32[16,1,1024]{2,1,0:T(1,128)S(1)}, u32[]{:S(2)}, u32[]{:S(2)}) async-start(f32[16,1,1024]{2,1,0:T(1,128)} %share.1), calls=%async_computation.1 | async-start | bytes 131072 | tf_op jit(solution)/shard_map/all_to_all | solution.py:318
  75.2 28.3 %collective-permute-start.8 = (bf16[3,128,256]{2,1,0:T(8,128)(2,1)S(1)}, bf16[3,128,256]{2,1,0:T(8,128)(2,1)S(1)}, u32[]{:S(2)}, u32[]{:S(2)}) collective-permute-start(bf16[3,128,256]{2,1,0:T(8,128)(2,1)S(1)} %stack.1), channel_id=1, source_target_pairs={{0,4},{4,0},{1,5},{5,1},{2,6},{6,2},{3,7},{7,3},{8,12},{12,8},{9,1... | collective-permute-start | bytes 589832 | tf_op jit(solution)/shard_map/ppermute | solution.py:303
  85.6 2.3 %collective-permute-start.7 = (bf16[256,256]{1,0:T(8,128)(2,1)S(1)}, bf16[256,256]{1,0:T(8,128)(2,1)S(1)}, u32[]{:S(2)}, u32[]{:S(2)}) collective-permute-start(bf16[256,256]{1,0:T(8,128)(2,1)S(1)} %get-tuple-element.21), channel_id=1, source_target_pairs={{0,8},{8,16},{16,24},{24,32},{32,40},{40,48},{48,56},{56,64},{64,7... | collective-permute-start | bytes 393224 | tf_op jit(solution)/shard_map/ppermute | solution.py:314

commit v9 on v8

--- a/solution.py
+++ b/solution.py
@@ -44,10 +44,24 @@
     run_all(moves, sems)
 
 
-def pack_parts_kernel(g_ref, g_to, sems):
-    chunk = g_ref.shape[-1]
-    moves = [(g_ref.at[:, z], g_to.at[:, :, :, z * chunk : (z + 1) * chunk]) for z in range(g_ref.shape[1])]
+def pack_parts_kernel(core_ref, g_ref, own, other, sems):
+    core, chunk = core_ref[0], g_ref.shape[-1]
+    moves = []
+    for z in range(g_ref.shape[2]):
+        lanes = slice(z * chunk, (z + 1) * chunk)
+        moves.append((g_ref.at[:, core, z], own.at[:, :, :, lanes]))
+        moves.append((g_ref.at[:, 1 - core, z], other.at[:, :, :, lanes]))
     run_all(moves, sems)
+
+
+def add_kernel(a_ref, b_ref, to):
+    to[...] = a_ref[...] + b_ref[...]
+
+
+def added(a, b):
+    vmem = pl.BlockSpec(memory_space=pltpu.VMEM)
+    outs = (jax.ShapeDtypeStruct(a.shape, a.dtype),)
+    return kernel_call(add_kernel, outs, (a, b), "add", in_specs=[vmem, vmem])[0]
 
 
 def pack_kernel(n, at_ref, q_ref, k_ref, v_ref, *refs):
@@ -108,16 +122,16 @@
     )
 
 
-def packed_parts(g):
-    yc, z, x, _, chunk = g.shape
+def packed_parts(core, g):
+    y, _, z, x, _, chunk = g.shape
     return kernel_call(
         pack_parts_kernel,
-        (jax.ShapeDtypeStruct((yc, x, 1, z * chunk), g.dtype),),
-        (g,),
+        (jax.ShapeDtypeStruct((y, x, 1, z * chunk), g.dtype),) * 2,
+        (core, g),
         "pack_parts",
-        scratch=(pltpu.SemaphoreType.DMA((z,)),),
-        in_specs=[pl.BlockSpec(memory_space=pl.ANY)],
-    )[0]
+        scratch=(pltpu.SemaphoreType.DMA((2 * z,)),),
+        in_specs=[pl.BlockSpec(memory_space=pltpu.SMEM), pl.BlockSpec(memory_space=pl.ANY)],
+    )
 
 
 def stack_kernel(n, *refs):
@@ -291,10 +305,11 @@
     at = lax.axis_index(AA).astype(jnp.int32).reshape(1)
     wide = queries.shape[2] // (z * n)
     reach = queries.shape[1] * 2
-    chunks = grad_parts.reshape(y * c, z, n, 1, -1)
+    chunks = grad_parts.reshape(y, c, z, n, 1, -1)
+    core = lax.axis_index("blk_1").astype(jnp.int32).reshape(1)
     kv_far = packed_far(at, queries[0], keys[0], values[0], n)
     sent = packed(at, queries[0], keys[0], values[0], n)
-    parts = packed_parts(chunks)
+    parts, parts_out = packed_parts(core, chunks)
 
     def along_x(value, hop):
         return lax.ppermute(value, "aa_1", [(x, (x + hop) % n) for x in range(n)])
@@ -303,9 +318,11 @@
         return lax.ppermute(value, "aa_0", [(s, 1 - s) for s in range(z)])
 
     kv_far = across_z(kv_far)
+    parts_in = lax.ppermute(parts_out, "blk_1", [(i, 1 - i) for i in range(c)])
     near = [sent[0]] + [along_x(sent[hop], hop) for hop in range(1, n)]
-    parts = parts.reshape(y * c * n, 1, -1)
-    parts = lax.all_to_all(parts, ("blk_0", "blk_1", "aa_1"), 0, 0, tiled=True)
+    parts = added(parts, parts_in)
+    parts = parts.reshape(y * n, 1, -1)
+    parts = lax.all_to_all(parts, ("blk_0", "aa_1"), 0, 0, tiled=True)
     q_far = stacked(near[1:], wide)
     q_far = across_z(q_far)
     far = cut(at, kv_far, n)

time: 107 us -> 110 us (1.028)
  waiting for transfers between devices: 14.1 us -> 15.6 us
    ppermute x0 -> x1, starting transfers between devices: none -> 1.92 us  [step(): parts_in = lax.ppermute(parts_out, 'blk_1', [(i, 1 - i) for i in range(c)])]
    ppermute x0 -> x1, waiting for transfers between devices: none -> 1.5 us  [step(): parts_in = lax.ppermute(parts_out, 'blk_1', [(i, 1 - i) for i in range(c)])]
    pallas_call x10 -> x11, Pallas kernels: 9.56 us -> 9.36 us  [kernel_call(): return pl.pallas_call(body, **settings)(*ins)]
  transfers between devices with their start and end apart: 11 -> 12, of which waited for: 2 -> 3; matrix products, arithmetic and copies ran while one was open for 0% -> 0% of each run, Pallas kernels for 8% -> 7%
where the time goes in v9:
time: 110 us; the launch traced here: 109 us
  starting transfers between devices  82.1 us (75%)
  waiting for transfers between devices  15.6 us (14%)
  Pallas kernels  9.36 us (9%)
    ppermute x2, starting transfers between devices, across_z(): return lax.ppermute(value, 'aa_0', [(s, 1 - s) for s in range(z)])  27.8 us
    ppermute x6, starting transfers between devices, along_x(): return lax.ppermute(value, 'aa_1', [(x, (x + hop) % n) for x in range(n)])  20.6 us
    all_to_all x1, starting transfers between devices, step(): share = lax.all_to_all(share, ('dp', 'aa_0'), 0, 0, tiled=True)  20.4 us
    ppermute x2, waiting for transfers between devices, across_z(): return lax.ppermute(value, 'aa_0', [(s, 1 - s) for s in range(z)])  13.1 us
    all_to_all x1, starting transfers between devices, step(): parts = lax.all_to_all(parts, ('blk_0', 'aa_1'), 0, 0, tiled=True)  9.95 us
    pallas_call x11, Pallas kernels, kernel_call(): return pl.pallas_call(body, **settings)(*ins)  9.36 us
  transfers between devices with their start and end apart: 12, of which 3 were waited for; matrix products, arithmetic and copies ran while one was open for 0% of the time, Pallas kernels for 7%

profile of v9, /device:TPU:128, one launch (start us, length us, event | category | flops | bytes accessed | tf_op | source)
XLA Modules:
  0.0 109.0 jit_solution(14619939265344312214)
XLA Ops:
  0.6 1.0 copy-done.1
  1.7 0.1 pack_parts.1
  1.8 1.9 %collective-permute-start.9 = (f32[8,4,1,2048]{3,2,1,0:T(1,128)S(1)}, f32[8,4,1,2048]{3,2,1,0:T(1,128)S(1)}, u32[]{:S(2)}, u32[]{:S(2)}) collective-permute-start(f32[8,4,1,2048]{3,2,1,0:T(1,128)S(1)} %get-tuple-element.25), channel_id=1, source_target_pairs={{0,8},{8,0},{1,9},{9,1},{2,10},{10,2},{3,11},{11,3},{4,12},{12,4},... | collective-permute-start | bytes 786440 | tf_op jit(solution)/shard_map/ppermute | solution.py:321
  3.7 1.5 %collective-permute-done.9.b_ref = f32[8,4,1,2048]{3,2,1,0:T(1,128)S(1)} collective-permute-done((f32[8,4,1,2048]{3,2,1,0:T(1,128)S(1)}, f32[8,4,1,2048]{3,2,1,0:T(1,128)S(1)}, u32[]{:S(2)}, u32[]{:S(2)}) %collective-permute-start.9) | collective-permute-done | bytes 262176 | tf_op jit(solution)/shard_map/ppermute | solution.py:321
  5.2 0.7 add.5
  5.9 10.0 %all-to-all-start = ((f32[32,1,2048]{2,1,0:T(1,128)}), f32[32,1,2048]{2,1,0:T(1,128)S(1)}, u32[]{:S(2)}, u32[]{:S(2)}) async-start(f32[32,1,2048]{2,1,0:T(1,128)} %bitcast.7), calls=%async_computation | async-start | bytes 524288 | tf_op jit(solution)/shard_map/all_to_all | solution.py:325
  15.9 0.0 copy-start
  15.9 0.0 copy-start.2
  15.9 0.0 copy-start.3
  15.9 1.6 %pack_far.1 = bf16[3,128,256]{2,1,0:T(8,128)(2,1)} custom-call(s32[1]{0:T(128)} %bitcast.refs_0_, bf16[128,2048]{1,0:T(8,128)(2,1)} %bitcast.9, bf16[128,512]{1,0:T(8,128)(2,1)} %bitcast.12, bf16[128,512]{1,0:T(8,128)(2,1)} %bitcast.14), custom_call_target="tpu_custom_call" | custom-call | tf_op jit(solution)/shard_map/pack_far/pallas_call | solution.py:94
  17.6 17.6 %collective-permute-start.3 = (bf16[3,128,256]{2,1,0:T(8,128)(2,1)}, bf16[3,128,256]{2,1,0:T(8,128)(2,1)S(1)}, u32[]{:S(2)}, u32[]{:S(2)}) collective-permute-start(bf16[3,128,256]{2,1,0:T(8,128)(2,1)} %pack_far.1), channel_id=1, source_target_pairs={{0,4},{4,0},{1,5},{5,1},{2,6},{6,2},{3,7},{7,3},{8,12},{12,8},{9,1... | collective-permute-start | bytes 589832 | tf_op jit(solution)/shard_map/ppermute | solution.py:318
  35.2 0.3 pack.1
  35.5 3.7 %collective-permute-start = (bf16[128,768]{1,0:T(8,128)(2,1)S(1)}, bf16[128,768]{1,0:T(8,128)(2,1)S(1)}, u32[]{:S(2)}, u32[]{:S(2)}) collective-permute-start(bf16[128,768]{1,0:T(8,128)(2,1)S(1)} %get-tuple-element.15), channel_id=1, source_target_pairs={{0,1},{1,2},{2,3},{3,0},{4,5},{5,6},{6,7},{7,4},{8,9},{9,10},{10,1... | collective-permute-start | bytes 589832 | tf_op jit(solution)/shard_map/ppermute | solution.py:315
  39.2 4.6 %collective-permute-start.1 = (bf16[128,768]{1,0:T(8,128)(2,1)S(1)}, bf16[128,768]{1,0:T(8,128)(2,1)S(1)}, u32[]{:S(2)}, u32[]{:S(2)}) collective-permute-start(bf16[128,768]{1,0:T(8,128)(2,1)S(1)} %get-tuple-element.16), channel_id=1, source_target_pairs={{0,2},{1,3},{2,0},{3,1},{4,6},{5,7},{6,4},{7,5},{8,10},{9,11},{10,... | collective-permute-start | bytes 589832 | tf_op jit(solution)/shard_map/ppermute | solution.py:315
  43.8 3.4 %collective-permute-start.2 = (bf16[128,768]{1,0:T(8,128)(2,1)S(1)}, bf16[128,768]{1,0:T(8,128)(2,1)S(1)}, u32[]{:S(2)}, u32[]{:S(2)}) collective-permute-start(bf16[128,768]{1,0:T(8,128)(2,1)S(1)} %get-tuple-element.17), channel_id=1, source_target_pairs={{0,3},{1,0},{2,1},{3,2},{4,7},{5,4},{6,5},{7,6},{8,11},{9,8},{10,9... | collective-permute-start | bytes 589832 | tf_op jit(solution)/shard_map/ppermute | solution.py:315
  47.2 0.0 collective-permute-done.3.refs_1_.refs_4_
  47.2 2.5 %collective-permute-start.4 = (bf16[128,256]{1,0:T(8,128)(2,1)S(1)}, bf16[128,256]{1,0:T(8,128)(2,1)S(1)}, u32[]{:S(2)}, u32[]{:S(2)}) collective-permute-start(bf16[128,256]{1,0:T(8,128)(2,1)S(1)} %get-tuple-element.19), channel_id=1, source_target_pairs={{0,1},{1,2},{2,3},{3,0},{4,5},{5,6},{6,7},{7,4},{8,9},{9,10},{10,1... | collective-permute-start | bytes 196616 | tf_op jit(solution)/shard_map/ppermute | solution.py:315
  49.7 3.0 %collective-permute-start.5 = (bf16[128,256]{1,0:T(8,128)(2,1)S(1)}, bf16[128,256]{1,0:T(8,128)(2,1)S(1)}, u32[]{:S(2)}, u32[]{:S(2)}) collective-permute-start(bf16[128,256]{1,0:T(8,128)(2,1)S(1)} %get-tuple-element.20), channel_id=1, source_target_pairs={{0,2},{1,3},{2,0},{3,1},{4,6},{5,7},{6,4},{7,5},{8,10},{9,11},{10,... | collective-permute-start | bytes 196616 | tf_op jit(solution)/shard_map/ppermute | solution.py:315
  52.7 0.0 collective-permute-done.refs_2_.refs_0_.refs_4_
  52.8 3.5 %collective-permute-start.6 = (bf16[128,256]{1,0:T(8,128)(2,1)S(1)}, bf16[128,256]{1,0:T(8,128)(2,1)S(1)}, u32[]{:S(2)}, u32[]{:S(2)}) collective-permute-start(bf16[128,256]{1,0:T(8,128)(2,1)S(1)} %get-tuple-element.21), channel_id=1, source_target_pairs={{0,3},{1,0},{2,1},{3,2},{4,7},{5,4},{6,5},{7,6},{8,11},{9,8},{10,9... | collective-permute-start | bytes 196616 | tf_op jit(solution)/shard_map/ppermute | solution.py:315
  56.2 0.0 all-to-all-done.refs_0_
  56.2 0.8 share.1
  57.0 20.4 %all-to-all-start.1 = ((f32[16,1,1024]{2,1,0:T(1,128)}), f32[16,1,1024]{2,1,0:T(1,128)S(1)}, u32[]{:S(2)}, u32[]{:S(2)}) async-start(f32[16,1,1024]{2,1,0:T(1,128)} %share.1), calls=%async_computation.1 | async-start | bytes 131072 | tf_op jit(solution)/shard_map/all_to_all | solution.py:335
  77.4 0.0 collective-permute-done.1.refs_3_.refs_1_.refs_5_
  77.5 10.3 %collective-permute-start.8 = (bf16[3,128,256]{2,1,0:T(8,128)(2,1)S(1)}, bf16[3,128,256]{2,1,0:T(8,128)(2,1)S(1)}, u32[]{:S(2)}, u32[]{:S(2)}) collective-permute-start(bf16[3,128,256]{2,1,0:T(8,128)(2,1)S(1)} %stack.1), channel_id=1, source_target_pairs={{0,4},{4,0},{1,5},{5,1},{2,6},{6,2},{3,7},{7,3},{8,12},{12,8},{9,1... | collective-permute-start | bytes 589832 | tf_op jit(solution)/shard_map/ppermute | solution.py:318
  87.8 0.1 gather.1
  87.9 1.3 %collective-permute-start.7 = (bf16[256,256]{1,0:T(8,128)(2,1)S(1)}, bf16[256,256]{1,0:T(8,128)(2,1)S(1)}, u32[]{:S(2)}, u32[]{:S(2)}) collective-permute-start(bf16[256,256]{1,0:T(8,128)(2,1)S(1)} %get-tuple-element.23), channel_id=1, source_target_pairs={{0,8},{8,16},{16,24},{24,32},{32,40},{40,48},{48,56},{56,64},{64,7... | collective-permute-start | bytes 393224 | tf_op jit(solution)/shard_map/ppermute | solution.py:331
  89.2 1.0 collective-permute-done.7.refs_2_
  90.1 2.5 %attend.2.refs_5_ = bf16[1024,256]{1,0:T(8,128)(2,1)} custom-call(s32[1]{0:T(128)} %bitcast.refs_0_, bf16[1024,256]{1,0:T(8,128)(2,1)S(1)} %get-tuple-element.22.refs_1_, bf16[256,256]{1,0:T(8,128)(2,1)S(1)} %collective-permute-done.7.refs_2_, bf16[128,512]{1,0:T(8,128)(2,1)S(1)} %get-tuple-element.14.refs_1_.refs_3_, ...), custom_call_target="tpu_custom_call" | custom-call | flops 268435456 | bytes 1048576 | tf_op jit(solution)/shard_map/attend/pallas_call | solution.py:94
  92.7 13.1 %collective-permute-done.8.refs_3_ = bf16[3,128,256]{2,1,0:T(8,128)(2,1)S(1)} collective-permute-done((bf16[3,128,256]{2,1,0:T(8,128)(2,1)S(1)}, bf16[3,128,256]{2,1,0:T(8,128)(2,1)S(1)}, u32[]{:S(2)}, u32[]{:S(2)}) %collective-permute-start.8) | collective-permute-done | bytes 196640 | tf_op jit(solution)/shard_map/ppermute | solution.py:318
  105.8 2.5 %attend.3 = bf16[1024,256]{1,0:T(8,128)(2,1)} custom-call(s32[1]{0:T(128)} %bitcast.refs_0_, bf16[1024,256]{1,0:T(8,128)(2,1)S(1)} %get-tuple-element.22.refs_1_, bf16[256,256]{1,0:T(8,128)(2,1)S(1)} %collective-permute-done.7.refs_2_, bf16[3,128,256]{2,1,0:T(8,128)(2,1)S(1)} %collective-permute-done.8.refs_3_, ...), custom_call_target="tpu_custom_call", output_to_operand_aliasing={{}: (5, {})} | custom-call | flops 268435456 | bytes 1048576 | tf_op jit(solution)/shard_map/attend/pallas_call | solution.py:94
  108.4 0.6 mean.1
  (11 shorter events, 0.1 us)
Async XLA Ops:
  0.6 1.0 copy-start.1
  1.8 3.4 %collective-permute-start.9 = (f32[8,4,1,2048]{3,2,1,0:T(1,128)S(1)}, f32[8,4,1,2048]{3,2,1,0:T(1,128)S(1)}, u32[]{:S(2)}, u32[]{:S(2)}) collective-permute-start(f32[8,4,1,2048]{3,2,1,0:T(1,128)S(1)} %get-tuple-element.25), channel_id=1, source_target_pairs={{0,8},{8,0},{1,9},{9,1},{2,10},{10,2},{3,11},{11,3},{4,12},{12,4},... | collective-permute-start | bytes 786440 | tf_op jit(solution)/shard_map/ppermute | solution.py:321
  5.9 50.3 %all-to-all-start = ((f32[32,1,2048]{2,1,0:T(1,128)}), f32[32,1,2048]{2,1,0:T(1,128)S(1)}, u32[]{:S(2)}, u32[]{:S(2)}) async-start(f32[32,1,2048]{2,1,0:T(1,128)} %bitcast.7), calls=%async_computation | async-start | bytes 524288 | tf_op jit(solution)/shard_map/all_to_all | solution.py:325
  15.9 19.2 %copy-start = (bf16[1,128,2048]{2,1,0:T(8,128)(2,1)S(1)}, bf16[1,128,2048]{2,1,0:T(8,128)(2,1)}, u32[]{:S(2)}) copy-start(bf16[1,128,2048]{2,1,0:T(8,128)(2,1)} %param.4) | copy-start | bytes 1572868
  15.9 19.2 %copy-start.2 = (bf16[1,128,512]{2,1,0:T(8,128)(2,1)S(1)}, bf16[1,128,512]{2,1,0:T(8,128)(2,1)}, u32[]{:S(2)}) copy-start(bf16[1,128,512]{2,1,0:T(8,128)(2,1)} %param.5) | copy-start | bytes 393220
  15.9 19.2 %copy-start.3 = (bf16[1,128,512]{2,1,0:T(8,128)(2,1)S(1)}, bf16[1,128,512]{2,1,0:T(8,128)(2,1)}, u32[]{:S(2)}) copy-start(bf16[1,128,512]{2,1,0:T(8,128)(2,1)} %param.6) | copy-start | bytes 393220
  17.6 29.6 %collective-permute-start.3 = (bf16[3,128,256]{2,1,0:T(8,128)(2,1)}, bf16[3,128,256]{2,1,0:T(8,128)(2,1)S(1)}, u32[]{:S(2)}, u32[]{:S(2)}) collective-permute-start(bf16[3,128,256]{2,1,0:T(8,128)(2,1)} %pack_far.1), channel_id=1, source_target_pairs={{0,4},{4,0},{1,5},{5,1},{2,6},{6,2},{3,7},{7,3},{8,12},{12,8},{9,1... | collective-permute-start | bytes 589832 | tf_op jit(solution)/shard_map/ppermute | solution.py:318
  35.5 17.3 %collective-permute-start = (bf16[128,768]{1,0:T(8,128)(2,1)S(1)}, bf16[128,768]{1,0:T(8,128)(2,1)S(1)}, u32[]{:S(2)}, u32[]{:S(2)}) collective-permute-start(bf16[128,768]{1,0:T(8,128)(2,1)S(1)} %get-tuple-element.15), channel_id=1, source_target_pairs={{0,1},{1,2},{2,3},{3,0},{4,5},{5,6},{6,7},{7,4},{8,9},{9,10},{10,1... | collective-permute-start | bytes 589832 | tf_op jit(solution)/shard_map/ppermute | solution.py:315
  39.2 38.2 %collective-permute-start.1 = (bf16[128,768]{1,0:T(8,128)(2,1)S(1)}, bf16[128,768]{1,0:T(8,128)(2,1)S(1)}, u32[]{:S(2)}, u32[]{:S(2)}) collective-permute-start(bf16[128,768]{1,0:T(8,128)(2,1)S(1)} %get-tuple-element.16), channel_id=1, source_target_pairs={{0,2},{1,3},{2,0},{3,1},{4,6},{5,7},{6,4},{7,5},{8,10},{9,11},{10,... | collective-permute-start | bytes 589832 | tf_op jit(solution)/shard_map/ppermute | solution.py:315
  43.8 33.7 %collective-permute-start.2 = (bf16[128,768]{1,0:T(8,128)(2,1)S(1)}, bf16[128,768]{1,0:T(8,128)(2,1)S(1)}, u32[]{:S(2)}, u32[]{:S(2)}) collective-permute-start(bf16[128,768]{1,0:T(8,128)(2,1)S(1)} %get-tuple-element.17), channel_id=1, source_target_pairs={{0,3},{1,0},{2,1},{3,2},{4,7},{5,4},{6,5},{7,6},{8,11},{9,8},{10,9... | collective-permute-start | bytes 589832 | tf_op jit(solution)/shard_map/ppermute | solution.py:315
  47.2 40.6 %collective-permute-start.4 = (bf16[128,256]{1,0:T(8,128)(2,1)S(1)}, bf16[128,256]{1,0:T(8,128)(2,1)S(1)}, u32[]{:S(2)}, u32[]{:S(2)}) collective-permute-start(bf16[128,256]{1,0:T(8,128)(2,1)S(1)} %get-tuple-element.19), channel_id=1, source_target_pairs={{0,1},{1,2},{2,3},{3,0},{4,5},{5,6},{6,7},{7,4},{8,9},{9,10},{10,1... | collective-permute-start | bytes 196616 | tf_op jit(solution)/shard_map/ppermute | solution.py:315
  49.7 38.1 %collective-permute-start.5 = (bf16[128,256]{1,0:T(8,128)(2,1)S(1)}, bf16[128,256]{1,0:T(8,128)(2,1)S(1)}, u32[]{:S(2)}, u32[]{:S(2)}) collective-permute-start(bf16[128,256]{1,0:T(8,128)(2,1)S(1)} %get-tuple-element.20), channel_id=1, source_target_pairs={{0,2},{1,3},{2,0},{3,1},{4,6},{5,7},{6,4},{7,5},{8,10},{9,11},{10,... | collective-permute-start | bytes 196616 | tf_op jit(solution)/shard_map/ppermute | solution.py:315
  52.8 35.0 %collective-permute-start.6 = (bf16[128,256]{1,0:T(8,128)(2,1)S(1)}, bf16[128,256]{1,0:T(8,128)(2,1)S(1)}, u32[]{:S(2)}, u32[]{:S(2)}) collective-permute-start(bf16[128,256]{1,0:T(8,128)(2,1)S(1)} %get-tuple-element.21), channel_id=1, source_target_pairs={{0,3},{1,0},{2,1},{3,2},{4,7},{5,4},{6,5},{7,6},{8,11},{9,8},{10,9... | collective-permute-start | bytes 196616 | tf_op jit(solution)/shard_map/ppermute | solution.py:315
  57.0 51.3 %all-to-all-start.1 = ((f32[16,1,1024]{2,1,0:T(1,128)}), f32[16,1,1024]{2,1,0:T(1,128)S(1)}, u32[]{:S(2)}, u32[]{:S(2)}) async-start(f32[16,1,1024]{2,1,0:T(1,128)} %share.1), calls=%async_computation.1 | async-start | bytes 131072 | tf_op jit(solution)/shard_map/all_to_all | solution.py:335
  77.5 28.3 %collective-permute-start.8 = (bf16[3,128,256]{2,1,0:T(8,128)(2,1)S(1)}, bf16[3,128,256]{2,1,0:T(8,128)(2,1)S(1)}, u32[]{:S(2)}, u32[]{:S(2)}) collective-permute-start(bf16[3,128,256]{2,1,0:T(8,128)(2,1)S(1)} %stack.1), channel_id=1, source_target_pairs={{0,4},{4,0},{1,5},{5,1},{2,6},{6,2},{3,7},{7,3},{8,12},{12,8},{9,1... | collective-permute-start | bytes 589832 | tf_op jit(solution)/shard_map/ppermute | solution.py:318
  87.9 2.3 %collective-permute-start.7 = (bf16[256,256]{1,0:T(8,128)(2,1)S(1)}, bf16[256,256]{1,0:T(8,128)(2,1)S(1)}, u32[]{:S(2)}, u32[]{:S(2)}) collective-permute-start(bf16[256,256]{1,0:T(8,128)(2,1)S(1)} %get-tuple-element.23), channel_id=1, source_target_pairs={{0,8},{8,16},{16,24},{24,32},{32,40},{40,48},{48,56},{56,64},{64,7... | collective-permute-start | bytes 393224 | tf_op jit(solution)/shard_map/ppermute | solution.py:331
